TPU v7x, 512 devices: a whole 4x8x8 slice. The times are simulated.
512 devices in a mesh: sub: 16 (over z, core), blk: 32 (over x, y).
Axes of the slice: x: 4, y: 8, z: 8, core: 2. Of those that a mesh axis runs over, the one named last changes fastest.
Arguments:
- double_layer: bfloat16 [16, 2, 2048, 2048], P('sub', None, 'blk'), may hold values from -1 to 2
- single_layer: bfloat16 [16, 2, 2048, 2048], P('sub', None, 'blk'), may hold values from -1 to 2
- hypersingular: bfloat16 [16, 2, 2048, 2048], P('sub', None, 'blk'), may hold values from -1 to 2
- adjoint_double: bfloat16 [16, 2, 2048, 2048], P('sub', None, 'blk'), may hold values from -1 to 2
- matching: int32 [16, 1024], replicated, may hold values from 0 to 1023, each once within a row
- right_side: float32 [16, 2, 2, 2048, 64], P('sub', None, None, 'blk'), may hold values from -6 to 6
- start: float32 [16, 2, 2, 2048, 64], P('sub', None, None, 'blk'), may hold values from -4 to 4
Outputs:
- solution: float32 [16, 2, 2, 2048, 64], P('sub', None, None, 'blk')
Inputs may be any that keep to these rules, and one draw needn't show every extreme that they name: `matching`: each row is a permutation of 0 to 1023; row 0 pairs with no subdomain below and is not read.
All inputs are finite; a program needn't handle non-finite values.
Results may differ from a plain program's by a relative error of at most 0.015.
Values may be sent and summed in bfloat16 or wider, within the bound.
No kernel may reach another device: no remote copies, remote signals or barrier semaphores. Data moves between devices by JAX's collectives and lax.ppermute only.
A program may use at most 64 MiB of HBM per device.

v0:
```python
import jax
import jax.numpy as jnp
from jax import lax
from jax.sharding import Mesh
from jax.sharding import PartitionSpec as P

BASIS = 5
SUB = ("sub_0", "sub_1")
BLK = ("blk_0", "blk_1")
SUB_BLK = ("sub_0", "sub_1", "blk_0", "blk_1")


EPSILON = 1e-06


def passed_along(block, axis, distance):
    devices = range(lax.axis_size(axis))
    route = [(i - distance, i) for i in devices if i - distance in devices]
    return lax.ppermute(block, axis, route)


def copy_for_each(value, axis):
    peers = lax.axis_size(axis)
    return lax.all_to_all(
        jnp.broadcast_to(value[None], (peers, *value.shape)), axis, 0, 0, tiled=True
    )


def laid_out(blocks, dim):
    blocks = jnp.moveaxis(blocks, 0, dim)
    lengths = blocks.shape
    return blocks.reshape(*lengths[:dim], lengths[dim] * lengths[dim + 1], *lengths[dim + 2 :])


def gathered_copies(value, axis, dim):
    blocks = copy_for_each(value, axis)
    return laid_out(blocks, dim)


def over_axes(value, axes):
    for axis in axes:
        value = lax.psum(value, axis)
    return value


def complex_product(matrix, vector):
    width = vector.shape[-1] // 2
    count = matrix.shape[1]
    products = jnp.dot(
        matrix.reshape(2 * count, matrix.shape[2]), vector, preferred_element_type=jnp.float32
    )
    products = products.reshape(2, count, 2 * width)
    real_part = products[0, :, :width] - products[1, :, width:]
    imag_part = products[0, :, width:] + products[1, :, :width]
    return jnp.concatenate([real_part, imag_part], axis=-1)


def calderon(double_layer, single_layer, hypersingular, adjoint_double, vector):
    upper = complex_product(single_layer, vector[1]) - complex_product(double_layer, vector[0])
    lower = complex_product(hypersingular, vector[0]) + complex_product(adjoint_double, vector[1])
    return jnp.stack([upper, lower])


def inward(field):
    local_field = field[0]
    return jnp.concatenate([local_field[:, 0], local_field[:, 1]], axis=-1)


def outward(vector):
    width = vector.shape[-1] // 2
    return jnp.stack([vector[..., :width], vector[..., width:]], axis=1)[None]


def coupling_rows(gathered, matching, local_rows):
    subdomains = lax.axis_size(SUB)
    own_index = lax.axis_index(SUB)
    block_index = lax.axis_index(BLK)
    half_rows = local_rows // 2
    above_index = jnp.minimum(own_index + 1, subdomains - 1)
    perm_here = lax.dynamic_index_in_dim(matching, own_index, 0, keepdims=False)
    perm_above = lax.dynamic_index_in_dim(matching, above_index, 0, keepdims=False)
    window = block_index * half_rows
    odd_rows = gathered[:, 1::2]
    even_rows = gathered[:, 0::2]
    inverse_here = jnp.argsort(perm_here)
    send_upward = jnp.take(
        odd_rows, lax.dynamic_slice_in_dim(perm_above, window, half_rows), axis=1
    )
    send_downward = jnp.take(
        even_rows, lax.dynamic_slice_in_dim(inverse_here, window, half_rows), axis=1
    )
    lower_face = passed_along(send_upward, SUB, 1)
    upper_face = passed_along(send_downward, SUB, -1)
    joined = jnp.stack([lower_face, upper_face], axis=2)
    joined = joined.reshape(2, local_rows, gathered.shape[-1]).astype(jnp.float32)
    trace_signs = jnp.array([1.0, -1.0], jnp.float32).reshape(2, 1, 1)
    return joined * trace_signs


def preconditioned(operators, matching, vector):
    rounded = vector.astype(jnp.bfloat16)
    gathered = gathered_copies(rounded, BLK, 1)
    first_image = calderon(*operators, gathered)
    middle = first_image - 0.5 * coupling_rows(gathered, matching, vector.shape[1])
    middle_rounded = middle.astype(jnp.bfloat16)
    middle_full = gathered_copies(middle_rounded, BLK, 1)
    return calderon(*operators, middle_full)


def inner_local(first, second):
    totals = jnp.sum(first * second, axis=(0, 1))
    width = totals.shape[0] // 2
    return totals[:width] + totals[width:]


def spread(values):
    return jnp.concatenate([values, values])


def global_norm(vector):
    return jnp.sqrt(over_axes(inner_local(vector, vector), SUB_BLK) + EPSILON)


def body(double_layer, single_layer, hypersingular, adjoint_double, matching, right_side, start):
    operators = (double_layer[0], single_layer[0], hypersingular[0], adjoint_double[0])
    right_local = inward(right_side)
    start_local = inward(start)
    residual = right_local - preconditioned(operators, matching, start_local)
    beta = global_norm(residual)
    basis = [residual / spread(beta)]
    columns = []
    for column in range(BASIS):
        image = preconditioned(operators, matching, basis[column])
        local_dots = [inner_local(basis[earlier], image) for earlier in range(column + 1)]
        stacked_dots = jnp.stack(local_dots + [inner_local(image, image)])
        summed = over_axes(stacked_dots, SUB_BLK)
        coefficients = [summed[earlier] for earlier in range(column + 1)]
        for earlier in range(column + 1):
            image = image - spread(coefficients[earlier]) * basis[earlier]
        squares = summed[column + 1] - jnp.sum(summed[: column + 1] * summed[: column + 1], axis=0)
        height = jnp.sqrt(jnp.maximum(squares, 0.0) + EPSILON)
        if column + 1 < BASIS:
            basis.append(image / spread(height))
        filler = [jnp.zeros_like(height)] * (BASIS - 1 - column)
        columns.append(jnp.stack(coefficients + [height] + filler, axis=1))
    hessen = jnp.stack(columns, axis=2)
    gram = jnp.einsum("rij,rik->rjk", hessen, hessen, precision=lax.Precision.HIGHEST)
    target = beta[:, None] * hessen[:, 0, :]
    factor = jnp.linalg.cholesky(gram)
    weights = jax.scipy.linalg.cho_solve((factor, True), target[..., None])[..., 0]
    solution = start_local
    for column in range(BASIS):
        solution = solution + spread(weights[:, column]) * basis[column]
    return outward(solution)


def solution(mesh):
    torus = Mesh(mesh.devices.reshape(8, 2, 4, 8), ("sub_0", "sub_1", "blk_0", "blk_1"))
    placed = (
        P(SUB, None, BLK, None),
        P(SUB, None, BLK, None),
        P(SUB, None, BLK, None),
        P(SUB, None, BLK, None),
        P(),
        P(SUB, None, None, BLK, None),
        P(SUB, None, None, BLK, None),
    )
    return jax.shard_map(
        body, mesh=torus, in_specs=placed, out_specs=P(SUB, None, None, BLK, None), check_vma=False
    )
```

profile of v0, /device:TPU:1, one launch (start us, length us, event | category | flops | bytes accessed | tf_op | source)
XLA Modules:
  0.0 822.3 jit_solution(2891582693578804265)
XLA Ops:
  2.9 10.5 %all-to-all-start = ((bf16[32,2,64,128]{3,2,1,0:T(8,128)(2,1)}), bf16[32,2,64,128]{3,2,1,0:T(8,128)(2,1)S(1)}, u32[]{:S(2)}, u32[]{:S(2)}) async-start(bf16[32,2,64,128]{3,2,1,0:T(8,128)(2,1)} %broadcast_in_dim.37), calls=%async_computation | async-start | bytes 2097152 | tf_op jit(solution)/shard_map/all_to_all | solution.py:24
  14.2 4.4 sort.27
  19.4 18.8 %all-to-all-done = bf16[32,2,64,128]{3,2,1,0:T(8,128)(2,1)S(1)} async-done(((bf16[32,2,64,128]{3,2,1,0:T(8,128)(2,1)}), bf16[32,2,64,128]{3,2,1,0:T(8,128)(2,1)S(1)}, u32[]{:S(2)}, u32[]{:S(2)}) %all-to-all-start) | async-done | bytes 1048608 | tf_op jit(solution)/shard_map/all_to_all | solution.py:24
  42.7 8.6 %collective-permute-start = (bf16[2,32,128]{2,0,1:T(2,128)(2,1)S(1)}, bf16[2,32,128]{2,0,1:T(2,128)(2,1)S(1)}, u32[]{:S(2)}, u32[]{:S(2)}) collective-permute-start(bf16[2,32,128]{2,0,1:T(2,128)(2,1)S(1)} %fusion.10), channel_id=1, source_target_pairs={{0,32},{32,64},{64,96},{96,128},{128,160},{160,192},{192,224},{224... | collective-permute-start | bytes 49160 | tf_op jit(solution)/shard_map/ppermute | solution.py:19
  60.8 4.9 all-to-all-start.1
  65.8 26.8 %all-to-all-done.1 = bf16[32,2,64,128]{3,2,1,0:T(8,128)(2,1)S(1)} async-done(((bf16[32,2,64,128]{3,2,1,0:T(8,128)(2,1)}), bf16[32,2,64,128]{3,2,1,0:T(8,128)(2,1)S(1)}, u32[]{:S(2)}, u32[]{:S(2)}) %all-to-all-start.1) | async-done | bytes 1048608 | tf_op jit(solution)/shard_map/all_to_all | solution.py:24
  94.6 16.8 %psum.168 = f32[64]{0:T(128)S(1)} all-reduce(f32[64]{0:T(128)S(1)} %slice_add_fusion.48), channel_id=1, replica_groups=mesh['sub_0'=8,'sub_1'=2,'blk_0'=4,'blk_1'=8] {'sub_0'}, use_global_device_ids=true, to_apply=%region_2.4 | all-reduce | flops 64 | bytes 512 | tf_op jit(solution)/shard_map/psum | solution.py:42
  111.3 9.4 %psum.169 = f32[64]{0:T(128)S(1)} all-reduce(f32[64]{0:T(128)S(1)} %psum.168), channel_id=1, replica_groups=mesh['sub_0'=8,'sub_1'=2,'blk_0'=4,'blk_1'=8] {'sub_1'}, use_global_device_ids=true, to_apply=%region_3.5 | all-reduce | flops 64 | bytes 512 | tf_op jit(solution)/shard_map/psum | solution.py:42
  120.7 6.5 psum.170
  127.2 12.4 %psum.171 = f32[64]{0:T(128)S(1)} all-reduce(f32[64]{0:T(128)S(1)} %psum.170), channel_id=1, replica_groups=mesh['sub_0'=8,'sub_1'=2,'blk_0'=4,'blk_1'=8] {'blk_1'}, use_global_device_ids=true, to_apply=%region_5.7 | all-reduce | flops 64 | bytes 512 | tf_op jit(solution)/shard_map/psum | solution.py:42
  140.5 24.6 %all_to_all.60 = bf16[32,2,64,128]{3,2,1,0:T(8,128)(2,1)S(1)} all-to-all(bf16[32,2,64,128]{3,2,1,0:T(8,128)(2,1)S(1)} %broadcast_in_dim.39), channel_id=1, replica_groups=mesh['sub_0'=8,'sub_1'=2,'blk_0'=4,'blk_1'=8] {'blk_0','blk_1'}, dimensions={0} | all-to-all | bytes 2097152 | tf_op jit(solution)/shard_map/all_to_all | solution.py:24
  175.7 10.9 %collective-permute-start.3 = (bf16[2,32,128]{2,0,1:T(2,128)(2,1)S(1)}, bf16[2,32,128]{2,0,1:T(2,128)(2,1)S(1)}, u32[]{:S(2)}, u32[]{:S(2)}) collective-permute-start(bf16[2,32,128]{2,0,1:T(2,128)(2,1)S(1)} %fusion.17), channel_id=1, source_target_pairs={{32,0},{64,32},{96,64},{128,96},{160,128},{192,160},{224,192},{256... | collective-permute-start | bytes 49160 | tf_op jit(solution)/shard_map/ppermute | solution.py:19
  191.4 31.0 %all_to_all.61 = bf16[32,2,64,128]{3,2,1,0:T(8,128)(2,1)S(1)} all-to-all(bf16[32,2,64,128]{3,2,1,0:T(8,128)(2,1)S(1)} %broadcast_in_dim.40), channel_id=1, replica_groups=mesh['sub_0'=8,'sub_1'=2,'blk_0'=4,'blk_1'=8] {'blk_0','blk_1'}, dimensions={0} | all-to-all | bytes 2097152 | tf_op jit(solution)/shard_map/all_to_all | solution.py:24
  224.3 11.1 %psum.172 = f32[2,64]{1,0:T(2,128)S(1)} all-reduce(f32[2,64]{1,0:T(2,128)S(1)} %pad_maximum_fusion.8), channel_id=1, replica_groups=mesh['sub_0'=8,'sub_1'=2,'blk_0'=4,'blk_1'=8] {'sub_0'}, use_global_device_ids=true, to_apply=%region_8.10 | all-reduce | flops 128 | bytes 1024 | tf_op jit(solution)/shard_map/psum | solution.py:42
  235.4 9.8 %psum.173 = f32[2,64]{1,0:T(2,128)S(1)} all-reduce(f32[2,64]{1,0:T(2,128)S(1)} %psum.172), channel_id=1, replica_groups=mesh['sub_0'=8,'sub_1'=2,'blk_0'=4,'blk_1'=8] {'sub_1'}, use_global_device_ids=true, to_apply=%region_9.11 | all-reduce | flops 128 | bytes 1024 | tf_op jit(solution)/shard_map/psum | solution.py:42
  245.3 6.5 psum.174
  251.7 12.8 %psum.175 = f32[2,64]{1,0:T(2,128)S(1)} all-reduce(f32[2,64]{1,0:T(2,128)S(1)} %psum.174), channel_id=1, replica_groups=mesh['sub_0'=8,'sub_1'=2,'blk_0'=4,'blk_1'=8] {'blk_1'}, use_global_device_ids=true, to_apply=%region_11.13 | all-reduce | flops 128 | bytes 1024 | tf_op jit(solution)/shard_map/psum | solution.py:42
  266.0 24.4 %all_to_all.62 = bf16[32,2,64,128]{3,2,1,0:T(8,128)(2,1)S(1)} all-to-all(bf16[32,2,64,128]{3,2,1,0:T(8,128)(2,1)S(1)} %broadcast_in_dim.41), channel_id=1, replica_groups=mesh['sub_0'=8,'sub_1'=2,'blk_0'=4,'blk_1'=8] {'blk_0','blk_1'}, dimensions={0} | all-to-all | bytes 2097152 | tf_op jit(solution)/shard_map/all_to_all | solution.py:24
  302.3 10.8 %collective-permute-start.5 = (bf16[2,32,128]{2,0,1:T(2,128)(2,1)}, bf16[2,32,128]{2,0,1:T(2,128)(2,1)S(1)}, u32[]{:S(2)}, u32[]{:S(2)}) collective-permute-start(bf16[2,32,128]{2,0,1:T(2,128)(2,1)} %fusion.18), channel_id=1, source_target_pairs={{32,0},{64,32},{96,64},{128,96},{160,128},{192,160},{224,192},{256... | collective-permute-start | bytes 49160 | tf_op jit(solution)/shard_map/ppermute | solution.py:19
  319.6 33.4 %all_to_all.63 = bf16[32,2,64,128]{3,2,1,0:T(8,128)(2,1)S(1)} all-to-all(bf16[32,2,64,128]{3,2,1,0:T(8,128)(2,1)S(1)} %broadcast_in_dim.42), channel_id=1, replica_groups=mesh['sub_0'=8,'sub_1'=2,'blk_0'=4,'blk_1'=8] {'blk_0','blk_1'}, dimensions={0} | all-to-all | bytes 2097152 | tf_op jit(solution)/shard_map/all_to_all | solution.py:24
  355.1 12.0 %psum.176 = f32[3,64]{1,0:T(4,128)S(1)} all-reduce(f32[3,64]{1,0:T(4,128)S(1)} %pad_maximum_fusion.6), channel_id=1, replica_groups=mesh['sub_0'=8,'sub_1'=2,'blk_0'=4,'blk_1'=8] {'sub_0'}, use_global_device_ids=true, to_apply=%region_15.17 | all-reduce | flops 192 | bytes 1536 | tf_op jit(solution)/shard_map/psum | solution.py:42
  367.1 6.6 psum.177
  373.7 6.5 psum.178
  380.2 13.4 %psum.179 = f32[3,64]{1,0:T(4,128)S(1)} all-reduce(f32[3,64]{1,0:T(4,128)S(1)} %psum.178), channel_id=1, replica_groups=mesh['sub_0'=8,'sub_1'=2,'blk_0'=4,'blk_1'=8] {'blk_1'}, use_global_device_ids=true, to_apply=%region_18.20 | all-reduce | flops 192 | bytes 1536 | tf_op jit(solution)/shard_map/psum | solution.py:42
  395.2 24.3 %all_to_all.64 = bf16[32,2,64,128]{3,2,1,0:T(8,128)(2,1)S(1)} all-to-all(bf16[32,2,64,128]{3,2,1,0:T(8,128)(2,1)S(1)} %broadcast_in_dim.43), channel_id=1, replica_groups=mesh['sub_0'=8,'sub_1'=2,'blk_0'=4,'blk_1'=8] {'blk_0','blk_1'}, dimensions={0} | all-to-all | bytes 2097152 | tf_op jit(solution)/shard_map/all_to_all | solution.py:24
  419.5 3.7 slice.1145
  432.1 11.3 %collective-permute-start.7 = (bf16[2,32,128]{2,0,1:T(2,128)(2,1)}, bf16[2,32,128]{2,0,1:T(2,128)(2,1)}, u32[]{:S(2)}, u32[]{:S(2)}) collective-permute-start(bf16[2,32,128]{2,0,1:T(2,128)(2,1)} %fusion.19), channel_id=1, source_target_pairs={{32,0},{64,32},{96,64},{128,96},{160,128},{192,160},{224,192},{256... | collective-permute-start | bytes 49160 | tf_op jit(solution)/shard_map/ppermute | solution.py:19
  449.3 30.4 %all_to_all.65 = bf16[32,2,64,128]{3,2,1,0:T(8,128)(2,1)S(1)} all-to-all(bf16[32,2,64,128]{3,2,1,0:T(8,128)(2,1)S(1)} %broadcast_in_dim.44), channel_id=1, replica_groups=mesh['sub_0'=8,'sub_1'=2,'blk_0'=4,'blk_1'=8] {'blk_0','blk_1'}, dimensions={0} | all-to-all | bytes 2097152 | tf_op jit(solution)/shard_map/all_to_all | solution.py:24
  481.9 16.2 %psum.180 = f32[4,64]{1,0:T(4,128)S(1)} all-reduce(f32[4,64]{1,0:T(4,128)S(1)} %pad_maximum_fusion.7), channel_id=1, replica_groups=mesh['sub_0'=8,'sub_1'=2,'blk_0'=4,'blk_1'=8] {'sub_0'}, use_global_device_ids=true, to_apply=%region_24.26 | all-reduce | flops 256 | bytes 2048 | tf_op jit(solution)/shard_map/psum | solution.py:42
  498.0 6.1 psum.181
  504.1 6.5 psum.182
  510.6 13.2 %psum.183 = f32[4,64]{1,0:T(4,128)S(1)} all-reduce(f32[4,64]{1,0:T(4,128)S(1)} %psum.182), channel_id=1, replica_groups=mesh['sub_0'=8,'sub_1'=2,'blk_0'=4,'blk_1'=8] {'blk_1'}, use_global_device_ids=true, to_apply=%region_27.29 | all-reduce | flops 256 | bytes 2048 | tf_op jit(solution)/shard_map/psum | solution.py:42
  525.3 23.8 %all_to_all.66 = bf16[32,2,64,128]{3,2,1,0:T(8,128)(2,1)S(1)} all-to-all(bf16[32,2,64,128]{3,2,1,0:T(8,128)(2,1)S(1)} %broadcast_in_dim.45), channel_id=1, replica_groups=mesh['sub_0'=8,'sub_1'=2,'blk_0'=4,'blk_1'=8] {'blk_0','blk_1'}, dimensions={0} | all-to-all | bytes 2097152 | tf_op jit(solution)/shard_map/all_to_all | solution.py:24
  562.4 10.8 %collective-permute-start.9 = (bf16[2,32,128]{2,0,1:T(2,128)(2,1)}, bf16[2,32,128]{2,0,1:T(2,128)(2,1)}, u32[]{:S(2)}, u32[]{:S(2)}) collective-permute-start(bf16[2,32,128]{2,0,1:T(2,128)(2,1)} %fusion.20), channel_id=1, source_target_pairs={{32,0},{64,32},{96,64},{128,96},{160,128},{192,160},{224,192},{256... | collective-permute-start | bytes 49160 | tf_op jit(solution)/shard_map/ppermute | solution.py:19
  579.8 30.8 %all_to_all.67 = bf16[32,2,64,128]{3,2,1,0:T(8,128)(2,1)S(1)} all-to-all(bf16[32,2,64,128]{3,2,1,0:T(8,128)(2,1)S(1)} %broadcast_in_dim.46), channel_id=1, replica_groups=mesh['sub_0'=8,'sub_1'=2,'blk_0'=4,'blk_1'=8] {'blk_0','blk_1'}, dimensions={0} | all-to-all | bytes 2097152 | tf_op jit(solution)/shard_map/all_to_all | solution.py:24
  612.9 16.0 %psum.184 = f32[5,64]{1,0:T(8,128)S(1)} all-reduce(f32[5,64]{1,0:T(8,128)S(1)} %stack.288), channel_id=1, replica_groups=mesh['sub_0'=8,'sub_1'=2,'blk_0'=4,'blk_1'=8] {'sub_0'}, use_global_device_ids=true, to_apply=%region_34.36 | all-reduce | flops 320 | bytes 2560 | tf_op jit(solution)/shard_map/psum | solution.py:42
  628.9 6.3 psum.185
  635.2 6.5 psum.186
  641.7 13.1 %psum.187 = f32[5,64]{1,0:T(8,128)S(1)} all-reduce(f32[5,64]{1,0:T(8,128)S(1)} %psum.186), channel_id=1, replica_groups=mesh['sub_0'=8,'sub_1'=2,'blk_0'=4,'blk_1'=8] {'blk_1'}, use_global_device_ids=true, to_apply=%region_37.39 | all-reduce | flops 320 | bytes 2560 | tf_op jit(solution)/shard_map/psum | solution.py:42
  657.0 24.0 %all_to_all.68 = bf16[32,2,64,128]{3,2,1,0:T(8,128)(2,1)S(1)} all-to-all(bf16[32,2,64,128]{3,2,1,0:T(8,128)(2,1)S(1)} %broadcast_in_dim.47), channel_id=1, replica_groups=mesh['sub_0'=8,'sub_1'=2,'blk_0'=4,'blk_1'=8] {'blk_0','blk_1'}, dimensions={0} | all-to-all | bytes 2097152 | tf_op jit(solution)/shard_map/all_to_all | solution.py:24
  694.2 11.3 %collective-permute-start.11 = (bf16[2,32,128]{2,0,1:T(2,128)(2,1)}, bf16[2,32,128]{2,0,1:T(2,128)(2,1)}, u32[]{:S(2)}, u32[]{:S(2)}) collective-permute-start(bf16[2,32,128]{2,0,1:T(2,128)(2,1)} %fusion.21), channel_id=1, source_target_pairs={{32,0},{64,32},{96,64},{128,96},{160,128},{192,160},{224,192},{256... | collective-permute-start | bytes 49160 | tf_op jit(solution)/shard_map/ppermute | solution.py:19
  713.4 5.4 all-to-all-start.11
  725.6 18.4 %all-to-all-done.11 = bf16[32,2,64,128]{3,2,1,0:T(8,128)(2,1)S(1)} async-done(((bf16[32,2,64,128]{3,2,1,0:T(8,128)(2,1)}), bf16[32,2,64,128]{3,2,1,0:T(8,128)(2,1)S(1)}, u32[]{:S(2)}, u32[]{:S(2)}) %all-to-all-start.11) | async-done | bytes 1048608 | tf_op jit(solution)/shard_map/all_to_all | solution.py:24
  747.1 15.8 %psum.188 = f32[6,64]{1,0:T(8,128)S(1)} all-reduce(f32[6,64]{1,0:T(8,128)S(1)} %stack.302), channel_id=1, replica_groups=mesh['sub_0'=8,'sub_1'=2,'blk_0'=4,'blk_1'=8] {'sub_0'}, use_global_device_ids=true, to_apply=%region_45.47 | all-reduce | flops 384 | bytes 3072 | tf_op jit(solution)/shard_map/psum | solution.py:42
  762.8 6.3 psum.189
  769.2 6.5 psum.190
  775.6 12.9 %psum.191 = f32[6,64]{1,0:T(8,128)S(1)} all-reduce(f32[6,64]{1,0:T(8,128)S(1)} %psum.190), channel_id=1, replica_groups=mesh['sub_0'=8,'sub_1'=2,'blk_0'=4,'blk_1'=8] {'blk_1'}, use_global_device_ids=true, to_apply=%region_48.50 | all-reduce | flops 384 | bytes 3072 | tf_op jit(solution)/shard_map/psum | solution.py:42
  790.5 29.4 %custom-call.11 = f32[64,5,5]{2,1,0:T(8,128)S(1)} custom-call(f32[64,5,5]{2,1,0:T(8,128)S(1)} %fusion), custom_call_target="Cholesky" | custom-call | tf_op jit(solution)/shard_map/jit(cholesky)/cholesky | solution.py:149
  (481 shorter events, 138.0 us)
Async XLA Ops:
  0.0 56.9 %copy-start = (bf16[1,2,64,2048]{3,2,1,0:T(8,128)(2,1)S(1)}, bf16[1,2,64,2048]{3,2,1,0:T(8,128)(2,1)}, u32[]{:S(2)}) copy-start(bf16[1,2,64,2048]{3,2,1,0:T(8,128)(2,1)} %param.16) | copy-start | bytes 1572868
  2.9 35.4 %all-to-all-start = ((bf16[32,2,64,128]{3,2,1,0:T(8,128)(2,1)}), bf16[32,2,64,128]{3,2,1,0:T(8,128)(2,1)S(1)}, u32[]{:S(2)}, u32[]{:S(2)}) async-start(bf16[32,2,64,128]{3,2,1,0:T(8,128)(2,1)} %broadcast_in_dim.37), calls=%async_computation | async-start | bytes 2097152 | tf_op jit(solution)/shard_map/all_to_all | solution.py:24
  18.6 157.0 %copy-start.30 = (pred[32]{0:T(512)(128)(4,1)}, pred[32]{0:T(512)(128)(4,1)S(1)}, u32[]{:S(2)}) copy-start(pred[32]{0:T(512)(128)(4,1)S(1)} %get-tuple-element.40) | copy-start | bytes 100
  19.4 168.4 %copy-start.25 = (pred[32]{0:T(512)(128)(4,1)}, pred[32]{0:T(512)(128)(4,1)S(1)}, u32[]{:S(2)}) copy-start(pred[32]{0:T(512)(128)(4,1)S(1)} %get-tuple-element.38) | copy-start | bytes 100
  19.4 155.6 %copy-start.39 = (s32[1024]{0:T(1024)}, s32[1024]{0:T(1024)S(1)}, u32[]{:S(2)}) copy-start(s32[1024]{0:T(1024)S(1)} %get-tuple-element.215) | copy-start | bytes 12292
  19.4 167.7 %copy-start.38 = (s32[1024]{0:T(1024)}, s32[1024]{0:T(1024)S(1)}, u32[]{:S(2)}) copy-start(s32[1024]{0:T(1024)S(1)} %get-tuple-element.216) | copy-start | bytes 12292
  42.7 15.9 %collective-permute-start = (bf16[2,32,128]{2,0,1:T(2,128)(2,1)S(1)}, bf16[2,32,128]{2,0,1:T(2,128)(2,1)S(1)}, u32[]{:S(2)}, u32[]{:S(2)}) collective-permute-start(bf16[2,32,128]{2,0,1:T(2,128)(2,1)S(1)} %fusion.10), channel_id=1, source_target_pairs={{0,32},{32,64},{64,96},{96,128},{128,160},{160,192},{192,224},{224... | collective-permute-start | bytes 49160 | tf_op jit(solution)/shard_map/ppermute | solution.py:19
  52.6 6.1 collective-permute-start.1
  54.5 1.0 copy-start.2
  55.6 1.0 copy-start.3
  56.9 1.0 copy-start.1
  60.8 5.0 copy-start.24
  60.8 31.8 %all-to-all-start.1 = ((bf16[32,2,64,128]{3,2,1,0:T(8,128)(2,1)}), bf16[32,2,64,128]{3,2,1,0:T(8,128)(2,1)S(1)}, u32[]{:S(2)}, u32[]{:S(2)}) async-start(bf16[32,2,64,128]{3,2,1,0:T(8,128)(2,1)} %broadcast_in_dim.38), calls=%async_computation.1 | async-start | bytes 2097152 | tf_op jit(solution)/shard_map/all_to_all | solution.py:24
  173.4 1.0 copy-start.9
  174.5 12.1 %copy-start.5 = (bf16[2,1024,128]{2,1,0:T(8,128)(2,1)S(1)}, bf16[2,1024,128]{2,1,0:T(8,128)(2,1)}, u32[]{:S(2)}) copy-start(bf16[2,1024,128]{2,1,0:T(8,128)(2,1)} %slice.1052) | copy-start | bytes 1572868
  175.7 14.6 %collective-permute-start.3 = (bf16[2,32,128]{2,0,1:T(2,128)(2,1)S(1)}, bf16[2,32,128]{2,0,1:T(2,128)(2,1)S(1)}, u32[]{:S(2)}, u32[]{:S(2)}) collective-permute-start(bf16[2,32,128]{2,0,1:T(2,128)(2,1)S(1)} %fusion.17), channel_id=1, source_target_pairs={{32,0},{64,32},{96,64},{128,96},{160,128},{192,160},{224,192},{256... | collective-permute-start | bytes 49160 | tf_op jit(solution)/shard_map/ppermute | solution.py:19
  187.9 3.1 collective-permute-start.2
  298.7 1.0 copy-start.10
  299.7 13.5 %copy-start.6 = (bf16[2,1024,128]{2,1,0:T(8,128)(2,1)S(1)}, bf16[2,1024,128]{2,1,0:T(8,128)(2,1)}, u32[]{:S(2)}) copy-start(bf16[2,1024,128]{2,1,0:T(8,128)(2,1)} %slice.1096) | copy-start | bytes 1572868
  302.3 15.9 %collective-permute-start.5 = (bf16[2,32,128]{2,0,1:T(2,128)(2,1)}, bf16[2,32,128]{2,0,1:T(2,128)(2,1)S(1)}, u32[]{:S(2)}, u32[]{:S(2)}) collective-permute-start(bf16[2,32,128]{2,0,1:T(2,128)(2,1)} %fusion.18), channel_id=1, source_target_pairs={{32,0},{64,32},{96,64},{128,96},{160,128},{192,160},{224,192},{256... | collective-permute-start | bytes 49160 | tf_op jit(solution)/shard_map/ppermute | solution.py:19
  314.6 4.0 collective-permute-start.4
  428.4 1.0 copy-start.11
  429.4 14.0 %copy-start.7 = (bf16[2,1024,128]{2,1,0:T(8,128)(2,1)S(1)}, bf16[2,1024,128]{2,1,0:T(8,128)(2,1)}, u32[]{:S(2)}) copy-start(bf16[2,1024,128]{2,1,0:T(8,128)(2,1)} %slice.1144) | copy-start | bytes 1572868
  432.1 15.4 %collective-permute-start.7 = (bf16[2,32,128]{2,0,1:T(2,128)(2,1)}, bf16[2,32,128]{2,0,1:T(2,128)(2,1)}, u32[]{:S(2)}, u32[]{:S(2)}) collective-permute-start(bf16[2,32,128]{2,0,1:T(2,128)(2,1)} %fusion.19), channel_id=1, source_target_pairs={{32,0},{64,32},{96,64},{128,96},{160,128},{192,160},{224,192},{256... | collective-permute-start | bytes 49160 | tf_op jit(solution)/shard_map/ppermute | solution.py:19
  443.4 1.4 copy-start.27
  444.0 2.9 copy-start.17
  445.0 3.2 collective-permute-start.6
  523.8 0.8 copy-start.37
  558.7 1.0 copy-start.12
  559.7 13.5 %copy-start.8 = (bf16[2,1024,128]{2,1,0:T(8,128)(2,1)S(1)}, bf16[2,1024,128]{2,1,0:T(8,128)(2,1)}, u32[]{:S(2)}) copy-start(bf16[2,1024,128]{2,1,0:T(8,128)(2,1)} %slice.1195) | copy-start | bytes 1572868
  562.4 15.7 %collective-permute-start.9 = (bf16[2,32,128]{2,0,1:T(2,128)(2,1)}, bf16[2,32,128]{2,0,1:T(2,128)(2,1)}, u32[]{:S(2)}, u32[]{:S(2)}) collective-permute-start(bf16[2,32,128]{2,0,1:T(2,128)(2,1)} %fusion.20), channel_id=1, source_target_pairs={{32,0},{64,32},{96,64},{128,96},{160,128},{192,160},{224,192},{256... | collective-permute-start | bytes 49160 | tf_op jit(solution)/shard_map/ppermute | solution.py:19
  573.2 1.4 copy-start.28
  573.8 2.9 copy-start.18
  574.8 4.0 collective-permute-start.8
  576.7 0.8 copy-start.15
  654.8 0.9 copy-start.36
  690.5 1.0 copy-start.13
  691.6 14.0 %copy-start.4 = (bf16[2,1024,128]{2,1,0:T(8,128)(2,1)S(1)}, bf16[2,1024,128]{2,1,0:T(8,128)(2,1)}, u32[]{:S(2)}) copy-start(bf16[2,1024,128]{2,1,0:T(8,128)(2,1)} %slice.1249) | copy-start | bytes 1572868
  694.2 16.4 %collective-permute-start.11 = (bf16[2,32,128]{2,0,1:T(2,128)(2,1)}, bf16[2,32,128]{2,0,1:T(2,128)(2,1)}, u32[]{:S(2)}, u32[]{:S(2)}) collective-permute-start(bf16[2,32,128]{2,0,1:T(2,128)(2,1)} %fusion.21), channel_id=1, source_target_pairs={{32,0},{64,32},{96,64},{128,96},{160,128},{192,160},{224,192},{256... | collective-permute-start | bytes 49160 | tf_op jit(solution)/shard_map/ppermute | solution.py:19
  705.5 1.4 copy-start.29
  706.1 3.2 copy-start.16
  707.1 4.2 collective-permute-start.10
  709.3 0.8 copy-start.14
  713.4 30.6 %all-to-all-start.11 = ((bf16[32,2,64,128]{3,2,1,0:T(8,128)(2,1)}), bf16[32,2,64,128]{3,2,1,0:T(8,128)(2,1)S(1)}, u32[]{:S(2)}, u32[]{:S(2)}) async-start(bf16[32,2,64,128]{3,2,1,0:T(8,128)(2,1)} %broadcast_in_dim.48), calls=%async_computation.11 | async-start | bytes 2097152 | tf_op jit(solution)/shard_map/all_to_all | solution.py:24
  719.5 5.4 copy-start.47
  745.7 0.8 copy-start.23
  820.0 0.9 copy-start.22
  820.1 0.9 copy-start.20
  (28 other events, 18.1 us)
where the time goes:
time: 836 us; the launch traced here: 822 us
  blocking collectives  496 us (59%)
  starting transfers between devices  97.6 us (12%)
  local copies, waits for them, and re-layouts  88.4 us (11%)
  waiting for transfers between devices  64.9 us (8%)
  other arithmetic  55.6 us (7%)
  matrix products  17.5 us (2%)
    psum x24, blocking collectives, over_axes(): value = lax.psum(value, axis)  249 us
    all_to_all x9, blocking collectives, copy_for_each(): lax.all_to_all(jnp.broadcast_to(value[None], (peers, *value.shape)), axis...  247 us
    ppermute x12, starting transfers between devices, passed_along(): return lax.ppermute(block, axis, route)  76.8 us
    all_to_all x3, waiting for transfers between devices, copy_for_each(): lax.all_to_all(jnp.broadcast_to(value[None], (peers, *value.shape)), axis...  64 us
    another operation x4, other arithmetic, body(): factor = jnp.linalg.cholesky(gram)  29.5 us
    unnamed x139, local copies, waits for them, and re-layouts  26.8 us
    all_to_all x3, starting transfers between devices, copy_for_each(): lax.all_to_all(jnp.broadcast_to(value[None], (peers, *value.shape)), axis...  20.8 us
    slice x6, local copies, waits for them, and re-layouts, coupling_rows(): even_rows = gathered[:, 0::2]  19.9 us
  transfers between devices with their start and end apart: 15, of which 5 were waited for; matrix products, arithmetic and copies ran while one was open for 3% of the time, Pallas kernels for 0%

commit v1 on v0

v1 whole, which is shorter than its diff:
```python
import jax
import jax.numpy as jnp
from jax import lax
from jax.sharding import Mesh
from jax.sharding import PartitionSpec as P

BASIS = 5
SUB = ("sub_0", "sub_1")
BLK = ("blk_0", "blk_1")


EPSILON = 1e-06


def passed_along(block, axis, distance):
    devices = range(lax.axis_size(axis))
    route = [(i - distance, i) for i in devices if i - distance in devices]
    return lax.ppermute(block, axis, route)


def copy_for_each(value, axis):
    peers = lax.axis_size(axis)
    return lax.all_to_all(
        jnp.broadcast_to(value[None], (peers, *value.shape)), axis, 0, 0, tiled=True
    )


def summed_over(value, axis):
    return jnp.sum(copy_for_each(value, axis), axis=0)


def summed_everywhere(value):
    return summed_over(summed_over(value, SUB), BLK)


def inward(field):
    local_field = field[0]
    return jnp.concatenate([local_field[:, 0], local_field[:, 1]], axis=-1)


def outward(vector):
    width = vector.shape[-1] // 2
    return jnp.stack([vector[..., :width], vector[..., width:]], axis=1)[None]


def tile_of_operators(double_layer, single_layer, hypersingular, adjoint_double):
    columns = lax.axis_size("blk_0")
    grid = ((-double_layer, single_layer), (hypersingular, adjoint_double))
    traces = []
    for line in grid:
        pieces = []
        for part in range(2):
            for operator in line:
                rows, full = operator[part].shape
                pieces.append(
                    jnp.moveaxis(operator[part].reshape(rows, columns, full // columns), 1, 0)
                )
        traces.append(jnp.concatenate(pieces, axis=-1))
    strips = jnp.concatenate(traces, axis=1)
    blocks = lax.all_to_all(strips, "blk_0", 0, 0, tiled=True)
    return blocks.reshape(-1, blocks.shape[-1])


def selectors(matching, local_rows):
    subdomains = lax.axis_size(SUB)
    lines = lax.axis_size("blk_0")
    own_index = lax.axis_index(SUB)
    above_index = jnp.minimum(own_index + 1, subdomains - 1)
    perm_here = lax.dynamic_index_in_dim(matching, own_index, 0, keepdims=False)
    perm_above = lax.dynamic_index_in_dim(matching, above_index, 0, keepdims=False)
    half_rows = local_rows // 2
    half = perm_here.shape[0]
    spots = jnp.arange(half, dtype=jnp.int32)

    def window(values):
        table = values.reshape(lines, lax.axis_size("blk_1"), half_rows)
        return lax.dynamic_index_in_dim(
            table, lax.axis_index("blk_1"), 1, keepdims=False
        ).reshape(-1)

    wanted = window(spots)
    inverse_here = jnp.sum(
        jnp.where(perm_here[None, :] == wanted[:, None], spots[None, :], 0), axis=1
    )
    dofs = jnp.concatenate([2 * window(perm_above) + 1, 2 * inverse_here])
    width = 2 * half // lines
    columns = lax.axis_index("blk_0") * width + jnp.arange(width, dtype=jnp.int32)
    return (dofs[:, None] == columns[None, :]).astype(jnp.bfloat16)


def gathered_columns(vector):
    blocks = copy_for_each(vector, "blk_1")
    return jnp.moveaxis(blocks, 0, 1).reshape(
        vector.shape[0], blocks.shape[0] * vector.shape[1], vector.shape[2]
    )


def partial_products(tile, columns):
    width = columns.shape[-1] // 2
    turned = jnp.concatenate([-columns[..., width:], columns[..., :width]], axis=-1)
    stacked = jnp.stack([columns, turned]).reshape(tile.shape[1], 2 * width)
    products = jnp.dot(tile, stacked, preferred_element_type=jnp.float32)
    return products.reshape(lax.axis_size("blk_0"), 2, -1, 2 * width)


def coupling_partials(selector, columns):
    lines = lax.axis_size("blk_0")
    chosen = jnp.einsum(
        "sk,tkn->tsn", selector, columns, preferred_element_type=jnp.float32
    ).astype(jnp.bfloat16)
    middle = chosen.shape[1] // 2
    lower_face = passed_along(chosen[:, :middle], SUB, 1)
    upper_face = passed_along(chosen[:, middle:], SUB, -1)
    joined = jnp.stack([lower_face, upper_face], axis=2)
    joined = joined.reshape(2, lines, 2 * middle // lines, chosen.shape[-1])
    signs = jnp.array([1.0, -1.0], jnp.float32).reshape(1, 2, 1, 1)
    return jnp.moveaxis(joined, 1, 0).astype(jnp.float32) * signs


def reduced_rows(partials):
    return jnp.sum(lax.all_to_all(partials, "blk_0", 0, 0, tiled=True), axis=0)


def preconditioned(tile, selector, vector):
    columns = gathered_columns(vector.astype(jnp.bfloat16))
    first = partial_products(tile, columns) - 0.5 * coupling_partials(selector, columns)
    middle = reduced_rows(first)
    middle_columns = gathered_columns(middle.astype(jnp.bfloat16))
    return reduced_rows(partial_products(tile, middle_columns))


def inner_local(first, second):
    totals = jnp.sum(first * second, axis=(0, 1))
    width = totals.shape[0] // 2
    return totals[:width] + totals[width:]


def spread(values):
    return jnp.concatenate([values, values])


def least_squares(hessen, beta):
    gram = [
        [sum(a * b for a, b in zip(hessen[row], hessen[column])) for column in range(row + 1)]
        for row in range(BASIS)
    ]
    factor = [[None] * BASIS for _ in range(BASIS)]
    inverse = [None] * BASIS
    for row in range(BASIS):
        for column in range(row):
            rest = gram[row][column]
            for k in range(column):
                rest = rest - factor[row][k] * factor[column][k]
            factor[row][column] = rest * inverse[column]
        rest = gram[row][row]
        for k in range(row):
            rest = rest - factor[row][k] * factor[row][k]
        factor[row][row] = jnp.sqrt(rest)
        inverse[row] = 1.0 / factor[row][row]
    forward = []
    for row in range(BASIS):
        rest = beta * hessen[row][0]
        for k in range(row):
            rest = rest - factor[row][k] * forward[k]
        forward.append(rest * inverse[row])
    weights = [None] * BASIS
    for row in reversed(range(BASIS)):
        rest = forward[row]
        for k in range(row + 1, BASIS):
            rest = rest - factor[k][row] * weights[k]
        weights[row] = rest * inverse[row]
    return weights


def body(double_layer, single_layer, hypersingular, adjoint_double, matching, right_side, start):
    tile = tile_of_operators(
        double_layer[0], single_layer[0], hypersingular[0], adjoint_double[0]
    )
    right_local = inward(right_side)
    start_local = inward(start)
    selector = selectors(matching, right_local.shape[1])
    residual = right_local - preconditioned(tile, selector, start_local)
    beta = jnp.sqrt(summed_everywhere(inner_local(residual, residual)[None])[0] + EPSILON)
    basis = [residual / spread(beta)]
    hessen = []
    for column in range(BASIS):
        image = preconditioned(tile, selector, basis[column])
        local_dots = [inner_local(vector, image) for vector in basis]
        summed = summed_everywhere(jnp.stack(local_dots + [inner_local(image, image)]))
        squares = summed[column + 1] - jnp.sum(summed[: column + 1] * summed[: column + 1], axis=0)
        height = jnp.sqrt(jnp.maximum(squares, 0.0) + EPSILON)
        if column + 1 < BASIS:
            for earlier in range(column + 1):
                image = image - spread(summed[earlier]) * basis[earlier]
            basis.append(image / spread(height))
        filler = [jnp.zeros_like(height)] * (BASIS - 1 - column)
        hessen.append([summed[earlier] for earlier in range(column + 1)] + [height] + filler)
    weights = least_squares(hessen, beta)
    solution = start_local
    for column in range(BASIS):
        solution = solution + spread(weights[column]) * basis[column]
    return outward(solution)


def solution(mesh):
    torus = Mesh(mesh.devices.reshape(8, 2, 4, 8), ("sub_0", "sub_1", "blk_0", "blk_1"))
    placed = (
        P(SUB, None, BLK, None),
        P(SUB, None, BLK, None),
        P(SUB, None, BLK, None),
        P(SUB, None, BLK, None),
        P(),
        P(SUB, None, None, BLK, None),
        P(SUB, None, None, BLK, None),
    )
    return jax.shard_map(
        body, mesh=torus, in_specs=placed, out_specs=P(SUB, None, None, BLK, None), check_vma=False
    )
```

time: 836 us -> 532 us (0.64); the launches traced: 822 us -> 530 us
  blocking collectives: 496 us -> 384 us
  local copies, waits for them, and re-layouts: 88.4 us -> 12.4 us
  other arithmetic: 55.6 us -> 20.1 us
  starting transfers between devices: 97.6 us -> 62.9 us
  waiting for transfers between devices: 64.9 us -> 37.4 us
    psum x24 -> x0, blocking collectives: 249 us -> none  [over_axes(): value = lax.psum(value, axis)]
    all_to_all x0 -> x11, blocking collectives: none -> 91.8 us  [reduced_rows(): return jnp.sum(lax.all_to_all(partials, 'blk_0', 0, 0, tiled=True), axis=0)]
    all_to_all x3 -> x2, waiting for transfers between devices: 64 us -> 12.8 us  [copy_for_each(): lax.all_to_all(jnp.broadcast_to(value[None], (peers, *value.shape)), axis...]
    all_to_all x9 -> x22, blocking collectives: 247 us -> 292 us  [copy_for_each(): lax.all_to_all(jnp.broadcast_to(value[None], (peers, *value.shape)), axis...]
    slice x25 -> x10, local copies, waits for them, and re-layouts: 40.5 us -> 1.4 us  [the longest x4 1.25 us: tile_of_operators(): operator[part].reshape(rows, columns, full // columns)]
    ppermute x12, starting transfers between devices: 76.8 us -> 42.9 us  [passed_along(): return lax.ppermute(block, axis, route)]
    another operation x32 -> x47, other arithmetic: 31.9 us -> 3.9 us  [the longest x24 2.41 us: partial_products(): stacked = jnp.stack([columns, turned]).reshape(tile.shape[1], 2 * width)]
    unnamed x139 -> x106, local copies, waits for them, and re-layouts: 26.8 us -> 4.1 us
  transfers between devices with their start and end apart: 15 -> 16, of which waited for: 5 -> 10; matrix products, arithmetic and copies ran while one was open for 3% -> 2% of each run, Pallas kernels for 0% -> 0%
where the time goes in v1:
time: 532 us; the launch traced here: 530 us
  blocking collectives  384 us (72%)
  starting transfers between devices  62.9 us (12%)
  waiting for transfers between devices  37.4 us (7%)
  other arithmetic  20.1 us (4%)
  local copies, waits for them, and re-layouts  12.4 us (2%)
  matrix products  11.3 us (2%)
    all_to_all x22, blocking collectives, copy_for_each(): lax.all_to_all(jnp.broadcast_to(value[None], (peers, *value.shape)), axis...  292 us
    all_to_all x11, blocking collectives, reduced_rows(): return jnp.sum(lax.all_to_all(partials, 'blk_0', 0, 0, tiled=True), axis=0)  91.8 us
    ppermute x12, starting transfers between devices, passed_along(): return lax.ppermute(block, axis, route)  42.9 us
    all_to_all x1, waiting for transfers between devices, tile_of_operators(): blocks = lax.all_to_all(strips, 'blk_0', 0, 0, tiled=True)  13 us
    all_to_all x2, waiting for transfers between devices, copy_for_each(): lax.all_to_all(jnp.broadcast_to(value[None], (peers, *value.shape)), axis...  12.8 us
    all_to_all x2, starting transfers between devices, copy_for_each(): lax.all_to_all(jnp.broadcast_to(value[None], (peers, *value.shape)), axis...  11.5 us
  transfers between devices with their start and end apart: 16, of which 10 were waited for; matrix products, arithmetic and copies ran while one was open for 2% of the time, Pallas kernels for 0%

profile of v1, /device:TPU:1, one launch (start us, length us, event | category | flops | bytes accessed | tf_op | source)
XLA Modules:
  0.0 529.7 jit_solution(14475091750694610466)
XLA Ops:
  1.9 7.6 %all-to-all-start.1 = ((bf16[8,2,64,128]{3,2,1,0:T(8,128)(2,1)}), bf16[8,2,64,128]{3,2,1,0:T(8,128)(2,1)S(1)}, u32[]{:S(2)}, u32[]{:S(2)}) async-start(bf16[8,2,64,128]{3,2,1,0:T(8,128)(2,1)} %broadcast_in_dim.62), calls=%async_computation.1 | async-start | bytes 524288 | tf_op jit(solution)/shard_map/all_to_all | solution.py:23
  15.5 3.5 all-to-all-done.1
  18.9 5.1 all-to-all-start
  24.9 4.5 collective-permute-start.1
  29.4 3.9 collective-permute-start
  34.8 13.0 %all-to-all-done = bf16[4,128,2048]{2,1,0:T(8,128)(2,1)S(1)} async-done(((bf16[4,128,2048]{2,1,0:T(8,128)(2,1)}), bf16[4,128,2048]{2,1,0:T(8,128)(2,1)S(1)}, u32[]{:S(2)}, u32[]{:S(2)}) %all-to-all-start) | async-done | bytes 2097184 | tf_op jit(solution)/shard_map/all_to_all | solution.py:60
  48.5 7.9 %all_to_all.185 = f32[4,2,64,128]{3,2,1,0:T(8,128)S(1)} all-to-all(f32[4,2,64,128]{3,2,1,0:T(8,128)S(1)} %convolution_subtract_fusion.5), channel_id=1, replica_groups=mesh['sub_0'=8,'sub_1'=2,'blk_0'=4,'blk_1'=8] {'blk_0'}, dimensions={0} | all-to-all | bytes 524288 | tf_op jit(solution)/shard_map/all_to_all | solution.py:121
  57.2 3.9 all-to-all-start.3
  61.1 9.3 %all-to-all-done.3 = bf16[8,2,64,128]{3,2,1,0:T(8,128)(2,1)S(1)} async-done(((bf16[8,2,64,128]{3,2,1,0:T(8,128)(2,1)}), bf16[8,2,64,128]{3,2,1,0:T(8,128)(2,1)S(1)}, u32[]{:S(2)}, u32[]{:S(2)}) %all-to-all-start.3) | async-done | bytes 262176 | tf_op jit(solution)/shard_map/all_to_all | solution.py:23
  72.2 3.4 all-to-all-start.4
  75.7 5.5 %all-to-all-done.4 = f32[4,2,64,128]{3,2,1,0:T(8,128)S(1)} async-done(((f32[4,2,64,128]{3,2,1,0:T(8,128)}), f32[4,2,64,128]{3,2,1,0:T(8,128)S(1)}, u32[]{:S(2)}, u32[]{:S(2)}) %all-to-all-start.4) | async-done | bytes 262176 | tf_op jit(solution)/shard_map/all_to_all | solution.py:121
  81.3 23.5 %all_to_all.186 = f32[16,1,64]{2,1,0:T(1,128)S(1)} all-to-all(f32[16,1,64]{2,1,0:T(1,128)S(1)} %broadcast_in_dim.66), channel_id=1, replica_groups=mesh['sub_0'=8,'sub_1'=2,'blk_0'=4,'blk_1'=8] {'sub_0','sub_1'}, dimensions={0} | all-to-all | bytes 8192 | tf_op jit(solution)/shard_map/all_to_all | solution.py:23
  104.9 11.6 %all_to_all.187 = f32[32,1,64]{2,1,0:T(1,128)S(1)} all-to-all(f32[32,1,64]{2,1,0:T(1,128)S(1)} %broadcast_in_dim.67), channel_id=1, replica_groups=mesh['sub_0'=8,'sub_1'=2,'blk_0'=4,'blk_1'=8] {'blk_0','blk_1'}, dimensions={0} | all-to-all | bytes 16384 | tf_op jit(solution)/shard_map/all_to_all | solution.py:23
  117.3 12.0 %all_to_all.188 = bf16[8,2,64,128]{3,2,1,0:T(8,128)(2,1)S(1)} all-to-all(bf16[8,2,64,128]{3,2,1,0:T(8,128)(2,1)S(1)} %broadcast_in_dim.68), channel_id=1, replica_groups=mesh['sub_0'=8,'sub_1'=2,'blk_0'=4,'blk_1'=8] {'blk_1'}, dimensions={0} | all-to-all | bytes 524288 | tf_op jit(solution)/shard_map/all_to_all | solution.py:23
  129.9 5.1 collective-permute-start.3
  139.3 9.0 %all_to_all.189 = f32[4,2,64,128]{3,2,1,0:T(8,128)S(1)} all-to-all(f32[4,2,64,128]{3,2,1,0:T(8,128)S(1)} %convolution_subtract_fusion.4), channel_id=1, replica_groups=mesh['sub_0'=8,'sub_1'=2,'blk_0'=4,'blk_1'=8] {'blk_0'}, dimensions={0} | all-to-all | bytes 524288 | tf_op jit(solution)/shard_map/all_to_all | solution.py:121
  148.4 12.7 %all_to_all.190 = bf16[8,2,64,128]{3,2,1,0:T(8,128)(2,1)S(1)} all-to-all(bf16[8,2,64,128]{3,2,1,0:T(8,128)(2,1)S(1)} %broadcast_in_dim.69), channel_id=1, replica_groups=mesh['sub_0'=8,'sub_1'=2,'blk_0'=4,'blk_1'=8] {'blk_1'}, dimensions={0} | all-to-all | bytes 524288 | tf_op jit(solution)/shard_map/all_to_all | solution.py:23
  162.2 7.9 %all_to_all.191 = f32[4,2,64,128]{3,2,1,0:T(8,128)S(1)} all-to-all(f32[4,2,64,128]{3,2,1,0:T(8,128)S(1)} %fusion.95), channel_id=1, replica_groups=mesh['sub_0'=8,'sub_1'=2,'blk_0'=4,'blk_1'=8] {'blk_0'}, dimensions={0} | all-to-all | bytes 524288 | tf_op jit(solution)/shard_map/all_to_all | solution.py:121
  170.4 13.8 %all_to_all.192 = f32[16,1,128]{2,1,0:T(1,128)S(1)} all-to-all(f32[16,1,128]{2,1,0:T(1,128)S(1)} %reshape.469), channel_id=1, replica_groups=mesh['sub_0'=8,'sub_1'=2,'blk_0'=4,'blk_1'=8] {'sub_0','sub_1'}, dimensions={0} | all-to-all | bytes 16384 | tf_op jit(solution)/shard_map/all_to_all | solution.py:23
  185.8 11.6 %all_to_all.193 = f32[32,1,128]{2,1,0:T(1,128)S(1)} all-to-all(f32[32,1,128]{2,1,0:T(1,128)S(1)} %reshape.471), channel_id=1, replica_groups=mesh['sub_0'=8,'sub_1'=2,'blk_0'=4,'blk_1'=8] {'blk_0','blk_1'}, dimensions={0} | all-to-all | bytes 32768 | tf_op jit(solution)/shard_map/all_to_all | solution.py:23
  199.0 12.0 %all_to_all.194 = bf16[8,2,64,128]{3,2,1,0:T(8,128)(2,1)S(1)} all-to-all(bf16[8,2,64,128]{3,2,1,0:T(8,128)(2,1)S(1)} %broadcast_in_dim.72), channel_id=1, replica_groups=mesh['sub_0'=8,'sub_1'=2,'blk_0'=4,'blk_1'=8] {'blk_1'}, dimensions={0} | all-to-all | bytes 524288 | tf_op jit(solution)/shard_map/all_to_all | solution.py:23
  211.6 5.1 collective-permute-start.5
  221.1 9.0 %all_to_all.195 = f32[4,2,64,128]{3,2,1,0:T(8,128)S(1)} all-to-all(f32[4,2,64,128]{3,2,1,0:T(8,128)S(1)} %convolution_subtract_fusion.3), channel_id=1, replica_groups=mesh['sub_0'=8,'sub_1'=2,'blk_0'=4,'blk_1'=8] {'blk_0'}, dimensions={0} | all-to-all | bytes 524288 | tf_op jit(solution)/shard_map/all_to_all | solution.py:121
  230.1 12.7 %all_to_all.196 = bf16[8,2,64,128]{3,2,1,0:T(8,128)(2,1)S(1)} all-to-all(bf16[8,2,64,128]{3,2,1,0:T(8,128)(2,1)S(1)} %broadcast_in_dim.73), channel_id=1, replica_groups=mesh['sub_0'=8,'sub_1'=2,'blk_0'=4,'blk_1'=8] {'blk_1'}, dimensions={0} | all-to-all | bytes 524288 | tf_op jit(solution)/shard_map/all_to_all | solution.py:23
  243.9 7.9 %all_to_all.197 = f32[4,2,64,128]{3,2,1,0:T(8,128)S(1)} all-to-all(f32[4,2,64,128]{3,2,1,0:T(8,128)S(1)} %fusion.96), channel_id=1, replica_groups=mesh['sub_0'=8,'sub_1'=2,'blk_0'=4,'blk_1'=8] {'blk_0'}, dimensions={0} | all-to-all | bytes 524288 | tf_op jit(solution)/shard_map/all_to_all | solution.py:121
  252.2 14.1 %all_to_all.198 = f32[16,1,192]{2,1,0:T(1,128)S(1)} all-to-all(f32[16,1,192]{2,1,0:T(1,128)S(1)} %reshape.473), channel_id=1, replica_groups=mesh['sub_0'=8,'sub_1'=2,'blk_0'=4,'blk_1'=8] {'sub_0','sub_1'}, dimensions={0} | all-to-all | bytes 24576 | tf_op jit(solution)/shard_map/all_to_all | solution.py:23
  267.3 11.7 %all_to_all.199 = f32[32,1,192]{2,1,0:T(1,128)S(1)} all-to-all(f32[32,1,192]{2,1,0:T(1,128)S(1)} %reshape.475), channel_id=1, replica_groups=mesh['sub_0'=8,'sub_1'=2,'blk_0'=4,'blk_1'=8] {'blk_0','blk_1'}, dimensions={0} | all-to-all | bytes 49152 | tf_op jit(solution)/shard_map/all_to_all | solution.py:23
  280.3 12.6 %all_to_all.200 = bf16[8,2,64,128]{3,2,1,0:T(8,128)(2,1)S(1)} all-to-all(bf16[8,2,64,128]{3,2,1,0:T(8,128)(2,1)S(1)} %broadcast_in_dim.76), channel_id=1, replica_groups=mesh['sub_0'=8,'sub_1'=2,'blk_0'=4,'blk_1'=8] {'blk_1'}, dimensions={0} | all-to-all | bytes 524288 | tf_op jit(solution)/shard_map/all_to_all | solution.py:23
  293.5 4.5 collective-permute-start.7
  302.4 8.8 %all_to_all.201 = f32[4,2,64,128]{3,2,1,0:T(8,128)S(1)} all-to-all(f32[4,2,64,128]{3,2,1,0:T(8,128)S(1)} %convolution_subtract_fusion.2), channel_id=1, replica_groups=mesh['sub_0'=8,'sub_1'=2,'blk_0'=4,'blk_1'=8] {'blk_0'}, dimensions={0} | all-to-all | bytes 524288 | tf_op jit(solution)/shard_map/all_to_all | solution.py:121
  311.3 12.7 %all_to_all.202 = bf16[8,2,64,128]{3,2,1,0:T(8,128)(2,1)S(1)} all-to-all(bf16[8,2,64,128]{3,2,1,0:T(8,128)(2,1)S(1)} %broadcast_in_dim.77), channel_id=1, replica_groups=mesh['sub_0'=8,'sub_1'=2,'blk_0'=4,'blk_1'=8] {'blk_1'}, dimensions={0} | all-to-all | bytes 524288 | tf_op jit(solution)/shard_map/all_to_all | solution.py:23
  325.0 7.9 %all_to_all.203 = f32[4,2,64,128]{3,2,1,0:T(8,128)S(1)} all-to-all(f32[4,2,64,128]{3,2,1,0:T(8,128)S(1)} %fusion.97), channel_id=1, replica_groups=mesh['sub_0'=8,'sub_1'=2,'blk_0'=4,'blk_1'=8] {'blk_0'}, dimensions={0} | all-to-all | bytes 524288 | tf_op jit(solution)/shard_map/all_to_all | solution.py:121
  333.4 14.8 %all_to_all.204 = f32[16,1,256]{2,1,0:T(1,128)S(1)} all-to-all(f32[16,1,256]{2,1,0:T(1,128)S(1)} %reshape.477), channel_id=1, replica_groups=mesh['sub_0'=8,'sub_1'=2,'blk_0'=4,'blk_1'=8] {'sub_0','sub_1'}, dimensions={0} | all-to-all | bytes 32768 | tf_op jit(solution)/shard_map/all_to_all | solution.py:23
  349.2 11.7 %all_to_all.205 = f32[32,1,256]{2,1,0:T(1,128)S(1)} all-to-all(f32[32,1,256]{2,1,0:T(1,128)S(1)} %reshape.479), channel_id=1, replica_groups=mesh['sub_0'=8,'sub_1'=2,'blk_0'=4,'blk_1'=8] {'blk_0','blk_1'}, dimensions={0} | all-to-all | bytes 65536 | tf_op jit(solution)/shard_map/all_to_all | solution.py:23
  362.3 12.6 %all_to_all.206 = bf16[8,2,64,128]{3,2,1,0:T(8,128)(2,1)S(1)} all-to-all(bf16[8,2,64,128]{3,2,1,0:T(8,128)(2,1)S(1)} %broadcast_in_dim.80), channel_id=1, replica_groups=mesh['sub_0'=8,'sub_1'=2,'blk_0'=4,'blk_1'=8] {'blk_1'}, dimensions={0} | all-to-all | bytes 524288 | tf_op jit(solution)/shard_map/all_to_all | solution.py:23
  375.5 4.5 collective-permute-start.9
  384.4 8.8 %all_to_all.207 = f32[4,2,64,128]{3,2,1,0:T(8,128)S(1)} all-to-all(f32[4,2,64,128]{3,2,1,0:T(8,128)S(1)} %convolution_subtract_fusion.1), channel_id=1, replica_groups=mesh['sub_0'=8,'sub_1'=2,'blk_0'=4,'blk_1'=8] {'blk_0'}, dimensions={0} | all-to-all | bytes 524288 | tf_op jit(solution)/shard_map/all_to_all | solution.py:121
  393.2 12.7 %all_to_all.208 = bf16[8,2,64,128]{3,2,1,0:T(8,128)(2,1)S(1)} all-to-all(bf16[8,2,64,128]{3,2,1,0:T(8,128)(2,1)S(1)} %broadcast_in_dim.81), channel_id=1, replica_groups=mesh['sub_0'=8,'sub_1'=2,'blk_0'=4,'blk_1'=8] {'blk_1'}, dimensions={0} | all-to-all | bytes 524288 | tf_op jit(solution)/shard_map/all_to_all | solution.py:23
  407.1 7.9 %all_to_all.209 = f32[4,2,64,128]{3,2,1,0:T(8,128)S(1)} all-to-all(f32[4,2,64,128]{3,2,1,0:T(8,128)S(1)} %fusion.98), channel_id=1, replica_groups=mesh['sub_0'=8,'sub_1'=2,'blk_0'=4,'blk_1'=8] {'blk_0'}, dimensions={0} | all-to-all | bytes 524288 | tf_op jit(solution)/shard_map/all_to_all | solution.py:121
  415.6 14.8 %all_to_all.210 = f32[16,1,320]{2,1,0:T(1,128)S(1)} all-to-all(f32[16,1,320]{2,1,0:T(1,128)S(1)} %reshape.481), channel_id=1, replica_groups=mesh['sub_0'=8,'sub_1'=2,'blk_0'=4,'blk_1'=8] {'sub_0','sub_1'}, dimensions={0} | all-to-all | bytes 40960 | tf_op jit(solution)/shard_map/all_to_all | solution.py:23
  431.4 12.0 %all_to_all.211 = f32[32,1,320]{2,1,0:T(1,128)S(1)} all-to-all(f32[32,1,320]{2,1,0:T(1,128)S(1)} %reshape.483), channel_id=1, replica_groups=mesh['sub_0'=8,'sub_1'=2,'blk_0'=4,'blk_1'=8] {'blk_0','blk_1'}, dimensions={0} | all-to-all | bytes 81920 | tf_op jit(solution)/shard_map/all_to_all | solution.py:23
  446.1 12.6 %all_to_all.212 = bf16[8,2,64,128]{3,2,1,0:T(8,128)(2,1)S(1)} all-to-all(bf16[8,2,64,128]{3,2,1,0:T(8,128)(2,1)S(1)} %broadcast_in_dim.84), channel_id=1, replica_groups=mesh['sub_0'=8,'sub_1'=2,'blk_0'=4,'blk_1'=8] {'blk_1'}, dimensions={0} | all-to-all | bytes 524288 | tf_op jit(solution)/shard_map/all_to_all | solution.py:23
  459.3 4.5 collective-permute-start.11
  468.1 8.8 %all_to_all.213 = f32[4,2,64,128]{3,2,1,0:T(8,128)S(1)} all-to-all(f32[4,2,64,128]{3,2,1,0:T(8,128)S(1)} %convolution_subtract_fusion), channel_id=1, replica_groups=mesh['sub_0'=8,'sub_1'=2,'blk_0'=4,'blk_1'=8] {'blk_0'}, dimensions={0} | all-to-all | bytes 524288 | tf_op jit(solution)/shard_map/all_to_all | solution.py:121
  477.0 12.7 %all_to_all.214 = bf16[8,2,64,128]{3,2,1,0:T(8,128)(2,1)S(1)} all-to-all(bf16[8,2,64,128]{3,2,1,0:T(8,128)(2,1)S(1)} %broadcast_in_dim.85), channel_id=1, replica_groups=mesh['sub_0'=8,'sub_1'=2,'blk_0'=4,'blk_1'=8] {'blk_1'}, dimensions={0} | all-to-all | bytes 524288 | tf_op jit(solution)/shard_map/all_to_all | solution.py:23
  491.0 7.9 %all_to_all.215 = f32[4,2,64,128]{3,2,1,0:T(8,128)S(1)} all-to-all(f32[4,2,64,128]{3,2,1,0:T(8,128)S(1)} %fusion.99), channel_id=1, replica_groups=mesh['sub_0'=8,'sub_1'=2,'blk_0'=4,'blk_1'=8] {'blk_0'}, dimensions={0} | all-to-all | bytes 524288 | tf_op jit(solution)/shard_map/all_to_all | solution.py:121
  499.5 14.9 %all_to_all.216 = f32[16,1,384]{2,1,0:T(1,128)S(1)} all-to-all(f32[16,1,384]{2,1,0:T(1,128)S(1)} %reshape.485), channel_id=1, replica_groups=mesh['sub_0'=8,'sub_1'=2,'blk_0'=4,'blk_1'=8] {'sub_0','sub_1'}, dimensions={0} | all-to-all | bytes 49152 | tf_op jit(solution)/shard_map/all_to_all | solution.py:23
  515.5 11.8 %all_to_all.217 = f32[32,1,384]{2,1,0:T(1,128)S(1)} all-to-all(f32[32,1,384]{2,1,0:T(1,128)S(1)} %reshape.487), channel_id=1, replica_groups=mesh['sub_0'=8,'sub_1'=2,'blk_0'=4,'blk_1'=8] {'blk_0','blk_1'}, dimensions={0} | all-to-all | bytes 98304 | tf_op jit(solution)/shard_map/all_to_all | solution.py:23
  (371 shorter events, 60.6 us)
Async XLA Ops:
  1.9 17.1 %all-to-all-start.1 = ((bf16[8,2,64,128]{3,2,1,0:T(8,128)(2,1)}), bf16[8,2,64,128]{3,2,1,0:T(8,128)(2,1)S(1)}, u32[]{:S(2)}, u32[]{:S(2)}) async-start(bf16[8,2,64,128]{3,2,1,0:T(8,128)(2,1)} %broadcast_in_dim.62), calls=%async_computation.1 | async-start | bytes 524288 | tf_op jit(solution)/shard_map/all_to_all | solution.py:23
  18.9 28.9 %all-to-all-start = ((bf16[4,128,2048]{2,1,0:T(8,128)(2,1)}), bf16[4,128,2048]{2,1,0:T(8,128)(2,1)S(1)}, u32[]{:S(2)}, u32[]{:S(2)}) async-start(bf16[4,128,2048]{2,1,0:T(8,128)(2,1)} %maximum_maximum_fusion), calls=%async_computation | async-start | bytes 4194304 | tf_op jit(solution)/shard_map/all_to_all | solution.py:60
  24.4 186.8 %copy-start.38 = (s32[256]{0:T(256)}, s32[256]{0:T(256)S(1)}, u32[]{:S(2)}) copy-start(s32[256]{0:T(256)S(1)} %pad_add_fusion) | copy-start | bytes 3076
  24.4 268.7 %copy-start.24 = (s32[512]{0:T(512)}, s32[512]{0:T(512)S(1)}, u32[]{:S(2)}) copy-start(s32[512]{0:T(512)S(1)} %iota_add_fusion.1) | copy-start | bytes 6148
  24.8 23.0 %copy-start.5 = (f32[2]{0:T(128)S(1)}, f32[2]{0:T(128)}, u32[]{:S(2)}) copy-start(f32[2]{0:T(128)} %constant.58.clone) | copy-start | bytes 28
  24.9 8.8 %collective-permute-start.1 = (bf16[2,128,128]{1,2,0:T(8,128)(2,1)S(1)}, bf16[2,128,128]{1,2,0:T(8,128)(2,1)S(1)}, u32[]{:S(2)}, u32[]{:S(2)}) collective-permute-start(bf16[2,128,128]{1,2,0:T(8,128)(2,1)S(1)} %get-tuple-element.102), channel_id=1, source_target_pairs={{32,0},{64,32},{96,64},{128,96},{160,128},{192,160},{224,192},{256... | collective-permute-start | bytes 196616 | tf_op jit(solution)/shard_map/ppermute | solution.py:18
  29.4 5.2 collective-permute-start
  57.2 13.2 %all-to-all-start.3 = ((bf16[8,2,64,128]{3,2,1,0:T(8,128)(2,1)}), bf16[8,2,64,128]{3,2,1,0:T(8,128)(2,1)S(1)}, u32[]{:S(2)}, u32[]{:S(2)}) async-start(bf16[8,2,64,128]{3,2,1,0:T(8,128)(2,1)} %broadcast_in_dim.65), calls=%async_computation.3 | async-start | bytes 524288 | tf_op jit(solution)/shard_map/all_to_all | solution.py:23
  72.2 8.9 %all-to-all-start.4 = ((f32[4,2,64,128]{3,2,1,0:T(8,128)}), f32[4,2,64,128]{3,2,1,0:T(8,128)S(1)}, u32[]{:S(2)}, u32[]{:S(2)}) async-start(f32[4,2,64,128]{3,2,1,0:T(8,128)} %fusion.94), calls=%async_computation.4 | async-start | bytes 524288 | tf_op jit(solution)/shard_map/all_to_all | solution.py:121
  129.9 7.5 %collective-permute-start.3 = (bf16[2,128,128]{1,2,0:T(8,128)(2,1)S(1)}, bf16[2,128,128]{1,2,0:T(8,128)(2,1)S(1)}, u32[]{:S(2)}, u32[]{:S(2)}) collective-permute-start(bf16[2,128,128]{1,2,0:T(8,128)(2,1)S(1)} %get-tuple-element.98), channel_id=1, source_target_pairs={{32,0},{64,32},{96,64},{128,96},{160,128},{192,160},{224,192},{256... | collective-permute-start | bytes 196616 | tf_op jit(solution)/shard_map/ppermute | solution.py:18
  135.0 3.4 collective-permute-start.2
  211.6 7.7 %collective-permute-start.5 = (bf16[2,128,128]{1,2,0:T(8,128)(2,1)S(1)}, bf16[2,128,128]{1,2,0:T(8,128)(2,1)S(1)}, u32[]{:S(2)}, u32[]{:S(2)}) collective-permute-start(bf16[2,128,128]{1,2,0:T(8,128)(2,1)S(1)} %get-tuple-element.96), channel_id=1, source_target_pairs={{32,0},{64,32},{96,64},{128,96},{160,128},{192,160},{224,192},{256... | collective-permute-start | bytes 196616 | tf_op jit(solution)/shard_map/ppermute | solution.py:18
  216.7 3.4 collective-permute-start.4
  251.8 41.3 %copy-start.39 = (s32[256]{0:T(256)S(1)}, s32[256]{0:T(256)}, u32[]{:S(2)}) copy-start(s32[256]{0:T(256)} %copy-done.38) | copy-start | bytes 3076
  293.5 6.8 %collective-permute-start.7 = (bf16[2,128,128]{1,2,0:T(8,128)(2,1)S(1)}, bf16[2,128,128]{1,2,0:T(8,128)(2,1)S(1)}, u32[]{:S(2)}, u32[]{:S(2)}) collective-permute-start(bf16[2,128,128]{1,2,0:T(8,128)(2,1)S(1)} %get-tuple-element.94), channel_id=1, source_target_pairs={{32,0},{64,32},{96,64},{128,96},{160,128},{192,160},{224,192},{256... | collective-permute-start | bytes 196616 | tf_op jit(solution)/shard_map/ppermute | solution.py:18
  298.1 3.4 collective-permute-start.6
  332.9 42.2 %copy-start.25 = (s32[512]{0:T(512)S(1)}, s32[512]{0:T(512)}, u32[]{:S(2)}) copy-start(s32[512]{0:T(512)} %copy-done.24) | copy-start | bytes 6148
  332.9 42.2 %copy-start.40 = (s32[256]{0:T(256)S(1)}, s32[256]{0:T(256)}, u32[]{:S(2)}) copy-start(s32[256]{0:T(256)} %copy-done.38) | copy-start | bytes 3076
  375.5 6.8 %collective-permute-start.9 = (bf16[2,128,128]{1,2,0:T(8,128)(2,1)S(1)}, bf16[2,128,128]{1,2,0:T(8,128)(2,1)S(1)}, u32[]{:S(2)}, u32[]{:S(2)}) collective-permute-start(bf16[2,128,128]{1,2,0:T(8,128)(2,1)S(1)} %get-tuple-element.92), channel_id=1, source_target_pairs={{32,0},{64,32},{96,64},{128,96},{160,128},{192,160},{224,192},{256... | collective-permute-start | bytes 196616 | tf_op jit(solution)/shard_map/ppermute | solution.py:18
  380.0 3.4 collective-permute-start.8
  406.3 38.1 %copy-start.7 = (f32[2,64]{1,0:T(2,128)S(1)}, f32[2,64]{1,0:T(2,128)}, u32[]{:S(2)}) copy-start(f32[2,64]{1,0:T(2,128)} %copy-done.6) | copy-start | bytes 1540
  406.3 38.1 %copy-start.10 = (f32[64]{0:T(128)S(1)}, f32[64]{0:T(128)}, u32[]{:S(2)}) copy-start(f32[64]{0:T(128)} %copy-done.9) | copy-start | bytes 772
  406.3 38.1 %copy-start.13 = (f32[64]{0:T(128)S(1)}, f32[64]{0:T(128)}, u32[]{:S(2)}) copy-start(f32[64]{0:T(128)} %copy-done.12) | copy-start | bytes 772
  406.3 38.1 %copy-start.28 = (f32[64]{0:T(128)S(1)}, f32[64]{0:T(128)}, u32[]{:S(2)}) copy-start(f32[64]{0:T(128)} %copy-done.27) | copy-start | bytes 772
  406.3 38.1 %copy-start.31 = (f32[64]{0:T(128)S(1)}, f32[64]{0:T(128)}, u32[]{:S(2)}) copy-start(f32[64]{0:T(128)} %copy-done.30) | copy-start | bytes 772
  415.0 43.9 %copy-start.26 = (s32[512]{0:T(512)S(1)}, s32[512]{0:T(512)}, u32[]{:S(2)}) copy-start(s32[512]{0:T(512)} %copy-done.24) | copy-start | bytes 6148
  415.0 43.9 %copy-start.41 = (s32[256]{0:T(256)S(1)}, s32[256]{0:T(256)}, u32[]{:S(2)}) copy-start(s32[256]{0:T(256)} %copy-done.38) | copy-start | bytes 3076
  445.0 21.1 %copy-start.36 = (f32[64]{0:T(128)}, f32[64]{0:T(128)S(1)}, u32[]{:S(2)}) copy-start(f32[64]{0:T(128)S(1)} %get-tuple-element.42) | copy-start | bytes 772
  459.3 6.8 %collective-permute-start.11 = (bf16[2,128,128]{1,2,0:T(8,128)(2,1)S(1)}, bf16[2,128,128]{1,2,0:T(8,128)(2,1)S(1)}, u32[]{:S(2)}, u32[]{:S(2)}) collective-permute-start(bf16[2,128,128]{1,2,0:T(8,128)(2,1)S(1)} %get-tuple-element.90), channel_id=1, source_target_pairs={{32,0},{64,32},{96,64},{128,96},{160,128},{192,160},{224,192},{256... | collective-permute-start | bytes 196616 | tf_op jit(solution)/shard_map/ppermute | solution.py:18
  463.9 3.4 collective-permute-start.10
  490.1 38.1 %copy-start.8 = (f32[2,64]{1,0:T(2,128)S(1)}, f32[2,64]{1,0:T(2,128)}, u32[]{:S(2)}) copy-start(f32[2,64]{1,0:T(2,128)} %copy-done.6) | copy-start | bytes 1540
  490.1 38.1 %copy-start.11 = (f32[64]{0:T(128)S(1)}, f32[64]{0:T(128)}, u32[]{:S(2)}) copy-start(f32[64]{0:T(128)} %copy-done.9) | copy-start | bytes 772
  490.1 38.1 %copy-start.15 = (f32[64]{0:T(128)S(1)}, f32[64]{0:T(128)}, u32[]{:S(2)}) copy-start(f32[64]{0:T(128)} %get-tuple-element.33) | copy-start | bytes 772
  490.1 38.1 %copy-start.16 = (f32[64]{0:T(128)S(1)}, f32[64]{0:T(128)}, u32[]{:S(2)}) copy-start(f32[64]{0:T(128)} %get-tuple-element.34) | copy-start | bytes 772
  490.1 38.1 %copy-start.17 = (f32[64]{0:T(128)S(1)}, f32[64]{0:T(128)}, u32[]{:S(2)}) copy-start(f32[64]{0:T(128)} %get-tuple-element.35) | copy-start | bytes 772
  490.1 38.1 %copy-start.18 = (f32[64]{0:T(128)S(1)}, f32[64]{0:T(128)}, u32[]{:S(2)}) copy-start(f32[64]{0:T(128)} %get-tuple-element.36) | copy-start | bytes 772
  490.1 38.1 %copy-start.19 = (f32[64]{0:T(128)S(1)}, f32[64]{0:T(128)}, u32[]{:S(2)}) copy-start(f32[64]{0:T(128)} %get-tuple-element.37) | copy-start | bytes 772
  490.1 38.1 %copy-start.20 = (f32[64]{0:T(128)S(1)}, f32[64]{0:T(128)}, u32[]{:S(2)}) copy-start(f32[64]{0:T(128)} %get-tuple-element.38) | copy-start | bytes 772
  490.1 38.1 %copy-start.21 = (f32[64]{0:T(128)S(1)}, f32[64]{0:T(128)}, u32[]{:S(2)}) copy-start(f32[64]{0:T(128)} %get-tuple-element.39) | copy-start | bytes 772
  490.2 38.1 %copy-start.22 = (f32[64]{0:T(128)S(1)}, f32[64]{0:T(128)}, u32[]{:S(2)}) copy-start(f32[64]{0:T(128)} %get-tuple-element.40) | copy-start | bytes 772
  490.2 38.1 %copy-start.23 = (f32[64]{0:T(128)S(1)}, f32[64]{0:T(128)}, u32[]{:S(2)}) copy-start(f32[64]{0:T(128)} %get-tuple-element.41) | copy-start | bytes 772
  490.2 38.1 %copy-start.29 = (f32[64]{0:T(128)S(1)}, f32[64]{0:T(128)}, u32[]{:S(2)}) copy-start(f32[64]{0:T(128)} %copy-done.27) | copy-start | bytes 772
  490.2 38.1 %copy-start.32 = (f32[64]{0:T(128)S(1)}, f32[64]{0:T(128)}, u32[]{:S(2)}) copy-start(f32[64]{0:T(128)} %copy-done.30) | copy-start | bytes 772
  490.2 38.1 %copy-start.37 = (f32[64]{0:T(128)S(1)}, f32[64]{0:T(128)}, u32[]{:S(2)}) copy-start(f32[64]{0:T(128)} %copy-done.36) | copy-start | bytes 772
  490.2 38.2 %copy-start.14 = (f32[64]{0:T(128)S(1)}, f32[64]{0:T(128)}, u32[]{:S(2)}) copy-start(f32[64]{0:T(128)} %copy-done.12) | copy-start | bytes 772
  490.2 38.2 %copy-start.33 = (f32[64]{0:T(128)S(1)}, f32[64]{0:T(128)}, u32[]{:S(2)}) copy-start(f32[64]{0:T(128)} %get-tuple-element.30) | copy-start | bytes 772
  490.2 38.2 %copy-start.34 = (f32[64]{0:T(128)S(1)}, f32[64]{0:T(128)}, u32[]{:S(2)}) copy-start(f32[64]{0:T(128)} %get-tuple-element.31) | copy-start | bytes 772
  490.2 38.2 %copy-start.35 = (f32[64]{0:T(128)S(1)}, f32[64]{0:T(128)}, u32[]{:S(2)}) copy-start(f32[64]{0:T(128)} %get-tuple-element.32) | copy-start | bytes 772
  (10 other events, 78.3 us)

commit v2 on v1

--- a/solution.py
+++ b/solution.py
@@ -12,10 +12,16 @@
 EPSILON = 1e-06
 
 
-def passed_along(block, axis, distance):
-    devices = range(lax.axis_size(axis))
-    route = [(i - distance, i) for i in devices if i - distance in devices]
+def swapped_in_pairs(block, axis, first):
+    devices = lax.axis_size(axis)
+    route = []
+    for low in range(first, devices - 1, 2):
+        route += [(low, low + 1), (low + 1, low)]
     return lax.ppermute(block, axis, route)
+
+
+def on_even_subdomain():
+    return lax.axis_index(SUB) % 2 == 0
 
 
 def copy_for_each(value, axis):
@@ -82,16 +88,21 @@
     inverse_here = jnp.sum(
         jnp.where(perm_here[None, :] == wanted[:, None], spots[None, :], 0), axis=1
     )
-    dofs = jnp.concatenate([2 * window(perm_above) + 1, 2 * inverse_here])
+    upward = 2 * window(perm_above) + 1
+    downward = 2 * inverse_here
+    even = on_even_subdomain()
+    dofs = jnp.concatenate(
+        [jnp.where(even, upward, downward), jnp.where(even, downward, upward)]
+    )
     width = 2 * half // lines
     columns = lax.axis_index("blk_0") * width + jnp.arange(width, dtype=jnp.int32)
     return (dofs[:, None] == columns[None, :]).astype(jnp.bfloat16)
 
 
-def gathered_columns(vector):
-    blocks = copy_for_each(vector, "blk_1")
-    return jnp.moveaxis(blocks, 0, 1).reshape(
-        vector.shape[0], blocks.shape[0] * vector.shape[1], vector.shape[2]
+def side_by_side(blocks):
+    count, rows, width = blocks.shape
+    return jnp.moveaxis(blocks.reshape(count, 2, rows // 2, width), 0, 1).reshape(
+        2, count * rows // 2, width
     )
 
 
@@ -100,7 +111,7 @@
     turned = jnp.concatenate([-columns[..., width:], columns[..., :width]], axis=-1)
     stacked = jnp.stack([columns, turned]).reshape(tile.shape[1], 2 * width)
     products = jnp.dot(tile, stacked, preferred_element_type=jnp.float32)
-    return products.reshape(lax.axis_size("blk_0"), 2, -1, 2 * width)
+    return products.reshape(lax.axis_size("blk_0"), -1, 2 * width)
 
 
 def coupling_partials(selector, columns):
@@ -109,24 +120,62 @@
         "sk,tkn->tsn", selector, columns, preferred_element_type=jnp.float32
     ).astype(jnp.bfloat16)
     middle = chosen.shape[1] // 2
-    lower_face = passed_along(chosen[:, :middle], SUB, 1)
-    upper_face = passed_along(chosen[:, middle:], SUB, -1)
+    inner_face = swapped_in_pairs(chosen[:, :middle], SUB, 0)
+    outer_face = swapped_in_pairs(chosen[:, middle:], SUB, 1)
+    even = on_even_subdomain()
+    lower_face = jnp.where(even, outer_face, inner_face)
+    upper_face = jnp.where(even, inner_face, outer_face)
     joined = jnp.stack([lower_face, upper_face], axis=2)
     joined = joined.reshape(2, lines, 2 * middle // lines, chosen.shape[-1])
     signs = jnp.array([1.0, -1.0], jnp.float32).reshape(1, 2, 1, 1)
-    return jnp.moveaxis(joined, 1, 0).astype(jnp.float32) * signs
+    signed = jnp.moveaxis(joined, 1, 0).astype(jnp.float32) * signs
+    return signed.reshape(lines, -1, signed.shape[-1])
 
 
 def reduced_rows(partials):
     return jnp.sum(lax.all_to_all(partials, "blk_0", 0, 0, tiled=True), axis=0)
 
 
-def preconditioned(tile, selector, vector):
-    columns = gathered_columns(vector.astype(jnp.bfloat16))
+def padded_rows(value, multiple):
+    missing = -value.shape[0] % multiple
+    return jnp.pad(value, ((0, missing), (0, 0)))
+
+
+def in_three_pieces(value):
+    high = lax.reduce_precision(value, 8, 7)
+    middle = lax.reduce_precision(value - high, 8, 7)
+    low = lax.reduce_precision(value - high - middle, 8, 7)
+    return jnp.concatenate([high, middle, low]).astype(jnp.bfloat16)
+
+
+def preconditioned(tile, selector, vector, dots=None):
+    shape = vector.shape
+    width = shape[-1]
+    columns = side_by_side(
+        copy_for_each(vector.astype(jnp.bfloat16).reshape(-1, width), "blk_1")
+    )
+    if dots is not None:
+        dots = summed_over(dots, SUB)
     first = partial_products(tile, columns) - 0.5 * coupling_partials(selector, columns)
-    middle = reduced_rows(first)
-    middle_columns = gathered_columns(middle.astype(jnp.bfloat16))
-    return reduced_rows(partial_products(tile, middle_columns))
+    middle = reduced_rows(first).astype(jnp.bfloat16)
+    rows = middle.shape[0]
+    if dots is None:
+        middle_columns = side_by_side(copy_for_each(middle, "blk_1"))
+        return reduced_rows(partial_products(tile, middle_columns)).reshape(shape)
+    count, narrow = dots.shape
+    packed = padded_rows(dots, 2).reshape(-1, width)
+    lines = packed.shape[0]
+    pieces = padded_rows(in_three_pieces(packed), 16)
+    blocks = copy_for_each(jnp.concatenate([middle, pieces]), "blk_1")
+    carried = blocks[:, rows : rows + 3 * lines].astype(jnp.float32)
+    carried = jnp.sum(carried.reshape(-1, 3, lines, width), axis=(0, 1))
+    second = partial_products(tile, side_by_side(blocks[:, :rows]))
+    carried = jnp.broadcast_to(
+        padded_rows(carried, 8)[None], (second.shape[0], lines + -lines % 8, width)
+    )
+    total = reduced_rows(jnp.concatenate([second, carried], axis=1))
+    dots = total[rows : rows + lines].reshape(-1, narrow)[:count]
+    return total[:rows].reshape(shape), dots
 
 
 def inner_local(first, second):
@@ -179,22 +228,56 @@
     right_local = inward(right_side)
     start_local = inward(start)
     selector = selectors(matching, right_local.shape[1])
-    residual = right_local - preconditioned(tile, selector, start_local)
-    beta = jnp.sqrt(summed_everywhere(inner_local(residual, residual)[None])[0] + EPSILON)
+    start_image = preconditioned(tile, selector, start_local)
+    residual = right_local - start_image
+    local_dots = jnp.stack(
+        [
+            inner_local(residual, residual),
+            inner_local(start_local, start_image),
+            inner_local(start_local, start_local),
+        ]
+    )
+    applied, sums = preconditioned(tile, selector, residual, local_dots)
+    beta = jnp.sqrt(sums[0] + EPSILON)
+    shift = sums[1] / (sums[2] + EPSILON)
     basis = [residual / spread(beta)]
+    images = [applied / spread(beta)]
+    gram = (sums[0] / (beta * beta))[None, None]
     hessen = []
     for column in range(BASIS):
-        image = preconditioned(tile, selector, basis[column])
-        local_dots = [inner_local(vector, image) for vector in basis]
-        summed = summed_everywhere(jnp.stack(local_dots + [inner_local(image, image)]))
-        squares = summed[column + 1] - jnp.sum(summed[: column + 1] * summed[: column + 1], axis=0)
-        height = jnp.sqrt(jnp.maximum(squares, 0.0) + EPSILON)
+        ahead = images[column] - spread(shift) * basis[column]
+        local_dots = [inner_local(vector, ahead) for vector in basis]
+        local_dots = jnp.stack(local_dots + [inner_local(ahead, ahead)])
         if column + 1 < BASIS:
+            applied, sums = preconditioned(tile, selector, ahead, local_dots)
+        else:
+            sums = summed_everywhere(local_dots)
+        dots = sums[: column + 1]
+        coefficients = dots + shift * gram[:, column]
+        removed = jnp.concatenate([coefficients[:column], dots[column:] + shift * (gram[column:, column] - 1.0)])
+        overlaps = jnp.sum(gram * removed[None], axis=1)
+        squares = jnp.maximum(
+            sums[column + 1] - jnp.sum(removed * (2.0 * dots - overlaps), axis=0), 0.0
+        )
+        height = jnp.sqrt(squares + EPSILON)
+        if column + 1 < BASIS:
+            following = ahead
             for earlier in range(column + 1):
-                image = image - spread(summed[earlier]) * basis[earlier]
-            basis.append(image / spread(height))
+                following = following - spread(removed[earlier]) * basis[earlier]
+                applied = applied - spread(removed[earlier]) * images[earlier]
+            basis.append(following / spread(height))
+            images.append(applied / spread(height))
+            side = (dots - overlaps) / height
+            corner = squares / (height * height)
+            gram = jnp.concatenate(
+                [
+                    jnp.concatenate([gram, side[:, None]], axis=1),
+                    jnp.concatenate([side, corner[None]])[None],
+                ]
+            )
+            shift = coefficients[column]
         filler = [jnp.zeros_like(height)] * (BASIS - 1 - column)
-        hessen.append([summed[earlier] for earlier in range(column + 1)] + [height] + filler)
+        hessen.append([coefficients[earlier] for earlier in range(column + 1)] + [height] + filler)
     weights = least_squares(hessen, beta)
     solution = start_local
     for column in range(BASIS):

time: 532 us -> 505 us (0.949)
  blocking collectives: 384 us -> 130 us
  waiting for transfers between devices: 37.4 us -> 186 us
  starting transfers between devices: 62.9 us -> 119 us
  local copies, waits for them, and re-layouts: 12.4 us -> 24.9 us
    all_to_all x22 -> x7, blocking collectives: 292 us -> 106 us  [copy_for_each(): lax.all_to_all(jnp.broadcast_to(value[None], (peers, *value.shape)), axis...]
    all_to_all x2 -> x12, waiting for transfers between devices: 12.8 us -> 113 us  [copy_for_each(): lax.all_to_all(jnp.broadcast_to(value[None], (peers, *value.shape)), axis...]
    all_to_all x11 -> x3, blocking collectives: 91.8 us -> 23.9 us  [reduced_rows(): return jnp.sum(lax.all_to_all(partials, 'blk_0', 0, 0, tiled=True), axis=0)]
    all_to_all x1 -> x9, waiting for transfers between devices: 5.47 us -> 54.7 us  [reduced_rows(): return jnp.sum(lax.all_to_all(partials, 'blk_0', 0, 0, tiled=True), axis=0)]
    all_to_all x2 -> x12, starting transfers between devices: 11.5 us -> 50.4 us  [copy_for_each(): lax.all_to_all(jnp.broadcast_to(value[None], (peers, *value.shape)), axis...]
    all_to_all x1 -> x9, starting transfers between devices: 3.4 us -> 30.9 us  [reduced_rows(): return jnp.sum(lax.all_to_all(partials, 'blk_0', 0, 0, tiled=True), axis=0)]
    ppermute x12, starting transfers between devices: 42.9 us -> 32.4 us  [swapped_in_pairs(): return lax.ppermute(block, axis, route)]
    broadcast_in_dim x24 -> x19, local copies, waits for them, and re-layouts: 2.09 us -> 7.65 us  [copy_for_each(): jnp.broadcast_to(value[None], (peers, *value.shape))]
  transfers between devices with their start and end apart: 16 -> 34, of which waited for: 10 -> 32; matrix products, arithmetic and copies ran while one was open for 2% -> 3% of each run, Pallas kernels for 0% -> 0%
where the time goes in v2:
time: 505 us; the launch traced here: 502 us
  waiting for transfers between devices  186 us (37%)
  blocking collectives  130 us (26%)
  starting transfers between devices  119 us (24%)
  local copies, waits for them, and re-layouts  24.9 us (5%)
  other arithmetic  23.7 us (5%)
  matrix products  14.9 us (3%)
    all_to_all x12, waiting for transfers between devices, copy_for_each(): lax.all_to_all(jnp.broadcast_to(value[None], (peers, *value.shape)), axis...  113 us
    all_to_all x7, blocking collectives, copy_for_each(): lax.all_to_all(jnp.broadcast_to(value[None], (peers, *value.shape)), axis...  106 us
    all_to_all x9, waiting for transfers between devices, reduced_rows(): return jnp.sum(lax.all_to_all(partials, 'blk_0', 0, 0, tiled=True), axis=0)  54.7 us
    all_to_all x12, starting transfers between devices, copy_for_each(): lax.all_to_all(jnp.broadcast_to(value[None], (peers, *value.shape)), axis...  50.4 us
    ppermute x12, starting transfers between devices, swapped_in_pairs(): return lax.ppermute(block, axis, route)  32.4 us
    all_to_all x9, starting transfers between devices, reduced_rows(): return jnp.sum(lax.all_to_all(partials, 'blk_0', 0, 0, tiled=True), axis=0)  30.9 us
    all_to_all x3, blocking collectives, reduced_rows(): return jnp.sum(lax.all_to_all(partials, 'blk_0', 0, 0, tiled=True), axis=0)  23.9 us
    all_to_all x1, waiting for transfers between devices, tile_of_operators(): blocks = lax.all_to_all(strips, 'blk_0', 0, 0, tiled=True)  13.4 us
  transfers between devices with their start and end apart: 34, of which 32 were waited for; matrix products, arithmetic and copies ran while one was open for 3% of the time, Pallas kernels for 0%

profile of v2, /device:TPU:1, one launch (start us, length us, event | category | flops | bytes accessed | tf_op | source)
XLA Modules:
  0.0 501.7 jit_solution(1163532272674784991)
XLA Ops:
  1.9 7.6 %all-to-all-start.1 = ((bf16[8,128,128]{2,1,0:T(8,128)(2,1)}), bf16[8,128,128]{2,1,0:T(8,128)(2,1)S(1)}, u32[]{:S(2)}, u32[]{:S(2)}) async-start(bf16[8,128,128]{2,1,0:T(8,128)(2,1)} %broadcast_in_dim.74), calls=%async_computation.1 | async-start | bytes 524288 | tf_op jit(solution)/shard_map/all_to_all | solution.py:29
  18.9 5.1 %all-to-all-start = ((bf16[4,128,2048]{2,1,0:T(8,128)(2,1)}), bf16[4,128,2048]{2,1,0:T(8,128)(2,1)S(1)}, u32[]{:S(2)}, u32[]{:S(2)}) async-start(bf16[4,128,2048]{2,1,0:T(8,128)(2,1)} %maximum_maximum_fusion), calls=%async_computation | async-start | bytes 4194304 | tf_op jit(solution)/shard_map/all_to_all | solution.py:66
  24.4 6.5 %collective-permute-start = (bf16[2,128,128]{1,2,0:T(8,128)(2,1)S(1)}, bf16[2,128,128]{1,2,0:T(8,128)(2,1)S(1)}, u32[]{:S(2)}, u32[]{:S(2)}) collective-permute-start(bf16[2,128,128]{1,2,0:T(8,128)(2,1)S(1)} %get-tuple-element.124), channel_id=1, source_target_pairs={{32,64},{64,32},{96,128},{128,96},{160,192},{192,160},{224,256},{2... | collective-permute-start | bytes 196616 | tf_op jit(solution)/shard_map/ppermute | solution.py:20
  34.4 13.4 %all-to-all-done = bf16[4,128,2048]{2,1,0:T(8,128)(2,1)S(1)} async-done(((bf16[4,128,2048]{2,1,0:T(8,128)(2,1)}), bf16[4,128,2048]{2,1,0:T(8,128)(2,1)S(1)}, u32[]{:S(2)}, u32[]{:S(2)}) %all-to-all-start) | async-done | bytes 2097184 | tf_op jit(solution)/shard_map/all_to_all | solution.py:66
  48.5 7.9 %all_to_all.160 = f32[4,128,128]{2,1,0:T(8,128)S(1)} all-to-all(f32[4,128,128]{2,1,0:T(8,128)S(1)} %convolution_subtract_fusion.5), channel_id=1, replica_groups=mesh['sub_0'=8,'sub_1'=2,'blk_0'=4,'blk_1'=8] {'blk_0'}, dimensions={0} | all-to-all | bytes 524288 | tf_op jit(solution)/shard_map/all_to_all | solution.py:136
  57.2 4.6 all-to-all-start.3
  62.6 8.6 %all-to-all-done.3 = bf16[8,128,128]{2,1,0:T(8,128)(2,1)S(1)} async-done(((bf16[8,128,128]{2,1,0:T(8,128)(2,1)}), bf16[8,128,128]{2,1,0:T(8,128)(2,1)S(1)}, u32[]{:S(2)}, u32[]{:S(2)}) %all-to-all-start.3) | async-done | bytes 262176 | tf_op jit(solution)/shard_map/all_to_all | solution.py:29
  76.5 5.4 %all-to-all-done.4 = f32[4,128,128]{2,1,0:T(8,128)S(1)} async-done(((f32[4,128,128]{2,1,0:T(8,128)}), f32[4,128,128]{2,1,0:T(8,128)S(1)}, u32[]{:S(2)}, u32[]{:S(2)}) %all-to-all-start.4) | async-done | bytes 262176 | tf_op jit(solution)/shard_map/all_to_all | solution.py:136
  82.4 24.3 %all_to_all.161 = f32[16,1,192]{2,1,0:T(1,128)S(1)} all-to-all(f32[16,1,192]{2,1,0:T(1,128)S(1)} %reshape.910), channel_id=1, replica_groups=mesh['sub_0'=8,'sub_1'=2,'blk_0'=4,'blk_1'=8] {'sub_0','sub_1'}, dimensions={0} | all-to-all | bytes 24576 | tf_op jit(solution)/shard_map/all_to_all | solution.py:29
  107.4 3.4 all-to-all-start.5
  112.2 10.9 %all-to-all-done.5 = bf16[8,128,128]{2,1,0:T(8,128)(2,1)S(1)} async-done(((bf16[8,128,128]{2,1,0:T(8,128)(2,1)}), bf16[8,128,128]{2,1,0:T(8,128)(2,1)S(1)}, u32[]{:S(2)}, u32[]{:S(2)}) %all-to-all-start.5) | async-done | bytes 262176 | tf_op jit(solution)/shard_map/all_to_all | solution.py:29
  134.6 6.5 %all-to-all-done.6 = f32[4,128,128]{2,1,0:T(8,128)S(1)} async-done(((f32[4,128,128]{2,1,0:T(8,128)}), f32[4,128,128]{2,1,0:T(8,128)S(1)}, u32[]{:S(2)}, u32[]{:S(2)}) %all-to-all-start.6) | async-done | bytes 262176 | tf_op jit(solution)/shard_map/all_to_all | solution.py:136
  141.2 13.2 %all_to_all.162 = bf16[8,144,128]{2,1,0:T(8,128)(2,1)S(1)} all-to-all(bf16[8,144,128]{2,1,0:T(8,128)(2,1)S(1)} %broadcast_in_dim.80), channel_id=1, replica_groups=mesh['sub_0'=8,'sub_1'=2,'blk_0'=4,'blk_1'=8] {'blk_1'}, dimensions={0} | all-to-all | bytes 589824 | tf_op jit(solution)/shard_map/all_to_all | solution.py:29
  155.6 8.0 %all_to_all.163 = f32[4,136,128]{2,1,0:T(8,128)S(1)} all-to-all(f32[4,136,128]{2,1,0:T(8,128)S(1)} %pad_maximum_fusion.12), channel_id=1, replica_groups=mesh['sub_0'=8,'sub_1'=2,'blk_0'=4,'blk_1'=8] {'blk_0'}, dimensions={0} | all-to-all | bytes 557056 | tf_op jit(solution)/shard_map/all_to_all | solution.py:136
  164.2 14.0 %all_to_all.164 = f32[16,1,128]{2,1,0:T(1,128)S(1)} all-to-all(f32[16,1,128]{2,1,0:T(1,128)S(1)} %reshape.912), channel_id=1, replica_groups=mesh['sub_0'=8,'sub_1'=2,'blk_0'=4,'blk_1'=8] {'sub_0','sub_1'}, dimensions={0} | all-to-all | bytes 16384 | tf_op jit(solution)/shard_map/all_to_all | solution.py:29
  178.9 3.4 all-to-all-start.10
  183.1 10.2 %all-to-all-done.10 = bf16[8,128,128]{2,1,0:T(8,128)(2,1)S(1)} async-done(((bf16[8,128,128]{2,1,0:T(8,128)(2,1)}), bf16[8,128,128]{2,1,0:T(8,128)(2,1)S(1)}, u32[]{:S(2)}, u32[]{:S(2)}) %all-to-all-start.10) | async-done | bytes 262176 | tf_op jit(solution)/shard_map/all_to_all | solution.py:29
  193.9 3.8 collective-permute-start.4
  206.1 6.5 %all-to-all-done.11 = f32[4,128,128]{2,1,0:T(8,128)S(1)} async-done(((f32[4,128,128]{2,1,0:T(8,128)}), f32[4,128,128]{2,1,0:T(8,128)S(1)}, u32[]{:S(2)}, u32[]{:S(2)}) %all-to-all-start.11) | async-done | bytes 262176 | tf_op jit(solution)/shard_map/all_to_all | solution.py:136
  212.7 13.2 %all_to_all.165 = bf16[8,144,128]{2,1,0:T(8,128)(2,1)S(1)} all-to-all(bf16[8,144,128]{2,1,0:T(8,128)(2,1)S(1)} %broadcast_in_dim.84), channel_id=1, replica_groups=mesh['sub_0'=8,'sub_1'=2,'blk_0'=4,'blk_1'=8] {'blk_1'}, dimensions={0} | all-to-all | bytes 589824 | tf_op jit(solution)/shard_map/all_to_all | solution.py:29
  227.1 8.0 %all_to_all.166 = f32[4,136,128]{2,1,0:T(8,128)S(1)} all-to-all(f32[4,136,128]{2,1,0:T(8,128)S(1)} %pad_maximum_fusion.13), channel_id=1, replica_groups=mesh['sub_0'=8,'sub_1'=2,'blk_0'=4,'blk_1'=8] {'blk_0'}, dimensions={0} | all-to-all | bytes 557056 | tf_op jit(solution)/shard_map/all_to_all | solution.py:136
  236.2 13.7 %all_to_all.167 = f32[16,1,192]{2,1,0:T(1,128)S(1)} all-to-all(f32[16,1,192]{2,1,0:T(1,128)S(1)} %reshape.914), channel_id=1, replica_groups=mesh['sub_0'=8,'sub_1'=2,'blk_0'=4,'blk_1'=8] {'sub_0','sub_1'}, dimensions={0} | all-to-all | bytes 24576 | tf_op jit(solution)/shard_map/all_to_all | solution.py:29
  254.9 11.4 %all-to-all-done.15 = bf16[8,128,128]{2,1,0:T(8,128)(2,1)S(1)} async-done(((bf16[8,128,128]{2,1,0:T(8,128)(2,1)}), bf16[8,128,128]{2,1,0:T(8,128)(2,1)S(1)}, u32[]{:S(2)}, u32[]{:S(2)}) %all-to-all-start.15) | async-done | bytes 262176 | tf_op jit(solution)/shard_map/all_to_all | solution.py:29
  277.8 6.5 %all-to-all-done.16 = f32[4,128,128]{2,1,0:T(8,128)S(1)} async-done(((f32[4,128,128]{2,1,0:T(8,128)}), f32[4,128,128]{2,1,0:T(8,128)S(1)}, u32[]{:S(2)}, u32[]{:S(2)}) %all-to-all-start.16) | async-done | bytes 262176 | tf_op jit(solution)/shard_map/all_to_all | solution.py:136
  285.2 3.4 all-to-all-start.18
  288.6 11.1 %all-to-all-done.18 = bf16[8,144,128]{2,1,0:T(8,128)(2,1)S(1)} async-done(((bf16[8,144,128]{2,1,0:T(8,128)(2,1)}), bf16[8,144,128]{2,1,0:T(8,128)(2,1)S(1)}, u32[]{:S(2)}, u32[]{:S(2)}) %all-to-all-start.18) | async-done | bytes 294944 | tf_op jit(solution)/shard_map/all_to_all | solution.py:29
  301.7 3.4 all-to-all-start.19
  305.2 5.5 %all-to-all-done.19 = f32[4,136,128]{2,1,0:T(8,128)S(1)} async-done(((f32[4,136,128]{2,1,0:T(8,128)}), f32[4,136,128]{2,1,0:T(8,128)S(1)}, u32[]{:S(2)}, u32[]{:S(2)}) %all-to-all-start.19) | async-done | bytes 278560 | tf_op jit(solution)/shard_map/all_to_all | solution.py:136
  314.8 13.9 %all_to_all.168 = f32[16,1,256]{2,1,0:T(1,128)S(1)} all-to-all(f32[16,1,256]{2,1,0:T(1,128)S(1)} %reshape.916), channel_id=1, replica_groups=mesh['sub_0'=8,'sub_1'=2,'blk_0'=4,'blk_1'=8] {'sub_0','sub_1'}, dimensions={0} | all-to-all | bytes 32768 | tf_op jit(solution)/shard_map/all_to_all | solution.py:29
  329.4 3.4 all-to-all-start.20
  334.2 10.9 %all-to-all-done.20 = bf16[8,128,128]{2,1,0:T(8,128)(2,1)S(1)} async-done(((bf16[8,128,128]{2,1,0:T(8,128)(2,1)}), bf16[8,128,128]{2,1,0:T(8,128)(2,1)S(1)}, u32[]{:S(2)}, u32[]{:S(2)}) %all-to-all-start.20) | async-done | bytes 262176 | tf_op jit(solution)/shard_map/all_to_all | solution.py:29
  357.3 6.5 %all-to-all-done.21 = f32[4,128,128]{2,1,0:T(8,128)S(1)} async-done(((f32[4,128,128]{2,1,0:T(8,128)}), f32[4,128,128]{2,1,0:T(8,128)S(1)}, u32[]{:S(2)}, u32[]{:S(2)}) %all-to-all-start.21) | async-done | bytes 262176 | tf_op jit(solution)/shard_map/all_to_all | solution.py:136
  364.6 3.4 all-to-all-start.23
  368.9 10.3 %all-to-all-done.23 = bf16[8,144,128]{2,1,0:T(8,128)(2,1)S(1)} async-done(((bf16[8,144,128]{2,1,0:T(8,128)(2,1)}), bf16[8,144,128]{2,1,0:T(8,128)(2,1)S(1)}, u32[]{:S(2)}, u32[]{:S(2)}) %all-to-all-start.23) | async-done | bytes 294944 | tf_op jit(solution)/shard_map/all_to_all | solution.py:29
  381.2 3.6 all-to-all-start.24
  384.9 5.5 %all-to-all-done.24 = f32[4,136,128]{2,1,0:T(8,128)S(1)} async-done(((f32[4,136,128]{2,1,0:T(8,128)}), f32[4,136,128]{2,1,0:T(8,128)S(1)}, u32[]{:S(2)}, u32[]{:S(2)}) %all-to-all-start.24) | async-done | bytes 278560 | tf_op jit(solution)/shard_map/all_to_all | solution.py:136
  393.1 13.9 %all_to_all.169 = f32[16,1,320]{2,1,0:T(1,128)S(1)} all-to-all(f32[16,1,320]{2,1,0:T(1,128)S(1)} %reshape.918), channel_id=1, replica_groups=mesh['sub_0'=8,'sub_1'=2,'blk_0'=4,'blk_1'=8] {'sub_0','sub_1'}, dimensions={0} | all-to-all | bytes 40960 | tf_op jit(solution)/shard_map/all_to_all | solution.py:29
  407.8 3.6 all-to-all-start.25
  412.8 10.8 %all-to-all-done.25 = bf16[8,128,128]{2,1,0:T(8,128)(2,1)S(1)} async-done(((bf16[8,128,128]{2,1,0:T(8,128)(2,1)}), bf16[8,128,128]{2,1,0:T(8,128)(2,1)S(1)}, u32[]{:S(2)}, u32[]{:S(2)}) %all-to-all-start.25) | async-done | bytes 262176 | tf_op jit(solution)/shard_map/all_to_all | solution.py:29
  435.3 6.5 %all-to-all-done.26 = f32[4,128,128]{2,1,0:T(8,128)S(1)} async-done(((f32[4,128,128]{2,1,0:T(8,128)}), f32[4,128,128]{2,1,0:T(8,128)S(1)}, u32[]{:S(2)}, u32[]{:S(2)}) %all-to-all-start.26) | async-done | bytes 262176 | tf_op jit(solution)/shard_map/all_to_all | solution.py:136
  442.6 3.4 all-to-all-start.28
  446.1 11.0 %all-to-all-done.28 = bf16[8,144,128]{2,1,0:T(8,128)(2,1)S(1)} async-done(((bf16[8,144,128]{2,1,0:T(8,128)(2,1)}), bf16[8,144,128]{2,1,0:T(8,128)(2,1)S(1)}, u32[]{:S(2)}, u32[]{:S(2)}) %all-to-all-start.28) | async-done | bytes 294944 | tf_op jit(solution)/shard_map/all_to_all | solution.py:29
  459.5 3.4 all-to-all-start.29
  463.0 5.5 %all-to-all-done.29 = f32[4,136,128]{2,1,0:T(8,128)S(1)} async-done(((f32[4,136,128]{2,1,0:T(8,128)}), f32[4,136,128]{2,1,0:T(8,128)S(1)}, u32[]{:S(2)}, u32[]{:S(2)}) %all-to-all-start.29) | async-done | bytes 278560 | tf_op jit(solution)/shard_map/all_to_all | solution.py:136
  470.9 6.8 %all-to-all-start.30 = ((f32[16,1,384]{2,1,0:T(1,128)}), f32[16,1,384]{2,1,0:T(1,128)S(1)}, u32[]{:S(2)}, u32[]{:S(2)}) async-start(f32[16,1,384]{2,1,0:T(1,128)} %reshape.920), calls=%async_computation.30 | async-start | bytes 49152 | tf_op jit(solution)/shard_map/all_to_all | solution.py:29
  477.7 7.3 %all-to-all-done.30 = f32[16,1,384]{2,1,0:T(1,128)S(1)} async-done(((f32[16,1,384]{2,1,0:T(1,128)}), f32[16,1,384]{2,1,0:T(1,128)S(1)}, u32[]{:S(2)}, u32[]{:S(2)}) %all-to-all-start.30) | async-done | bytes 24608 | tf_op jit(solution)/shard_map/all_to_all | solution.py:29
  486.5 3.9 all-to-all-start.31
  490.4 8.8 %all-to-all-done.31 = f32[32,1,384]{2,1,0:T(1,128)S(1)} async-done(((f32[32,1,384]{2,1,0:T(1,128)}), f32[32,1,384]{2,1,0:T(1,128)S(1)}, u32[]{:S(2)}, u32[]{:S(2)}) %all-to-all-start.31) | async-done | bytes 49184 | tf_op jit(solution)/shard_map/all_to_all | solution.py:29
  (648 shorter events, 116.3 us)
Async XLA Ops:
  1.0 60.8 %copy-start.12 = (f32[2,64,64]{2,1,0:T(8,128)}, f32[2,64,64]{2,1,0:T(8,128)S(1)}, u32[]{:S(2)}) copy-start(f32[2,64,64]{2,1,0:T(8,128)S(1)} %get-tuple-element.127) | copy-start | bytes 98308
  1.0 60.8 %copy-start.14 = (f32[2,64,64]{2,1,0:T(8,128)}, f32[2,64,64]{2,1,0:T(8,128)S(1)}, u32[]{:S(2)}) copy-start(f32[2,64,64]{2,1,0:T(8,128)S(1)} %get-tuple-element.128) | copy-start | bytes 98308
  1.9 17.1 %all-to-all-start.1 = ((bf16[8,128,128]{2,1,0:T(8,128)(2,1)}), bf16[8,128,128]{2,1,0:T(8,128)(2,1)S(1)}, u32[]{:S(2)}, u32[]{:S(2)}) async-start(bf16[8,128,128]{2,1,0:T(8,128)(2,1)} %broadcast_in_dim.74), calls=%async_computation.1 | async-start | bytes 524288 | tf_op jit(solution)/shard_map/all_to_all | solution.py:29
  16.2 250.2 %copy-start.93 = (s32[512]{0:T(512)}, s32[512]{0:T(512)S(1)}, u32[]{:S(2)}) copy-start(s32[512]{0:T(512)S(1)} %iota_add_fusion.1) | copy-start | bytes 6148
  18.9 28.9 %all-to-all-start = ((bf16[4,128,2048]{2,1,0:T(8,128)(2,1)}), bf16[4,128,2048]{2,1,0:T(8,128)(2,1)S(1)}, u32[]{:S(2)}, u32[]{:S(2)}) async-start(bf16[4,128,2048]{2,1,0:T(8,128)(2,1)} %maximum_maximum_fusion), calls=%async_computation | async-start | bytes 4194304 | tf_op jit(solution)/shard_map/all_to_all | solution.py:66
  24.0 242.3 %copy-start.110 = (s32[256]{0:T(256)}, s32[256]{0:T(256)S(1)}, u32[]{:S(2)}) copy-start(s32[256]{0:T(256)S(1)} %pad_add_fusion) | copy-start | bytes 3076
  24.4 8.8 %collective-permute-start = (bf16[2,128,128]{1,2,0:T(8,128)(2,1)S(1)}, bf16[2,128,128]{1,2,0:T(8,128)(2,1)S(1)}, u32[]{:S(2)}, u32[]{:S(2)}) collective-permute-start(bf16[2,128,128]{1,2,0:T(8,128)(2,1)S(1)} %get-tuple-element.124), channel_id=1, source_target_pairs={{32,64},{64,32},{96,128},{128,96},{160,192},{192,160},{224,256},{2... | collective-permute-start | bytes 196616 | tf_op jit(solution)/shard_map/ppermute | solution.py:20
  31.0 3.1 collective-permute-start.1
  57.2 14.0 %all-to-all-start.3 = ((bf16[8,128,128]{2,1,0:T(8,128)(2,1)}), bf16[8,128,128]{2,1,0:T(8,128)(2,1)S(1)}, u32[]{:S(2)}, u32[]{:S(2)}) async-start(bf16[8,128,128]{2,1,0:T(8,128)(2,1)} %broadcast_in_dim.77), calls=%async_computation.3 | async-start | bytes 524288 | tf_op jit(solution)/shard_map/all_to_all | solution.py:29
  73.0 8.9 %all-to-all-start.4 = ((f32[4,128,128]{2,1,0:T(8,128)}), f32[4,128,128]{2,1,0:T(8,128)S(1)}, u32[]{:S(2)}, u32[]{:S(2)}) async-start(f32[4,128,128]{2,1,0:T(8,128)} %fusion.167), calls=%async_computation.4 | async-start | bytes 524288 | tf_op jit(solution)/shard_map/all_to_all | solution.py:136
  107.4 15.6 %all-to-all-start.5 = ((bf16[8,128,128]{2,1,0:T(8,128)(2,1)}), bf16[8,128,128]{2,1,0:T(8,128)(2,1)S(1)}, u32[]{:S(2)}, u32[]{:S(2)}) async-start(bf16[8,128,128]{2,1,0:T(8,128)(2,1)} %broadcast_in_dim.78), calls=%async_computation.5 | async-start | bytes 524288 | tf_op jit(solution)/shard_map/all_to_all | solution.py:29
  123.6 5.6 %collective-permute-start.2 = (bf16[2,128,128]{1,2,0:T(8,128)(2,1)S(1)}, bf16[2,128,128]{1,2,0:T(8,128)(2,1)S(1)}, u32[]{:S(2)}, u32[]{:S(2)}) collective-permute-start(bf16[2,128,128]{1,2,0:T(8,128)(2,1)S(1)} %get-tuple-element.120), channel_id=1, source_target_pairs={{32,64},{64,32},{96,128},{128,96},{160,192},{192,160},{224,256},{2... | collective-permute-start | bytes 196616 | tf_op jit(solution)/shard_map/ppermute | solution.py:20
  126.2 3.1 collective-permute-start.3
  131.1 10.0 %all-to-all-start.6 = ((f32[4,128,128]{2,1,0:T(8,128)}), f32[4,128,128]{2,1,0:T(8,128)S(1)}, u32[]{:S(2)}, u32[]{:S(2)}) async-start(f32[4,128,128]{2,1,0:T(8,128)} %convolution_subtract_fusion.4), calls=%async_computation.6 | async-start | bytes 524288 | tf_op jit(solution)/shard_map/all_to_all | solution.py:136
  163.7 124.9 %copy-start.53 = (f32[4,64]{1,0:T(4,128)}, f32[4,64]{1,0:T(4,128)S(1)}, u32[]{:S(2)}) copy-start(f32[4,64]{1,0:T(4,128)S(1)} %reshape.818) | copy-start | bytes 3076
  163.8 71.7 %copy-start.85 = (f32[128]{0:T(128)}, f32[128]{0:T(128)S(1)}, u32[]{:S(2)}) copy-start(f32[128]{0:T(128)S(1)} %pad_maximum_fusion.39) | copy-start | bytes 1540
  163.9 71.7 %copy-start.28 = (f32[128]{0:T(128)}, f32[128]{0:T(128)S(1)}, u32[]{:S(2)}) copy-start(f32[128]{0:T(128)S(1)} %pad_maximum_fusion.38) | copy-start | bytes 1540
  178.9 14.4 %all-to-all-start.10 = ((bf16[8,128,128]{2,1,0:T(8,128)(2,1)}), bf16[8,128,128]{2,1,0:T(8,128)(2,1)S(1)}, u32[]{:S(2)}, u32[]{:S(2)}) async-start(bf16[8,128,128]{2,1,0:T(8,128)(2,1)} %broadcast_in_dim.82), calls=%async_computation.10 | async-start | bytes 524288 | tf_op jit(solution)/shard_map/all_to_all | solution.py:29
  193.9 6.2 %collective-permute-start.4 = (bf16[2,128,128]{1,2,0:T(8,128)(2,1)S(1)}, bf16[2,128,128]{1,2,0:T(8,128)(2,1)S(1)}, u32[]{:S(2)}, u32[]{:S(2)}) collective-permute-start(bf16[2,128,128]{1,2,0:T(8,128)(2,1)S(1)} %get-tuple-element.116), channel_id=1, source_target_pairs={{32,64},{64,32},{96,128},{128,96},{160,192},{192,160},{224,256},{2... | collective-permute-start | bytes 196616 | tf_op jit(solution)/shard_map/ppermute | solution.py:20
  197.7 3.1 collective-permute-start.5
  202.6 10.0 %all-to-all-start.11 = ((f32[4,128,128]{2,1,0:T(8,128)}), f32[4,128,128]{2,1,0:T(8,128)S(1)}, u32[]{:S(2)}, u32[]{:S(2)}) async-start(f32[4,128,128]{2,1,0:T(8,128)} %convolution_subtract_fusion.3), calls=%async_computation.11 | async-start | bytes 524288 | tf_op jit(solution)/shard_map/all_to_all | solution.py:136
  235.2 70.0 %copy-start.25 = (f32[1,64]{1,0:T(1,128)}, f32[1,64]{1,0:T(1,128)S(1)}, u32[]{:S(2)}) copy-start(f32[1,64]{1,0:T(1,128)S(1)} %get-tuple-element.59) | copy-start | bytes 772
  250.7 15.6 %all-to-all-start.15 = ((bf16[8,128,128]{2,1,0:T(8,128)(2,1)}), bf16[8,128,128]{2,1,0:T(8,128)(2,1)S(1)}, u32[]{:S(2)}, u32[]{:S(2)}) async-start(bf16[8,128,128]{2,1,0:T(8,128)(2,1)} %broadcast_in_dim.86), calls=%async_computation.15 | async-start | bytes 524288 | tf_op jit(solution)/shard_map/all_to_all | solution.py:29
  266.9 5.6 %collective-permute-start.6 = (bf16[2,128,128]{1,2,0:T(8,128)(2,1)S(1)}, bf16[2,128,128]{1,2,0:T(8,128)(2,1)S(1)}, u32[]{:S(2)}, u32[]{:S(2)}) collective-permute-start(bf16[2,128,128]{1,2,0:T(8,128)(2,1)S(1)} %get-tuple-element.112), channel_id=1, source_target_pairs={{32,64},{64,32},{96,128},{128,96},{160,192},{192,160},{224,256},{2... | collective-permute-start | bytes 196616 | tf_op jit(solution)/shard_map/ppermute | solution.py:20
  269.5 3.1 collective-permute-start.7
  274.4 10.0 %all-to-all-start.16 = ((f32[4,128,128]{2,1,0:T(8,128)}), f32[4,128,128]{2,1,0:T(8,128)S(1)}, u32[]{:S(2)}, u32[]{:S(2)}) async-start(f32[4,128,128]{2,1,0:T(8,128)} %convolution_subtract_fusion.2), calls=%async_computation.16 | async-start | bytes 524288 | tf_op jit(solution)/shard_map/all_to_all | solution.py:136
  285.2 14.5 %all-to-all-start.18 = ((bf16[8,144,128]{2,1,0:T(8,128)(2,1)}), bf16[8,144,128]{2,1,0:T(8,128)(2,1)S(1)}, u32[]{:S(2)}, u32[]{:S(2)}) async-start(bf16[8,144,128]{2,1,0:T(8,128)(2,1)} %broadcast_in_dim.88), calls=%async_computation.18 | async-start | bytes 589824 | tf_op jit(solution)/shard_map/all_to_all | solution.py:29
  300.9 44.2 %copy-start.94 = (s32[512]{0:T(512)S(1)}, s32[512]{0:T(512)}, u32[]{:S(2)}) copy-start(s32[512]{0:T(512)} %copy-done.93) | copy-start | bytes 6148
  300.9 44.2 %copy-start.111 = (s32[256]{0:T(256)S(1)}, s32[256]{0:T(256)}, u32[]{:S(2)}) copy-start(s32[256]{0:T(256)} %copy-done.110) | copy-start | bytes 3076
  301.7 9.0 %all-to-all-start.19 = ((f32[4,136,128]{2,1,0:T(8,128)}), f32[4,136,128]{2,1,0:T(8,128)S(1)}, u32[]{:S(2)}, u32[]{:S(2)}) async-start(f32[4,136,128]{2,1,0:T(8,128)} %pad_maximum_fusion.14), calls=%async_computation.19 | async-start | bytes 557056 | tf_op jit(solution)/shard_map/all_to_all | solution.py:136
  310.8 81.6 %copy-start = (f32[136,128]{1,0:T(8,128)}, f32[136,128]{1,0:T(8,128)S(1)}, u32[]{:S(2)}) copy-start(f32[136,128]{1,0:T(8,128)S(1)} %reduce_sum.579) | copy-start | bytes 208900
  329.4 15.6 %all-to-all-start.20 = ((bf16[8,128,128]{2,1,0:T(8,128)(2,1)}), bf16[8,128,128]{2,1,0:T(8,128)(2,1)S(1)}, u32[]{:S(2)}, u32[]{:S(2)}) async-start(bf16[8,128,128]{2,1,0:T(8,128)(2,1)} %broadcast_in_dim.92), calls=%async_computation.20 | async-start | bytes 524288 | tf_op jit(solution)/shard_map/all_to_all | solution.py:29
  345.7 5.6 %collective-permute-start.8 = (bf16[2,128,128]{1,2,0:T(8,128)(2,1)S(1)}, bf16[2,128,128]{1,2,0:T(8,128)(2,1)S(1)}, u32[]{:S(2)}, u32[]{:S(2)}) collective-permute-start(bf16[2,128,128]{1,2,0:T(8,128)(2,1)S(1)} %get-tuple-element.108), channel_id=1, source_target_pairs={{32,64},{64,32},{96,128},{128,96},{160,192},{192,160},{224,256},{2... | collective-permute-start | bytes 196616 | tf_op jit(solution)/shard_map/ppermute | solution.py:20
  348.3 3.1 collective-permute-start.9
  353.9 10.0 %all-to-all-start.21 = ((f32[4,128,128]{2,1,0:T(8,128)}), f32[4,128,128]{2,1,0:T(8,128)S(1)}, u32[]{:S(2)}, u32[]{:S(2)}) async-start(f32[4,128,128]{2,1,0:T(8,128)} %convolution_subtract_fusion.1), calls=%async_computation.21 | async-start | bytes 524288 | tf_op jit(solution)/shard_map/all_to_all | solution.py:136
  364.6 14.5 %all-to-all-start.23 = ((bf16[8,144,128]{2,1,0:T(8,128)(2,1)}), bf16[8,144,128]{2,1,0:T(8,128)(2,1)S(1)}, u32[]{:S(2)}, u32[]{:S(2)}) async-start(bf16[8,144,128]{2,1,0:T(8,128)(2,1)} %broadcast_in_dim.94), calls=%async_computation.23 | async-start | bytes 589824 | tf_op jit(solution)/shard_map/all_to_all | solution.py:29
  381.2 42.5 %copy-start.95 = (s32[512]{0:T(512)S(1)}, s32[512]{0:T(512)}, u32[]{:S(2)}) copy-start(s32[512]{0:T(512)} %copy-done.93) | copy-start | bytes 6148
  381.2 42.5 %copy-start.112 = (s32[256]{0:T(256)S(1)}, s32[256]{0:T(256)}, u32[]{:S(2)}) copy-start(s32[256]{0:T(256)} %copy-done.110) | copy-start | bytes 3076
  381.2 9.2 %all-to-all-start.24 = ((f32[4,136,128]{2,1,0:T(8,128)}), f32[4,136,128]{2,1,0:T(8,128)S(1)}, u32[]{:S(2)}, u32[]{:S(2)}) async-start(f32[4,136,128]{2,1,0:T(8,128)} %pad_maximum_fusion.15), calls=%async_computation.24 | async-start | bytes 557056 | tf_op jit(solution)/shard_map/all_to_all | solution.py:136
  407.8 15.9 %all-to-all-start.25 = ((bf16[8,128,128]{2,1,0:T(8,128)(2,1)}), bf16[8,128,128]{2,1,0:T(8,128)(2,1)S(1)}, u32[]{:S(2)}, u32[]{:S(2)}) async-start(bf16[8,128,128]{2,1,0:T(8,128)(2,1)} %broadcast_in_dim.97), calls=%async_computation.25 | async-start | bytes 524288 | tf_op jit(solution)/shard_map/all_to_all | solution.py:29
  424.3 5.6 %collective-permute-start.10 = (bf16[2,128,128]{1,2,0:T(8,128)(2,1)S(1)}, bf16[2,128,128]{1,2,0:T(8,128)(2,1)S(1)}, u32[]{:S(2)}, u32[]{:S(2)}) collective-permute-start(bf16[2,128,128]{1,2,0:T(8,128)(2,1)S(1)} %get-tuple-element.100), channel_id=1, source_target_pairs={{32,64},{64,32},{96,128},{128,96},{160,192},{192,160},{224,256},{2... | collective-permute-start | bytes 196616 | tf_op jit(solution)/shard_map/ppermute | solution.py:20
  426.9 3.1 collective-permute-start.11
  431.8 10.0 %all-to-all-start.26 = ((f32[4,128,128]{2,1,0:T(8,128)}), f32[4,128,128]{2,1,0:T(8,128)S(1)}, u32[]{:S(2)}, u32[]{:S(2)}) async-start(f32[4,128,128]{2,1,0:T(8,128)} %convolution_subtract_fusion), calls=%async_computation.26 | async-start | bytes 524288 | tf_op jit(solution)/shard_map/all_to_all | solution.py:136
  442.6 14.6 %all-to-all-start.28 = ((bf16[8,144,128]{2,1,0:T(8,128)(2,1)}), bf16[8,144,128]{2,1,0:T(8,128)(2,1)S(1)}, u32[]{:S(2)}, u32[]{:S(2)}) async-start(bf16[8,144,128]{2,1,0:T(8,128)(2,1)} %broadcast_in_dim.99), calls=%async_computation.28 | async-start | bytes 589824 | tf_op jit(solution)/shard_map/all_to_all | solution.py:29
  458.6 42.0 %slice-start = ((f32[136,128]{1,0:T(8,128)}), f32[128,128]{1,0:T(8,128)S(1)}, s32[]{:S(2)}) async-start(f32[136,128]{1,0:T(8,128)} %copy-done.2), calls=%async_computation.32 | async-start | bytes 131072 | tf_op jit(solution)/shard_map/slice | solution.py:178
  459.5 9.0 %all-to-all-start.29 = ((f32[4,136,128]{2,1,0:T(8,128)}), f32[4,136,128]{2,1,0:T(8,128)S(1)}, u32[]{:S(2)}, u32[]{:S(2)}) async-start(f32[4,136,128]{2,1,0:T(8,128)} %pad_maximum_fusion.16), calls=%async_computation.29 | async-start | bytes 557056 | tf_op jit(solution)/shard_map/all_to_all | solution.py:136
  470.9 14.1 %all-to-all-start.30 = ((f32[16,1,384]{2,1,0:T(1,128)}), f32[16,1,384]{2,1,0:T(1,128)S(1)}, u32[]{:S(2)}, u32[]{:S(2)}) async-start(f32[16,1,384]{2,1,0:T(1,128)} %reshape.920), calls=%async_computation.30 | async-start | bytes 49152 | tf_op jit(solution)/shard_map/all_to_all | solution.py:29
  486.5 12.7 %all-to-all-start.31 = ((f32[32,1,384]{2,1,0:T(1,128)}), f32[32,1,384]{2,1,0:T(1,128)S(1)}, u32[]{:S(2)}, u32[]{:S(2)}) async-start(f32[32,1,384]{2,1,0:T(1,128)} %reshape.922), calls=%async_computation.31 | async-start | bytes 98304 | tf_op jit(solution)/shard_map/all_to_all | solution.py:29
  (101 other events, 1440.3 us)

commit v3 on v2

--- a/solution.py
+++ b/solution.py
@@ -12,16 +12,10 @@
 EPSILON = 1e-06
 
 
-def swapped_in_pairs(block, axis, first):
-    devices = lax.axis_size(axis)
-    route = []
-    for low in range(first, devices - 1, 2):
-        route += [(low, low + 1), (low + 1, low)]
+def passed_along(block, axis, distance):
+    devices = range(lax.axis_size(axis))
+    route = [(i - distance, i) for i in devices if i - distance in devices]
     return lax.ppermute(block, axis, route)
-
-
-def on_even_subdomain():
-    return lax.axis_index(SUB) % 2 == 0
 
 
 def copy_for_each(value, axis):
@@ -88,12 +82,7 @@
     inverse_here = jnp.sum(
         jnp.where(perm_here[None, :] == wanted[:, None], spots[None, :], 0), axis=1
     )
-    upward = 2 * window(perm_above) + 1
-    downward = 2 * inverse_here
-    even = on_even_subdomain()
-    dofs = jnp.concatenate(
-        [jnp.where(even, upward, downward), jnp.where(even, downward, upward)]
-    )
+    dofs = jnp.concatenate([2 * window(perm_above) + 1, 2 * inverse_here])
     width = 2 * half // lines
     columns = lax.axis_index("blk_0") * width + jnp.arange(width, dtype=jnp.int32)
     return (dofs[:, None] == columns[None, :]).astype(jnp.bfloat16)
@@ -120,11 +109,8 @@
         "sk,tkn->tsn", selector, columns, preferred_element_type=jnp.float32
     ).astype(jnp.bfloat16)
     middle = chosen.shape[1] // 2
-    inner_face = swapped_in_pairs(chosen[:, :middle], SUB, 0)
-    outer_face = swapped_in_pairs(chosen[:, middle:], SUB, 1)
-    even = on_even_subdomain()
-    lower_face = jnp.where(even, outer_face, inner_face)
-    upper_face = jnp.where(even, inner_face, outer_face)
+    lower_face = passed_along(chosen[:, :middle], SUB, 1)
+    upper_face = passed_along(chosen[:, middle:], SUB, -1)
     joined = jnp.stack([lower_face, upper_face], axis=2)
     joined = joined.reshape(2, lines, 2 * middle // lines, chosen.shape[-1])
     signs = jnp.array([1.0, -1.0], jnp.float32).reshape(1, 2, 1, 1)
@@ -132,8 +118,12 @@
     return signed.reshape(lines, -1, signed.shape[-1])
 
 
+def exchanged_rows(partials):
+    return lax.all_to_all(partials, "blk_0", 0, 0, tiled=True).astype(jnp.float32)
+
+
 def reduced_rows(partials):
-    return jnp.sum(lax.all_to_all(partials, "blk_0", 0, 0, tiled=True), axis=0)
+    return jnp.sum(exchanged_rows(partials.astype(jnp.bfloat16)), axis=0)
 
 
 def padded_rows(value, multiple):
@@ -148,34 +138,48 @@
     return jnp.concatenate([high, middle, low]).astype(jnp.bfloat16)
 
 
+def pieces_of(dots, width):
+    packed = padded_rows(dots, 2).reshape(-1, width)
+    return padded_rows(in_three_pieces(packed), 16)
+
+
+def sum_of_pieces(blocks, lines):
+    carried = blocks[:, : 3 * lines].astype(jnp.float32)
+    return jnp.sum(carried.reshape(-1, 3, lines, carried.shape[-1]), axis=(0, 1))
+
+
 def preconditioned(tile, selector, vector, dots=None):
     shape = vector.shape
     width = shape[-1]
-    columns = side_by_side(
-        copy_for_each(vector.astype(jnp.bfloat16).reshape(-1, width), "blk_1")
-    )
+    payload = vector.astype(jnp.bfloat16).reshape(-1, width)
+    rows = payload.shape[0]
     if dots is not None:
+        payload, dots = lax.optimization_barrier((payload, dots))
+    blocks = copy_for_each(payload, "blk_1")
+    if dots is not None:
+        blocks, dots = lax.optimization_barrier((blocks, dots))
         dots = summed_over(dots, SUB)
+    columns = side_by_side(blocks)
     first = partial_products(tile, columns) - 0.5 * coupling_partials(selector, columns)
-    middle = reduced_rows(first).astype(jnp.bfloat16)
-    rows = middle.shape[0]
+    first = first.astype(jnp.bfloat16)
     if dots is None:
+        middle = reduced_rows(first).astype(jnp.bfloat16)
         middle_columns = side_by_side(copy_for_each(middle, "blk_1"))
         return reduced_rows(partial_products(tile, middle_columns)).reshape(shape)
     count, narrow = dots.shape
-    packed = padded_rows(dots, 2).reshape(-1, width)
-    lines = packed.shape[0]
-    pieces = padded_rows(in_three_pieces(packed), 16)
+    pieces = pieces_of(dots, width)
+    lines = -(-count * narrow // width)
+    first, pieces = lax.optimization_barrier((first, pieces))
+    middle = reduced_rows(first).astype(jnp.bfloat16)
     blocks = copy_for_each(jnp.concatenate([middle, pieces]), "blk_1")
-    carried = blocks[:, rows : rows + 3 * lines].astype(jnp.float32)
-    carried = jnp.sum(carried.reshape(-1, 3, lines, width), axis=(0, 1))
-    second = partial_products(tile, side_by_side(blocks[:, :rows]))
-    carried = jnp.broadcast_to(
-        padded_rows(carried, 8)[None], (second.shape[0], lines + -lines % 8, width)
-    )
-    total = reduced_rows(jnp.concatenate([second, carried], axis=1))
-    dots = total[rows : rows + lines].reshape(-1, narrow)[:count]
-    return total[:rows].reshape(shape), dots
+    second = partial_products(tile, side_by_side(blocks[:, :rows])).astype(jnp.bfloat16)
+    carried = in_three_pieces(sum_of_pieces(blocks[:, rows:], lines))
+    carried = padded_rows(carried, 16)
+    carried = jnp.broadcast_to(carried[None], (second.shape[0], *carried.shape))
+    exchanged = exchanged_rows(jnp.concatenate([second, carried], axis=1))
+    image = jnp.sum(exchanged[:, :rows], axis=0).reshape(shape)
+    dots = sum_of_pieces(exchanged[:, rows:], lines).reshape(-1, narrow)[:count]
+    return image, dots
 
 
 def inner_local(first, second):
@@ -248,6 +252,9 @@
         ahead = images[column] - spread(shift) * basis[column]
         local_dots = [inner_local(vector, ahead) for vector in basis]
         local_dots = jnp.stack(local_dots + [inner_local(ahead, ahead)])
+        ahead, local_dots, gram, shift, hessen, beta = lax.optimization_barrier(
+            (ahead, local_dots, gram, shift, hessen, beta)
+        )
         if column + 1 < BASIS:
             applied, sums = preconditioned(tile, selector, ahead, local_dots)
         else:

time: 505 us -> 458 us (0.907)
  waiting for transfers between devices: 186 us -> 75.4 us
  blocking collectives: 130 us -> 219 us
  starting transfers between devices: 119 us -> 105 us
  local copies, waits for them, and re-layouts: 24.9 us -> 18.5 us
    all_to_all x12 -> x8, waiting for transfers between devices: 113 us -> 56.6 us  [copy_for_each(): lax.all_to_all(jnp.broadcast_to(value[None], (peers, *value.shape)), axis...]
    all_to_all x3 -> x11, blocking collectives: 23.9 us -> 79.6 us  [exchanged_rows(): lax.all_to_all(partials, 'blk_0', 0, 0, tiled=True).astype(jnp.float32)]
    all_to_all x9 -> x1, waiting for transfers between devices: 54.7 us -> 4.72 us  [exchanged_rows(): lax.all_to_all(partials, 'blk_0', 0, 0, tiled=True).astype(jnp.float32)]
    all_to_all x7 -> x11, blocking collectives: 106 us -> 139 us  [copy_for_each(): lax.all_to_all(jnp.broadcast_to(value[None], (peers, *value.shape)), axis...]
    all_to_all x9 -> x1, starting transfers between devices: 30.9 us -> 3.33 us  [exchanged_rows(): lax.all_to_all(partials, 'blk_0', 0, 0, tiled=True).astype(jnp.float32)]
    ppermute x12, starting transfers between devices: 32.4 us -> 56.6 us  [passed_along(): return lax.ppermute(block, axis, route)]
    all_to_all x12 -> x8, starting transfers between devices: 50.4 us -> 40 us  [copy_for_each(): lax.all_to_all(jnp.broadcast_to(value[None], (peers, *value.shape)), axis...]
    broadcast_in_dim x19, local copies, waits for them, and re-layouts: 7.65 us -> 1.92 us  [copy_for_each(): jnp.broadcast_to(value[None], (peers, *value.shape))]
  transfers between devices with their start and end apart: 34 -> 22, of which waited for: 32 -> 11; matrix products, arithmetic and copies ran while one was open for 3% -> 4% of each run, Pallas kernels for 0% -> 0%
where the time goes in v3:
time: 458 us; the launch traced here: 455 us
  blocking collectives  219 us (48%)
  starting transfers between devices  105 us (23%)
  waiting for transfers between devices  75.4 us (16%)
  other arithmetic  23.4 us (5%)
  local copies, waits for them, and re-layouts  18.5 us (4%)
  matrix products  11.3 us (2%)
    all_to_all x11, blocking collectives, copy_for_each(): lax.all_to_all(jnp.broadcast_to(value[None], (peers, *value.shape)), axis...  139 us
    all_to_all x11, blocking collectives, exchanged_rows(): lax.all_to_all(partials, 'blk_0', 0, 0, tiled=True).astype(jnp.float32)  79.6 us
    all_to_all x8, waiting for transfers between devices, copy_for_each(): lax.all_to_all(jnp.broadcast_to(value[None], (peers, *value.shape)), axis...  56.6 us
    ppermute x12, starting transfers between devices, passed_along(): return lax.ppermute(block, axis, route)  56.6 us
    all_to_all x8, starting transfers between devices, copy_for_each(): lax.all_to_all(jnp.broadcast_to(value[None], (peers, *value.shape)), axis...  40 us
    all_to_all x1, waiting for transfers between devices, tile_of_operators(): blocks = lax.all_to_all(strips, 'blk_0', 0, 0, tiled=True)  13.1 us
    dot_general x12, matrix products, partial_products(): products = jnp.dot(tile, stacked, preferred_element_type=jnp.float32)  9.16 us
  transfers between devices with their start and end apart: 22, of which 11 were waited for; matrix products, arithmetic and copies ran while one was open for 4% of the time, Pallas kernels for 0%

profile of v3, /device:TPU:1, one launch (start us, length us, event | category | flops | bytes accessed | tf_op | source)
XLA Modules:
  0.0 455.4 jit_solution(859119580009614505)
XLA Ops:
  1.9 7.6 %all-to-all-start.1 = ((bf16[8,128,128]{2,1,0:T(8,128)(2,1)}), bf16[8,128,128]{2,1,0:T(8,128)(2,1)S(1)}, u32[]{:S(2)}, u32[]{:S(2)}) async-start(bf16[8,128,128]{2,1,0:T(8,128)(2,1)} %broadcast_in_dim.76), calls=%async_computation.1 | async-start | bytes 524288 | tf_op jit(solution)/shard_map/all_to_all | solution.py:23
  19.0 5.1 %all-to-all-start = ((bf16[4,128,2048]{2,1,0:T(8,128)(2,1)}), bf16[4,128,2048]{2,1,0:T(8,128)(2,1)S(1)}, u32[]{:S(2)}, u32[]{:S(2)}) async-start(bf16[4,128,2048]{2,1,0:T(8,128)(2,1)} %maximum_maximum_fusion), calls=%async_computation | async-start | bytes 4194304 | tf_op jit(solution)/shard_map/all_to_all | solution.py:60
  24.7 4.5 collective-permute-start.1
  29.2 3.9 collective-permute-start
  34.7 13.1 %all-to-all-done = bf16[4,128,2048]{2,1,0:T(8,128)(2,1)S(1)} async-done(((bf16[4,128,2048]{2,1,0:T(8,128)(2,1)}), bf16[4,128,2048]{2,1,0:T(8,128)(2,1)S(1)}, u32[]{:S(2)}, u32[]{:S(2)}) %all-to-all-start) | async-done | bytes 2097184 | tf_op jit(solution)/shard_map/all_to_all | solution.py:60
  48.6 7.2 %all_to_all.160 = bf16[4,128,128]{2,1,0:T(8,128)(2,1)S(1)} all-to-all(bf16[4,128,128]{2,1,0:T(8,128)(2,1)S(1)} %fusion), channel_id=1, replica_groups=mesh['sub_0'=8,'sub_1'=2,'blk_0'=4,'blk_1'=8] {'blk_0'}, dimensions={0} | all-to-all | bytes 262144 | tf_op jit(solution)/shard_map/all_to_all | solution.py:122
  56.5 3.9 all-to-all-start.3
  60.6 9.2 %all-to-all-done.3 = bf16[8,128,128]{2,1,0:T(8,128)(2,1)S(1)} async-done(((bf16[8,128,128]{2,1,0:T(8,128)(2,1)}), bf16[8,128,128]{2,1,0:T(8,128)(2,1)S(1)}, u32[]{:S(2)}, u32[]{:S(2)}) %all-to-all-start.3) | async-done | bytes 262176 | tf_op jit(solution)/shard_map/all_to_all | solution.py:23
  74.9 4.7 %all-to-all-done.4 = bf16[4,128,128]{2,1,0:T(8,128)(2,1)S(1)} async-done(((bf16[4,128,128]{2,1,0:T(8,128)(2,1)}), bf16[4,128,128]{2,1,0:T(8,128)(2,1)S(1)}, u32[]{:S(2)}, u32[]{:S(2)}) %all-to-all-start.4) | async-done | bytes 131104 | tf_op jit(solution)/shard_map/all_to_all | solution.py:122
  80.0 11.7 %all_to_all.161 = bf16[8,128,128]{2,1,0:T(8,128)(2,1)S(1)} all-to-all(bf16[8,128,128]{2,1,0:T(8,128)(2,1)S(1)} %broadcast_in_dim.80), channel_id=1, replica_groups=mesh['sub_0'=8,'sub_1'=2,'blk_0'=4,'blk_1'=8] {'blk_1'}, dimensions={0} | all-to-all | bytes 524288 | tf_op jit(solution)/shard_map/all_to_all | solution.py:23
  92.3 9.4 %collective-permute-start.3 = (bf16[2,128,128]{1,2,0:T(8,128)(2,1)S(1)}, bf16[2,128,128]{1,2,0:T(8,128)(2,1)S(1)}, u32[]{:S(2)}, u32[]{:S(2)}) collective-permute-start(bf16[2,128,128]{1,2,0:T(8,128)(2,1)S(1)} %get-tuple-element.336), channel_id=1, source_target_pairs={{32,0},{64,32},{96,64},{128,96},{160,128},{192,160},{224,192},{256... | collective-permute-start | bytes 196616 | tf_op jit(solution)/shard_map/ppermute | solution.py:18
  101.7 3.9 collective-permute-start.2
  106.3 9.5 %all-to-all-start.6 = ((f32[16,1,192]{2,1,0:T(1,128)}), f32[16,1,192]{2,1,0:T(1,128)S(1)}, u32[]{:S(2)}, u32[]{:S(2)}) async-start(f32[16,1,192]{2,1,0:T(1,128)} %reshape.777), calls=%async_computation.6 | async-start | bytes 32768 | tf_op jit(solution)/shard_map/all_to_all | solution.py:23
  116.1 7.1 %all-to-all-done.6 = f32[16,1,192]{2,1,0:T(1,128)S(1)} async-done(((f32[16,1,192]{2,1,0:T(1,128)}), f32[16,1,192]{2,1,0:T(1,128)S(1)}, u32[]{:S(2)}, u32[]{:S(2)}) %all-to-all-start.6) | async-done | bytes 12320 | tf_op jit(solution)/shard_map/all_to_all | solution.py:23
  126.5 7.2 %all_to_all.162 = bf16[4,128,128]{2,1,0:T(8,128)(2,1)S(1)} all-to-all(bf16[4,128,128]{2,1,0:T(8,128)(2,1)S(1)} %fusion.1), channel_id=1, replica_groups=mesh['sub_0'=8,'sub_1'=2,'blk_0'=4,'blk_1'=8] {'blk_0'}, dimensions={0} | all-to-all | bytes 262144 | tf_op jit(solution)/shard_map/all_to_all | solution.py:122
  133.8 12.9 %all_to_all.163 = bf16[8,144,128]{2,1,0:T(8,128)(2,1)S(1)} all-to-all(bf16[8,144,128]{2,1,0:T(8,128)(2,1)S(1)} %broadcast_in_dim.82), channel_id=1, replica_groups=mesh['sub_0'=8,'sub_1'=2,'blk_0'=4,'blk_1'=8] {'blk_1'}, dimensions={0} | all-to-all | bytes 589824 | tf_op jit(solution)/shard_map/all_to_all | solution.py:23
  147.9 7.3 %all_to_all.164 = bf16[4,144,128]{2,1,0:T(8,128)(2,1)S(1)} all-to-all(bf16[4,144,128]{2,1,0:T(8,128)(2,1)S(1)} %pad_maximum_fusion.12), channel_id=1, replica_groups=mesh['sub_0'=8,'sub_1'=2,'blk_0'=4,'blk_1'=8] {'blk_0'}, dimensions={0} | all-to-all | bytes 294912 | tf_op jit(solution)/shard_map/all_to_all | solution.py:122
  156.4 12.4 %all_to_all.165 = bf16[8,128,128]{2,1,0:T(8,128)(2,1)S(1)} all-to-all(bf16[8,128,128]{2,1,0:T(8,128)(2,1)S(1)} %broadcast_in_dim.84), channel_id=1, replica_groups=mesh['sub_0'=8,'sub_1'=2,'blk_0'=4,'blk_1'=8] {'blk_1'}, dimensions={0} | all-to-all | bytes 524288 | tf_op jit(solution)/shard_map/all_to_all | solution.py:23
  169.3 6.6 %collective-permute-start.5 = (bf16[2,128,128]{1,2,0:T(8,128)(2,1)S(1)}, bf16[2,128,128]{1,2,0:T(8,128)(2,1)S(1)}, u32[]{:S(2)}, u32[]{:S(2)}) collective-permute-start(bf16[2,128,128]{1,2,0:T(8,128)(2,1)S(1)} %get-tuple-element.330), channel_id=1, source_target_pairs={{32,0},{64,32},{96,64},{128,96},{160,128},{192,160},{224,192},{256... | collective-permute-start | bytes 196616 | tf_op jit(solution)/shard_map/ppermute | solution.py:18
  178.7 3.6 all-to-all-start.11
  182.6 6.8 %all-to-all-done.11 = f32[16,1,128]{2,1,0:T(1,128)S(1)} async-done(((f32[16,1,128]{2,1,0:T(1,128)}), f32[16,1,128]{2,1,0:T(1,128)S(1)}, u32[]{:S(2)}, u32[]{:S(2)}) %all-to-all-start.11) | async-done | bytes 8224 | tf_op jit(solution)/shard_map/all_to_all | solution.py:23
  192.7 7.2 %all_to_all.166 = bf16[4,128,128]{2,1,0:T(8,128)(2,1)S(1)} all-to-all(bf16[4,128,128]{2,1,0:T(8,128)(2,1)S(1)} %fusion.2), channel_id=1, replica_groups=mesh['sub_0'=8,'sub_1'=2,'blk_0'=4,'blk_1'=8] {'blk_0'}, dimensions={0} | all-to-all | bytes 262144 | tf_op jit(solution)/shard_map/all_to_all | solution.py:122
  200.0 12.7 %all_to_all.167 = bf16[8,144,128]{2,1,0:T(8,128)(2,1)S(1)} all-to-all(bf16[8,144,128]{2,1,0:T(8,128)(2,1)S(1)} %broadcast_in_dim.86), channel_id=1, replica_groups=mesh['sub_0'=8,'sub_1'=2,'blk_0'=4,'blk_1'=8] {'blk_1'}, dimensions={0} | all-to-all | bytes 589824 | tf_op jit(solution)/shard_map/all_to_all | solution.py:23
  213.9 7.3 %all_to_all.168 = bf16[4,144,128]{2,1,0:T(8,128)(2,1)S(1)} all-to-all(bf16[4,144,128]{2,1,0:T(8,128)(2,1)S(1)} %pad_maximum_fusion.13), channel_id=1, replica_groups=mesh['sub_0'=8,'sub_1'=2,'blk_0'=4,'blk_1'=8] {'blk_0'}, dimensions={0} | all-to-all | bytes 294912 | tf_op jit(solution)/shard_map/all_to_all | solution.py:122
  222.8 12.4 %all_to_all.169 = bf16[8,128,128]{2,1,0:T(8,128)(2,1)S(1)} all-to-all(bf16[8,128,128]{2,1,0:T(8,128)(2,1)S(1)} %broadcast_in_dim.91), channel_id=1, replica_groups=mesh['sub_0'=8,'sub_1'=2,'blk_0'=4,'blk_1'=8] {'blk_1'}, dimensions={0} | all-to-all | bytes 524288 | tf_op jit(solution)/shard_map/all_to_all | solution.py:23
  235.8 6.8 %collective-permute-start.7 = (bf16[2,128,128]{1,2,0:T(8,128)(2,1)S(1)}, bf16[2,128,128]{1,2,0:T(8,128)(2,1)S(1)}, u32[]{:S(2)}, u32[]{:S(2)}) collective-permute-start(bf16[2,128,128]{1,2,0:T(8,128)(2,1)S(1)} %get-tuple-element.328), channel_id=1, source_target_pairs={{32,0},{64,32},{96,64},{128,96},{160,128},{192,160},{224,192},{256... | collective-permute-start | bytes 196616 | tf_op jit(solution)/shard_map/ppermute | solution.py:18
  245.4 3.6 all-to-all-start.16
  249.2 7.2 %all-to-all-done.16 = f32[16,1,192]{2,1,0:T(1,128)S(1)} async-done(((f32[16,1,192]{2,1,0:T(1,128)}), f32[16,1,192]{2,1,0:T(1,128)S(1)}, u32[]{:S(2)}, u32[]{:S(2)}) %all-to-all-start.16) | async-done | bytes 12320 | tf_op jit(solution)/shard_map/all_to_all | solution.py:23
  258.3 7.2 %all_to_all.170 = bf16[4,128,128]{2,1,0:T(8,128)(2,1)S(1)} all-to-all(bf16[4,128,128]{2,1,0:T(8,128)(2,1)S(1)} %fusion.3), channel_id=1, replica_groups=mesh['sub_0'=8,'sub_1'=2,'blk_0'=4,'blk_1'=8] {'blk_0'}, dimensions={0} | all-to-all | bytes 262144 | tf_op jit(solution)/shard_map/all_to_all | solution.py:122
  265.6 12.9 %all_to_all.171 = bf16[8,144,128]{2,1,0:T(8,128)(2,1)S(1)} all-to-all(bf16[8,144,128]{2,1,0:T(8,128)(2,1)S(1)} %broadcast_in_dim.93), channel_id=1, replica_groups=mesh['sub_0'=8,'sub_1'=2,'blk_0'=4,'blk_1'=8] {'blk_1'}, dimensions={0} | all-to-all | bytes 589824 | tf_op jit(solution)/shard_map/all_to_all | solution.py:23
  279.8 7.3 %all_to_all.172 = bf16[4,144,128]{2,1,0:T(8,128)(2,1)S(1)} all-to-all(bf16[4,144,128]{2,1,0:T(8,128)(2,1)S(1)} %pad_maximum_fusion.14), channel_id=1, replica_groups=mesh['sub_0'=8,'sub_1'=2,'blk_0'=4,'blk_1'=8] {'blk_0'}, dimensions={0} | all-to-all | bytes 294912 | tf_op jit(solution)/shard_map/all_to_all | solution.py:122
  288.8 12.4 %all_to_all.173 = bf16[8,128,128]{2,1,0:T(8,128)(2,1)S(1)} all-to-all(bf16[8,128,128]{2,1,0:T(8,128)(2,1)S(1)} %broadcast_in_dim.96), channel_id=1, replica_groups=mesh['sub_0'=8,'sub_1'=2,'blk_0'=4,'blk_1'=8] {'blk_1'}, dimensions={0} | all-to-all | bytes 524288 | tf_op jit(solution)/shard_map/all_to_all | solution.py:23
  301.8 6.6 %collective-permute-start.9 = (bf16[2,128,128]{1,2,0:T(8,128)(2,1)S(1)}, bf16[2,128,128]{1,2,0:T(8,128)(2,1)S(1)}, u32[]{:S(2)}, u32[]{:S(2)}) collective-permute-start(bf16[2,128,128]{1,2,0:T(8,128)(2,1)S(1)} %get-tuple-element.326), channel_id=1, source_target_pairs={{32,0},{64,32},{96,64},{128,96},{160,128},{192,160},{224,192},{256... | collective-permute-start | bytes 196616 | tf_op jit(solution)/shard_map/ppermute | solution.py:18
  311.2 3.6 all-to-all-start.21
  315.0 7.2 %all-to-all-done.21 = f32[16,1,256]{2,1,0:T(1,128)S(1)} async-done(((f32[16,1,256]{2,1,0:T(1,128)}), f32[16,1,256]{2,1,0:T(1,128)S(1)}, u32[]{:S(2)}, u32[]{:S(2)}) %all-to-all-start.21) | async-done | bytes 16416 | tf_op jit(solution)/shard_map/all_to_all | solution.py:23
  325.6 7.2 %all_to_all.174 = bf16[4,128,128]{2,1,0:T(8,128)(2,1)S(1)} all-to-all(bf16[4,128,128]{2,1,0:T(8,128)(2,1)S(1)} %fusion.4), channel_id=1, replica_groups=mesh['sub_0'=8,'sub_1'=2,'blk_0'=4,'blk_1'=8] {'blk_0'}, dimensions={0} | all-to-all | bytes 262144 | tf_op jit(solution)/shard_map/all_to_all | solution.py:122
  332.9 12.9 %all_to_all.175 = bf16[8,144,128]{2,1,0:T(8,128)(2,1)S(1)} all-to-all(bf16[8,144,128]{2,1,0:T(8,128)(2,1)S(1)} %broadcast_in_dim.98), channel_id=1, replica_groups=mesh['sub_0'=8,'sub_1'=2,'blk_0'=4,'blk_1'=8] {'blk_1'}, dimensions={0} | all-to-all | bytes 589824 | tf_op jit(solution)/shard_map/all_to_all | solution.py:23
  347.1 7.3 %all_to_all.176 = bf16[4,144,128]{2,1,0:T(8,128)(2,1)S(1)} all-to-all(bf16[4,144,128]{2,1,0:T(8,128)(2,1)S(1)} %pad_maximum_fusion.15), channel_id=1, replica_groups=mesh['sub_0'=8,'sub_1'=2,'blk_0'=4,'blk_1'=8] {'blk_0'}, dimensions={0} | all-to-all | bytes 294912 | tf_op jit(solution)/shard_map/all_to_all | solution.py:122
  356.6 12.4 %all_to_all.177 = bf16[8,128,128]{2,1,0:T(8,128)(2,1)S(1)} all-to-all(bf16[8,128,128]{2,1,0:T(8,128)(2,1)S(1)} %broadcast_in_dim.102), channel_id=1, replica_groups=mesh['sub_0'=8,'sub_1'=2,'blk_0'=4,'blk_1'=8] {'blk_1'}, dimensions={0} | all-to-all | bytes 524288 | tf_op jit(solution)/shard_map/all_to_all | solution.py:23
  369.6 6.6 %collective-permute-start.11 = (bf16[2,128,128]{1,2,0:T(8,128)(2,1)S(1)}, bf16[2,128,128]{1,2,0:T(8,128)(2,1)S(1)}, u32[]{:S(2)}, u32[]{:S(2)}) collective-permute-start(bf16[2,128,128]{1,2,0:T(8,128)(2,1)S(1)} %get-tuple-element.324), channel_id=1, source_target_pairs={{32,0},{64,32},{96,64},{128,96},{160,128},{192,160},{224,192},{256... | collective-permute-start | bytes 196616 | tf_op jit(solution)/shard_map/ppermute | solution.py:18
  379.0 4.2 all-to-all-start.26
  383.4 7.3 %all-to-all-done.26 = f32[16,1,320]{2,1,0:T(1,128)S(1)} async-done(((f32[16,1,320]{2,1,0:T(1,128)}), f32[16,1,320]{2,1,0:T(1,128)S(1)}, u32[]{:S(2)}, u32[]{:S(2)}) %all-to-all-start.26) | async-done | bytes 20512 | tf_op jit(solution)/shard_map/all_to_all | solution.py:23
  394.1 7.2 %all_to_all.178 = bf16[4,128,128]{2,1,0:T(8,128)(2,1)S(1)} all-to-all(bf16[4,128,128]{2,1,0:T(8,128)(2,1)S(1)} %fusion.5), channel_id=1, replica_groups=mesh['sub_0'=8,'sub_1'=2,'blk_0'=4,'blk_1'=8] {'blk_0'}, dimensions={0} | all-to-all | bytes 262144 | tf_op jit(solution)/shard_map/all_to_all | solution.py:122
  401.4 12.9 %all_to_all.179 = bf16[8,144,128]{2,1,0:T(8,128)(2,1)S(1)} all-to-all(bf16[8,144,128]{2,1,0:T(8,128)(2,1)S(1)} %broadcast_in_dim.104), channel_id=1, replica_groups=mesh['sub_0'=8,'sub_1'=2,'blk_0'=4,'blk_1'=8] {'blk_1'}, dimensions={0} | all-to-all | bytes 589824 | tf_op jit(solution)/shard_map/all_to_all | solution.py:23
  415.7 7.3 %all_to_all.180 = bf16[4,144,128]{2,1,0:T(8,128)(2,1)S(1)} all-to-all(bf16[4,144,128]{2,1,0:T(8,128)(2,1)S(1)} %pad_maximum_fusion.16), channel_id=1, replica_groups=mesh['sub_0'=8,'sub_1'=2,'blk_0'=4,'blk_1'=8] {'blk_0'}, dimensions={0} | all-to-all | bytes 294912 | tf_op jit(solution)/shard_map/all_to_all | solution.py:122
  424.8 14.1 %all_to_all.181 = f32[16,1,384]{2,1,0:T(1,128)S(1)} all-to-all(f32[16,1,384]{2,1,0:T(1,128)S(1)} %reshape.787), channel_id=1, replica_groups=mesh['sub_0'=8,'sub_1'=2,'blk_0'=4,'blk_1'=8] {'sub_0','sub_1'}, dimensions={0} | all-to-all | bytes 49152 | tf_op jit(solution)/shard_map/all_to_all | solution.py:23
  440.4 3.9 all-to-all-start.31
  444.4 8.7 %all-to-all-done.31 = f32[32,1,384]{2,1,0:T(1,128)S(1)} async-done(((f32[32,1,384]{2,1,0:T(1,128)}), f32[32,1,384]{2,1,0:T(1,128)S(1)}, u32[]{:S(2)}, u32[]{:S(2)}) %all-to-all-start.31) | async-done | bytes 49184 | tf_op jit(solution)/shard_map/all_to_all | solution.py:23
  (592 shorter events, 69.0 us)
Async XLA Ops:
  1.0 59.4 %copy-start.5 = (f32[2,64,64]{2,1,0:T(8,128)}, f32[2,64,64]{2,1,0:T(8,128)S(1)}, u32[]{:S(2)}) copy-start(f32[2,64,64]{2,1,0:T(8,128)S(1)} %get-tuple-element.337) | copy-start | bytes 98308
  1.0 59.4 %copy-start.7 = (f32[2,64,64]{2,1,0:T(8,128)}, f32[2,64,64]{2,1,0:T(8,128)S(1)}, u32[]{:S(2)}) copy-start(f32[2,64,64]{2,1,0:T(8,128)S(1)} %get-tuple-element.338) | copy-start | bytes 98308
  1.9 17.1 %all-to-all-start.1 = ((bf16[8,128,128]{2,1,0:T(8,128)(2,1)}), bf16[8,128,128]{2,1,0:T(8,128)(2,1)S(1)}, u32[]{:S(2)}, u32[]{:S(2)}) async-start(bf16[8,128,128]{2,1,0:T(8,128)(2,1)} %broadcast_in_dim.76), calls=%async_computation.1 | async-start | bytes 524288 | tf_op jit(solution)/shard_map/all_to_all | solution.py:23
  19.0 28.9 %all-to-all-start = ((bf16[4,128,2048]{2,1,0:T(8,128)(2,1)}), bf16[4,128,2048]{2,1,0:T(8,128)(2,1)S(1)}, u32[]{:S(2)}, u32[]{:S(2)}) async-start(bf16[4,128,2048]{2,1,0:T(8,128)(2,1)} %maximum_maximum_fusion), calls=%async_computation | async-start | bytes 4194304 | tf_op jit(solution)/shard_map/all_to_all | solution.py:60
  24.2 67.5 %copy-start.81 = (s32[256]{0:T(256)}, s32[256]{0:T(256)S(1)}, u32[]{:S(2)}) copy-start(s32[256]{0:T(256)S(1)} %pad_add_fusion) | copy-start | bytes 3076
  24.2 211.0 %copy-start.67 = (s32[512]{0:T(512)}, s32[512]{0:T(512)S(1)}, u32[]{:S(2)}) copy-start(s32[512]{0:T(512)S(1)} %iota_add_fusion.1) | copy-start | bytes 6148
  24.7 8.8 %collective-permute-start.1 = (bf16[2,128,128]{1,2,0:T(8,128)(2,1)S(1)}, bf16[2,128,128]{1,2,0:T(8,128)(2,1)S(1)}, u32[]{:S(2)}, u32[]{:S(2)}) collective-permute-start(bf16[2,128,128]{1,2,0:T(8,128)(2,1)S(1)} %get-tuple-element.342), channel_id=1, source_target_pairs={{32,0},{64,32},{96,64},{128,96},{160,128},{192,160},{224,192},{256... | collective-permute-start | bytes 196616 | tf_op jit(solution)/shard_map/ppermute | solution.py:18
  29.2 5.2 %collective-permute-start = (bf16[2,128,128]{1,2,0:T(8,128)(2,1)S(1)}, bf16[2,128,128]{1,2,0:T(8,128)(2,1)S(1)}, u32[]{:S(2)}, u32[]{:S(2)}) collective-permute-start(bf16[2,128,128]{1,2,0:T(8,128)(2,1)S(1)} %get-tuple-element.341), channel_id=1, source_target_pairs={{0,32},{32,64},{64,96},{96,128},{128,160},{160,192},{192,224},{224... | collective-permute-start | bytes 196616 | tf_op jit(solution)/shard_map/ppermute | solution.py:18
  56.5 13.2 %all-to-all-start.3 = ((bf16[8,128,128]{2,1,0:T(8,128)(2,1)}), bf16[8,128,128]{2,1,0:T(8,128)(2,1)S(1)}, u32[]{:S(2)}, u32[]{:S(2)}) async-start(bf16[8,128,128]{2,1,0:T(8,128)(2,1)} %broadcast_in_dim.79), calls=%async_computation.3 | async-start | bytes 524288 | tf_op jit(solution)/shard_map/all_to_all | solution.py:23
  71.5 8.1 %all-to-all-start.4 = ((bf16[4,128,128]{2,1,0:T(8,128)(2,1)}), bf16[4,128,128]{2,1,0:T(8,128)(2,1)S(1)}, u32[]{:S(2)}, u32[]{:S(2)}) async-start(bf16[4,128,128]{2,1,0:T(8,128)(2,1)} %convolution_convert_fusion.10), calls=%async_computation.4 | async-start | bytes 262144 | tf_op jit(solution)/shard_map/all_to_all | solution.py:122
  92.3 32.3 %collective-permute-start.3 = (bf16[2,128,128]{1,2,0:T(8,128)(2,1)S(1)}, bf16[2,128,128]{1,2,0:T(8,128)(2,1)S(1)}, u32[]{:S(2)}, u32[]{:S(2)}) collective-permute-start(bf16[2,128,128]{1,2,0:T(8,128)(2,1)S(1)} %get-tuple-element.336), channel_id=1, source_target_pairs={{32,0},{64,32},{96,64},{128,96},{160,128},{192,160},{224,192},{256... | collective-permute-start | bytes 196616 | tf_op jit(solution)/shard_map/ppermute | solution.py:18
  101.7 22.9 %collective-permute-start.2 = (bf16[2,128,128]{1,2,0:T(8,128)(2,1)S(1)}, bf16[2,128,128]{1,2,0:T(8,128)(2,1)}, u32[]{:S(2)}, u32[]{:S(2)}) collective-permute-start(bf16[2,128,128]{1,2,0:T(8,128)(2,1)S(1)} %get-tuple-element.335), channel_id=1, source_target_pairs={{0,32},{32,64},{64,96},{96,128},{128,160},{160,192},{192,224},{224... | collective-permute-start | bytes 196616 | tf_op jit(solution)/shard_map/ppermute | solution.py:18
  106.3 16.9 %all-to-all-start.6 = ((f32[16,1,192]{2,1,0:T(1,128)}), f32[16,1,192]{2,1,0:T(1,128)S(1)}, u32[]{:S(2)}, u32[]{:S(2)}) async-start(f32[16,1,192]{2,1,0:T(1,128)} %reshape.777), calls=%async_computation.6 | async-start | bytes 32768 | tf_op jit(solution)/shard_map/all_to_all | solution.py:23
  147.8 21.0 %copy-start.82 = (s32[256]{0:T(256)S(1)}, s32[256]{0:T(256)}, u32[]{:S(2)}) copy-start(s32[256]{0:T(256)} %copy-done.81) | copy-start | bytes 3076
  156.0 132.0 %copy-start.25 = (f32[128]{0:T(128)}, f32[128]{0:T(128)S(1)}, u32[]{:S(2)}) copy-start(f32[128]{0:T(128)S(1)} %pad_maximum_fusion.39) | copy-start | bytes 1540
  169.3 20.9 %collective-permute-start.5 = (bf16[2,128,128]{1,2,0:T(8,128)(2,1)S(1)}, bf16[2,128,128]{1,2,0:T(8,128)(2,1)S(1)}, u32[]{:S(2)}, u32[]{:S(2)}) collective-permute-start(bf16[2,128,128]{1,2,0:T(8,128)(2,1)S(1)} %get-tuple-element.330), channel_id=1, source_target_pairs={{32,0},{64,32},{96,64},{128,96},{160,128},{192,160},{224,192},{256... | collective-permute-start | bytes 196616 | tf_op jit(solution)/shard_map/ppermute | solution.py:18
  176.0 14.3 %collective-permute-start.4 = (bf16[2,128,128]{1,2,0:T(8,128)(2,1)S(1)}, bf16[2,128,128]{1,2,0:T(8,128)(2,1)S(1)}, u32[]{:S(2)}, u32[]{:S(2)}) collective-permute-start(bf16[2,128,128]{1,2,0:T(8,128)(2,1)S(1)} %get-tuple-element.329), channel_id=1, source_target_pairs={{0,32},{32,64},{64,96},{96,128},{128,160},{160,192},{192,224},{224... | collective-permute-start | bytes 196616 | tf_op jit(solution)/shard_map/ppermute | solution.py:18
  178.7 10.6 %all-to-all-start.11 = ((f32[16,1,128]{2,1,0:T(1,128)}), f32[16,1,128]{2,1,0:T(1,128)S(1)}, u32[]{:S(2)}, u32[]{:S(2)}) async-start(f32[16,1,128]{2,1,0:T(1,128)} %reshape.779), calls=%async_computation.11 | async-start | bytes 16384 | tf_op jit(solution)/shard_map/all_to_all | solution.py:23
  213.9 21.4 %copy-start.83 = (s32[256]{0:T(256)S(1)}, s32[256]{0:T(256)}, u32[]{:S(2)}) copy-start(s32[256]{0:T(256)} %copy-done.81) | copy-start | bytes 3076
  235.8 21.4 %collective-permute-start.7 = (bf16[2,128,128]{1,2,0:T(8,128)(2,1)S(1)}, bf16[2,128,128]{1,2,0:T(8,128)(2,1)S(1)}, u32[]{:S(2)}, u32[]{:S(2)}) collective-permute-start(bf16[2,128,128]{1,2,0:T(8,128)(2,1)S(1)} %get-tuple-element.328), channel_id=1, source_target_pairs={{32,0},{64,32},{96,64},{128,96},{160,128},{192,160},{224,192},{256... | collective-permute-start | bytes 196616 | tf_op jit(solution)/shard_map/ppermute | solution.py:18
  242.6 14.7 %collective-permute-start.6 = (bf16[2,128,128]{1,2,0:T(8,128)(2,1)S(1)}, bf16[2,128,128]{1,2,0:T(8,128)(2,1)S(1)}, u32[]{:S(2)}, u32[]{:S(2)}) collective-permute-start(bf16[2,128,128]{1,2,0:T(8,128)(2,1)S(1)} %get-tuple-element.327), channel_id=1, source_target_pairs={{0,32},{32,64},{64,96},{96,128},{128,160},{160,192},{192,224},{224... | collective-permute-start | bytes 196616 | tf_op jit(solution)/shard_map/ppermute | solution.py:18
  245.4 11.0 %all-to-all-start.16 = ((f32[16,1,192]{2,1,0:T(1,128)}), f32[16,1,192]{2,1,0:T(1,128)S(1)}, u32[]{:S(2)}, u32[]{:S(2)}) async-start(f32[16,1,192]{2,1,0:T(1,128)} %reshape.781), calls=%async_computation.16 | async-start | bytes 32768 | tf_op jit(solution)/shard_map/all_to_all | solution.py:23
  279.7 21.4 %copy-start.68 = (s32[512]{0:T(512)S(1)}, s32[512]{0:T(512)}, u32[]{:S(2)}) copy-start(s32[512]{0:T(512)} %copy-done.67) | copy-start | bytes 6148
  279.8 21.4 %copy-start.84 = (s32[256]{0:T(256)S(1)}, s32[256]{0:T(256)}, u32[]{:S(2)}) copy-start(s32[256]{0:T(256)} %copy-done.81) | copy-start | bytes 3076
  301.6 23.2 %copy-start.23 = (f32[2]{0:T(128)S(1)}, f32[2]{0:T(128)}, u32[]{:S(2)}) copy-start(f32[2]{0:T(128)} %constant.80.clone) | copy-start | bytes 28
  301.8 21.3 %collective-permute-start.9 = (bf16[2,128,128]{1,2,0:T(8,128)(2,1)S(1)}, bf16[2,128,128]{1,2,0:T(8,128)(2,1)S(1)}, u32[]{:S(2)}, u32[]{:S(2)}) collective-permute-start(bf16[2,128,128]{1,2,0:T(8,128)(2,1)S(1)} %get-tuple-element.326), channel_id=1, source_target_pairs={{32,0},{64,32},{96,64},{128,96},{160,128},{192,160},{224,192},{256... | collective-permute-start | bytes 196616 | tf_op jit(solution)/shard_map/ppermute | solution.py:18
  308.4 14.7 %collective-permute-start.8 = (bf16[2,128,128]{1,2,0:T(8,128)(2,1)S(1)}, bf16[2,128,128]{1,2,0:T(8,128)(2,1)S(1)}, u32[]{:S(2)}, u32[]{:S(2)}) collective-permute-start(bf16[2,128,128]{1,2,0:T(8,128)(2,1)S(1)} %get-tuple-element.325), channel_id=1, source_target_pairs={{0,32},{32,64},{64,96},{96,128},{128,160},{160,192},{192,224},{224... | collective-permute-start | bytes 196616 | tf_op jit(solution)/shard_map/ppermute | solution.py:18
  311.2 11.0 %all-to-all-start.21 = ((f32[16,1,256]{2,1,0:T(1,128)}), f32[16,1,256]{2,1,0:T(1,128)S(1)}, u32[]{:S(2)}, u32[]{:S(2)}) async-start(f32[16,1,256]{2,1,0:T(1,128)} %reshape.783), calls=%async_computation.21 | async-start | bytes 32768 | tf_op jit(solution)/shard_map/all_to_all | solution.py:23
  347.1 21.9 %copy-start.69 = (s32[512]{0:T(512)S(1)}, s32[512]{0:T(512)}, u32[]{:S(2)}) copy-start(s32[512]{0:T(512)} %copy-done.67) | copy-start | bytes 6148
  347.1 21.9 %copy-start.85 = (s32[256]{0:T(256)S(1)}, s32[256]{0:T(256)}, u32[]{:S(2)}) copy-start(s32[256]{0:T(256)} %copy-done.81) | copy-start | bytes 3076
  354.6 15.0 %copy-start.34 = (f32[64]{0:T(128)}, f32[64]{0:T(128)S(1)}, u32[]{:S(2)}) copy-start(f32[64]{0:T(128)S(1)} %get-tuple-element.220) | copy-start | bytes 772
  354.6 15.0 %copy-start.48 = (f32[64]{0:T(128)}, f32[64]{0:T(128)S(1)}, u32[]{:S(2)}) copy-start(f32[64]{0:T(128)S(1)} %get-tuple-element.218) | copy-start | bytes 772
  369.4 23.8 %copy-start.24 = (f32[2]{0:T(128)S(1)}, f32[2]{0:T(128)}, u32[]{:S(2)}) copy-start(f32[2]{0:T(128)} %constant.80.clone) | copy-start | bytes 28
  369.6 22.6 %collective-permute-start.11 = (bf16[2,128,128]{1,2,0:T(8,128)(2,1)S(1)}, bf16[2,128,128]{1,2,0:T(8,128)(2,1)S(1)}, u32[]{:S(2)}, u32[]{:S(2)}) collective-permute-start(bf16[2,128,128]{1,2,0:T(8,128)(2,1)S(1)} %get-tuple-element.324), channel_id=1, source_target_pairs={{32,0},{64,32},{96,64},{128,96},{160,128},{192,160},{224,192},{256... | collective-permute-start | bytes 196616 | tf_op jit(solution)/shard_map/ppermute | solution.py:18
  376.2 16.0 %collective-permute-start.10 = (bf16[2,128,128]{1,2,0:T(8,128)(2,1)S(1)}, bf16[2,128,128]{1,2,0:T(8,128)(2,1)}, u32[]{:S(2)}, u32[]{:S(2)}) collective-permute-start(bf16[2,128,128]{1,2,0:T(8,128)(2,1)S(1)} %get-tuple-element.323), channel_id=1, source_target_pairs={{0,32},{32,64},{64,96},{96,128},{128,160},{160,192},{192,224},{224... | collective-permute-start | bytes 196616 | tf_op jit(solution)/shard_map/ppermute | solution.py:18
  379.0 11.7 %all-to-all-start.26 = ((f32[16,1,320]{2,1,0:T(1,128)}), f32[16,1,320]{2,1,0:T(1,128)S(1)}, u32[]{:S(2)}, u32[]{:S(2)}) async-start(f32[16,1,320]{2,1,0:T(1,128)} %reshape.785), calls=%async_computation.26 | async-start | bytes 49152 | tf_op jit(solution)/shard_map/all_to_all | solution.py:23
  415.6 28.7 %copy-start.30 = (f32[64]{0:T(128)S(1)}, f32[64]{0:T(128)}, u32[]{:S(2)}) copy-start(f32[64]{0:T(128)} %copy-done.28) | copy-start | bytes 772
  415.6 28.7 %copy-start.33 = (f32[64]{0:T(128)S(1)}, f32[64]{0:T(128)}, u32[]{:S(2)}) copy-start(f32[64]{0:T(128)} %copy-done.31) | copy-start | bytes 772
  415.6 28.7 %copy-start.45 = (f32[64]{0:T(128)S(1)}, f32[64]{0:T(128)}, u32[]{:S(2)}) copy-start(f32[64]{0:T(128)} %copy-done.44) | copy-start | bytes 772
  415.6 28.7 %copy-start.47 = (f32[64]{0:T(128)S(1)}, f32[64]{0:T(128)}, u32[]{:S(2)}) copy-start(f32[64]{0:T(128)} %copy-done.46) | copy-start | bytes 772
  415.6 28.7 %copy-start.49 = (f32[64]{0:T(128)S(1)}, f32[64]{0:T(128)}, u32[]{:S(2)}) copy-start(f32[64]{0:T(128)} %copy-done.48) | copy-start | bytes 772
  415.6 28.7 %copy-start.51 = (f32[64]{0:T(128)S(1)}, f32[64]{0:T(128)}, u32[]{:S(2)}) copy-start(f32[64]{0:T(128)} %copy-done.50) | copy-start | bytes 772
  415.6 28.7 %copy-start.62 = (f32[64]{0:T(128)S(1)}, f32[64]{0:T(128)}, u32[]{:S(2)}) copy-start(f32[64]{0:T(128)} %copy-done.61) | copy-start | bytes 772
  415.7 28.7 %copy-start.64 = (f32[64]{0:T(128)S(1)}, f32[64]{0:T(128)}, u32[]{:S(2)}) copy-start(f32[64]{0:T(128)} %copy-done.63) | copy-start | bytes 772
  415.7 28.7 %copy-start.66 = (f32[64]{0:T(128)S(1)}, f32[64]{0:T(128)}, u32[]{:S(2)}) copy-start(f32[64]{0:T(128)} %copy-done.65) | copy-start | bytes 772
  415.7 38.8 %copy-start.6 = (f32[2,64,64]{2,1,0:T(8,128)S(1)}, f32[2,64,64]{2,1,0:T(8,128)}, u32[]{:S(2)}) copy-start(f32[2,64,64]{2,1,0:T(8,128)} %copy-done.5) | copy-start | bytes 98308
  415.7 38.8 %copy-start.8 = (f32[2,64,64]{2,1,0:T(8,128)S(1)}, f32[2,64,64]{2,1,0:T(8,128)}, u32[]{:S(2)}) copy-start(f32[2,64,64]{2,1,0:T(8,128)} %copy-done.7) | copy-start | bytes 98308
  440.4 12.7 %all-to-all-start.31 = ((f32[32,1,384]{2,1,0:T(1,128)}), f32[32,1,384]{2,1,0:T(1,128)S(1)}, u32[]{:S(2)}, u32[]{:S(2)}) async-start(f32[32,1,384]{2,1,0:T(1,128)} %reshape.789), calls=%async_computation.31 | async-start | bytes 98304 | tf_op jit(solution)/shard_map/all_to_all | solution.py:23
  (60 other events, 431.1 us)

commit v4 on v3

--- a/solution.py
+++ b/solution.py
@@ -225,70 +225,138 @@
     return weights
 
 
+def product_of(first, second, gram):
+    total = 0.0
+    for i, left in first.items():
+        total = total + left * sum(gram[i][k] * right for k, right in second.items())
+    return total
+
+
+def combined(terms):
+    total = {}
+    for factor, coordinates in terms:
+        for i, value in coordinates.items():
+            total[i] = total[i] + factor * value if i in total else factor * value
+    return total
+
+
+def arnoldi_step(vectors, image, gram):
+    column = [product_of(vector, image, gram) for vector in vectors]
+    rest = combined([(1.0, image)] + [(-h, v) for h, v in zip(column, vectors)])
+    height = jnp.sqrt(jnp.maximum(product_of(rest, rest, gram), 0.0) + EPSILON)
+    inverse = 1.0 / height
+    return column, height, {i: value * inverse for i, value in rest.items()}
+
+
+def spanned(coordinates, vectors):
+    total = 0.0
+    for i, value in coordinates.items():
+        factor = value if isinstance(value, float) else spread(value)
+        total = total + factor * vectors[i]
+    return total
+
+
+def completed(known, values, size):
+    values = list(values)
+    table = [[None] * size for _ in range(size)]
+    for i in range(size):
+        for k in range(i + 1):
+            entry = known[i][k] if i < len(known) else values.pop(0)
+            table[i][k] = table[k][i] = entry
+    return table
+
+
+def rows_of_products(vectors, known):
+    return [
+        inner_local(vectors[i], vectors[k]) for i in range(known, len(vectors)) for k in range(i + 1)
+    ]
+
+
 def body(double_layer, single_layer, hypersingular, adjoint_double, matching, right_side, start):
     tile = tile_of_operators(
         double_layer[0], single_layer[0], hypersingular[0], adjoint_double[0]
     )
-    right_local = inward(right_side)
     start_local = inward(start)
-    selector = selectors(matching, right_local.shape[1])
+    selector = selectors(matching, start_local.shape[1])
     start_image = preconditioned(tile, selector, start_local)
-    residual = right_local - start_image
-    local_dots = jnp.stack(
+    start_image, start_again, right_side = lax.optimization_barrier(
+        (start_image, start_local, right_side)
+    )
+    residual = inward(right_side) - start_image
+    dots = jnp.stack(
         [
             inner_local(residual, residual),
-            inner_local(start_local, start_image),
-            inner_local(start_local, start_local),
+            inner_local(start_again, start_image),
+            inner_local(start_again, start_again),
         ]
     )
-    applied, sums = preconditioned(tile, selector, residual, local_dots)
+    applied, sums = preconditioned(tile, selector, residual, dots)
     beta = jnp.sqrt(sums[0] + EPSILON)
     shift = sums[1] / (sums[2] + EPSILON)
-    basis = [residual / spread(beta)]
-    images = [applied / spread(beta)]
-    gram = (sums[0] / (beta * beta))[None, None]
+    inverse = spread(1.0 / beta)
+    basis = [residual * inverse]
+    image = applied * inverse
+    gram = [[sums[0] / (beta * beta)]]
     hessen = []
-    for column in range(BASIS):
-        ahead = images[column] - spread(shift) * basis[column]
-        local_dots = [inner_local(vector, ahead) for vector in basis]
-        local_dots = jnp.stack(local_dots + [inner_local(ahead, ahead)])
-        ahead, local_dots, gram, shift, hessen, beta = lax.optimization_barrier(
-            (ahead, local_dots, gram, shift, hessen, beta)
+    for _ in range(BASIS // 2):
+        done = len(basis)
+        last = done - 1
+        wide = spread(shift)
+        first = image - wide * basis[last]
+        first, basis, hessen, gram, shift, wide, beta = lax.optimization_barrier(
+            (first, basis, hessen, gram, shift, wide, beta)
         )
-        if column + 1 < BASIS:
-            applied, sums = preconditioned(tile, selector, ahead, local_dots)
-        else:
-            sums = summed_everywhere(local_dots)
-        dots = sums[: column + 1]
-        coefficients = dots + shift * gram[:, column]
-        removed = jnp.concatenate([coefficients[:column], dots[column:] + shift * (gram[column:, column] - 1.0)])
-        overlaps = jnp.sum(gram * removed[None], axis=1)
-        squares = jnp.maximum(
-            sums[column + 1] - jnp.sum(removed * (2.0 * dots - overlaps), axis=0), 0.0
+        first_image = preconditioned(tile, selector, first)
+        first_image, first, basis = lax.optimization_barrier((first_image, first, basis))
+        second = first_image - wide * first
+        spanning = basis + [first, second]
+        dots = jnp.stack(rows_of_products(spanning, done))
+        second_image, sums = preconditioned(tile, selector, second, dots)
+        second_image, sums, spanning, hessen, gram, shift = lax.optimization_barrier(
+            (second_image, sums, spanning, hessen, gram, shift)
         )
-        height = jnp.sqrt(squares + EPSILON)
-        if column + 1 < BASIS:
-            following = ahead
-            for earlier in range(column + 1):
-                following = following - spread(removed[earlier]) * basis[earlier]
-                applied = applied - spread(removed[earlier]) * images[earlier]
-            basis.append(following / spread(height))
-            images.append(applied / spread(height))
-            side = (dots - overlaps) / height
-            corner = squares / (height * height)
-            gram = jnp.concatenate(
-                [
-                    jnp.concatenate([gram, side[:, None]], axis=1),
-                    jnp.concatenate([side, corner[None]])[None],
-                ]
-            )
-            shift = coefficients[column]
-        filler = [jnp.zeros_like(height)] * (BASIS - 1 - column)
-        hessen.append([coefficients[earlier] for earlier in range(column + 1)] + [height] + filler)
+        table = completed(gram, sums, done + 2)
+        images = [
+            {row: hessen[column][row] for row in range(column + 2)} for column in range(last)
+        ]
+        images.append({last: shift, done: 1.0})
+        images.append({done: shift, done + 1: 1.0})
+        vectors = [{i: 1.0} for i in range(done)]
+        column, height, following = arnoldi_step(vectors, images[last], table)
+        hessen.append(column + [height])
+        vectors.append(following)
+        image_ahead = combined([(value, images[i]) for i, value in following.items()])
+        column, height, following = arnoldi_step(vectors, image_ahead, table)
+        hessen.append(column + [height])
+        vectors.append(following)
+        local_images = [spanned(known, spanning) for known in images]
+        local_images.append(second_image)
+        image = spanned(following, local_images)
+        basis = [spanned(vector, spanning) for vector in vectors]
+        gram = [
+            [product_of(vectors[i], vectors[k], table) for k in range(i + 1)]
+            for i in range(len(vectors))
+        ]
+        shift = hessen[-1][-2]
+    ahead = image - spread(shift) * basis[-1]
+    dots = jnp.stack([inner_local(vector, ahead) for vector in basis + [ahead]])
+    dots, hessen, gram, shift, beta, start_again, basis = lax.optimization_barrier(
+        (dots, hessen, gram, shift, beta, start_again, basis)
+    )
+    sums = summed_everywhere(dots)
+    sums, hessen, gram, shift, beta, start_again, basis = lax.optimization_barrier(
+        (sums, hessen, gram, shift, beta, start_again, basis)
+    )
+    last = len(basis)
+    table = completed(gram, sums, last + 1)
+    vectors = [{i: 1.0} for i in range(last)]
+    column, height, _ = arnoldi_step(vectors, {last - 1: shift, last: 1.0}, table)
+    hessen.append(column + [height])
+    hessen = [list(column) + [jnp.zeros_like(beta)] * (BASIS + 1 - len(column)) for column in hessen]
     weights = least_squares(hessen, beta)
-    solution = start_local
-    for column in range(BASIS):
-        solution = solution + spread(weights[column]) * basis[column]
+    solution = start_again
+    for vector, weight in zip(basis, weights):
+        solution = solution + spread(weight) * vector
     return outward(solution)
 
 

time: 458 us -> 431 us (0.941)
  waiting for transfers between devices: 75.4 us -> 50.4 us
  blocking collectives: 219 us -> 230 us
  starting transfers between devices: 105 us -> 95.5 us
    all_to_all x8 -> x5, waiting for transfers between devices: 56.6 us -> 29.5 us  [copy_for_each(): lax.all_to_all(jnp.broadcast_to(value[None], (peers, *value.shape)), axis...]
    all_to_all x11 -> x12, blocking collectives: 139 us -> 150 us  [copy_for_each(): lax.all_to_all(jnp.broadcast_to(value[None], (peers, *value.shape)), axis...]
    all_to_all x8 -> x5, starting transfers between devices: 40 us -> 29.1 us  [copy_for_each(): lax.all_to_all(jnp.broadcast_to(value[None], (peers, *value.shape)), axis...]
  transfers between devices with their start and end apart: 22 -> 19, of which waited for: 11 -> 10; matrix products, arithmetic and copies ran while one was open for 4% -> 4% of each run, Pallas kernels for 0% -> 0%
where the time goes in v4:
time: 431 us; the launch traced here: 429 us
  blocking collectives  230 us (53%)
  starting transfers between devices  95.5 us (22%)
  waiting for transfers between devices  50.4 us (12%)
  other arithmetic  24 us (6%)
  local copies, waits for them, and re-layouts  14.9 us (3%)
  matrix products  11.9 us (3%)
    all_to_all x12, blocking collectives, copy_for_each(): lax.all_to_all(jnp.broadcast_to(value[None], (peers, *value.shape)), axis...  150 us
    all_to_all x11, blocking collectives, exchanged_rows(): lax.all_to_all(partials, 'blk_0', 0, 0, tiled=True).astype(jnp.float32)  80.1 us
    ppermute x12, starting transfers between devices, passed_along(): return lax.ppermute(block, axis, route)  58 us
    all_to_all x5, waiting for transfers between devices, copy_for_each(): lax.all_to_all(jnp.broadcast_to(value[None], (peers, *value.shape)), axis...  29.5 us
    all_to_all x5, starting transfers between devices, copy_for_each(): lax.all_to_all(jnp.broadcast_to(value[None], (peers, *value.shape)), axis...  29.1 us
    all_to_all x1, waiting for transfers between devices, tile_of_operators(): blocks = lax.all_to_all(strips, 'blk_0', 0, 0, tiled=True)  13.1 us
    dot_general x12, matrix products, partial_products(): products = jnp.dot(tile, stacked, preferred_element_type=jnp.float32)  9.16 us
  transfers between devices with their start and end apart: 19, of which 10 were waited for; matrix products, arithmetic and copies ran while one was open for 4% of the time, Pallas kernels for 0%

profile of v4, /device:TPU:1, one launch (start us, length us, event | category | flops | bytes accessed | tf_op | source)
XLA Modules:
  0.0 428.9 jit_solution(11272827727728949428)
XLA Ops:
  1.8 7.6 %all-to-all-start.1 = ((bf16[8,128,128]{2,1,0:T(8,128)(2,1)}), bf16[8,128,128]{2,1,0:T(8,128)(2,1)S(1)}, u32[]{:S(2)}, u32[]{:S(2)}) async-start(bf16[8,128,128]{2,1,0:T(8,128)(2,1)} %broadcast_in_dim.58), calls=%async_computation.1 | async-start | bytes 524288 | tf_op jit(solution)/shard_map/all_to_all | solution.py:23
  18.9 5.1 %all-to-all-start = ((bf16[4,128,2048]{2,1,0:T(8,128)(2,1)}), bf16[4,128,2048]{2,1,0:T(8,128)(2,1)S(1)}, u32[]{:S(2)}, u32[]{:S(2)}) async-start(bf16[4,128,2048]{2,1,0:T(8,128)(2,1)} %maximum_maximum_fusion), calls=%async_computation | async-start | bytes 4194304 | tf_op jit(solution)/shard_map/all_to_all | solution.py:60
  24.7 4.5 %collective-permute-start.1 = (bf16[2,128,128]{1,2,0:T(8,128)(2,1)S(1)}, bf16[2,128,128]{1,2,0:T(8,128)(2,1)S(1)}, u32[]{:S(2)}, u32[]{:S(2)}) collective-permute-start(bf16[2,128,128]{1,2,0:T(8,128)(2,1)S(1)} %get-tuple-element.466), channel_id=1, source_target_pairs={{32,0},{64,32},{96,64},{128,96},{160,128},{192,160},{224,192},{256... | collective-permute-start | bytes 196616 | tf_op jit(solution)/shard_map/ppermute | solution.py:18
  29.2 3.9 collective-permute-start
  34.7 13.1 %all-to-all-done = bf16[4,128,2048]{2,1,0:T(8,128)(2,1)S(1)} async-done(((bf16[4,128,2048]{2,1,0:T(8,128)(2,1)}), bf16[4,128,2048]{2,1,0:T(8,128)(2,1)S(1)}, u32[]{:S(2)}, u32[]{:S(2)}) %all-to-all-start) | async-done | bytes 2097184 | tf_op jit(solution)/shard_map/all_to_all | solution.py:60
  48.5 7.2 %all_to_all.150 = bf16[4,128,128]{2,1,0:T(8,128)(2,1)S(1)} all-to-all(bf16[4,128,128]{2,1,0:T(8,128)(2,1)S(1)} %fusion), channel_id=1, replica_groups=mesh['sub_0'=8,'sub_1'=2,'blk_0'=4,'blk_1'=8] {'blk_0'}, dimensions={0} | all-to-all | bytes 262144 | tf_op jit(solution)/shard_map/all_to_all | solution.py:122
  56.5 4.4 %all-to-all-start.3 = ((bf16[8,128,128]{2,1,0:T(8,128)(2,1)}), bf16[8,128,128]{2,1,0:T(8,128)(2,1)S(1)}, u32[]{:S(2)}, u32[]{:S(2)}) async-start(bf16[8,128,128]{2,1,0:T(8,128)(2,1)} %broadcast_in_dim.61), calls=%async_computation.3 | async-start | bytes 524288 | tf_op jit(solution)/shard_map/all_to_all | solution.py:23
  60.9 9.4 %all-to-all-done.3 = bf16[8,128,128]{2,1,0:T(8,128)(2,1)S(1)} async-done(((bf16[8,128,128]{2,1,0:T(8,128)(2,1)}), bf16[8,128,128]{2,1,0:T(8,128)(2,1)S(1)}, u32[]{:S(2)}, u32[]{:S(2)}) %all-to-all-start.3) | async-done | bytes 262176 | tf_op jit(solution)/shard_map/all_to_all | solution.py:23
  72.0 3.3 all-to-all-start.4
  75.5 4.7 %all-to-all-done.4 = bf16[4,128,128]{2,1,0:T(8,128)(2,1)S(1)} async-done(((bf16[4,128,128]{2,1,0:T(8,128)(2,1)}), bf16[4,128,128]{2,1,0:T(8,128)(2,1)S(1)}, u32[]{:S(2)}, u32[]{:S(2)}) %all-to-all-start.4) | async-done | bytes 131104 | tf_op jit(solution)/shard_map/all_to_all | solution.py:122
  80.6 11.7 %all_to_all.151 = bf16[8,128,128]{2,1,0:T(8,128)(2,1)S(1)} all-to-all(bf16[8,128,128]{2,1,0:T(8,128)(2,1)S(1)} %broadcast_in_dim.62), channel_id=1, replica_groups=mesh['sub_0'=8,'sub_1'=2,'blk_0'=4,'blk_1'=8] {'blk_1'}, dimensions={0} | all-to-all | bytes 524288 | tf_op jit(solution)/shard_map/all_to_all | solution.py:23
  93.0 9.9 %collective-permute-start.3 = (bf16[2,128,128]{1,2,0:T(8,128)(2,1)S(1)}, bf16[2,128,128]{1,2,0:T(8,128)(2,1)S(1)}, u32[]{:S(2)}, u32[]{:S(2)}) collective-permute-start(bf16[2,128,128]{1,2,0:T(8,128)(2,1)S(1)} %get-tuple-element.460), channel_id=1, source_target_pairs={{32,0},{64,32},{96,64},{128,96},{160,128},{192,160},{224,192},{256... | collective-permute-start | bytes 196616 | tf_op jit(solution)/shard_map/ppermute | solution.py:18
  102.9 3.9 collective-permute-start.2
  107.5 9.5 %all-to-all-start.6 = ((f32[16,1,192]{2,1,0:T(1,128)}), f32[16,1,192]{2,1,0:T(1,128)S(1)}, u32[]{:S(2)}, u32[]{:S(2)}) async-start(f32[16,1,192]{2,1,0:T(1,128)} %reshape.473), calls=%async_computation.6 | async-start | bytes 32768 | tf_op jit(solution)/shard_map/all_to_all | solution.py:23
  117.2 7.1 %all-to-all-done.6 = f32[16,1,192]{2,1,0:T(1,128)S(1)} async-done(((f32[16,1,192]{2,1,0:T(1,128)}), f32[16,1,192]{2,1,0:T(1,128)S(1)}, u32[]{:S(2)}, u32[]{:S(2)}) %all-to-all-start.6) | async-done | bytes 12320 | tf_op jit(solution)/shard_map/all_to_all | solution.py:23
  126.9 7.2 %all_to_all.152 = bf16[4,128,128]{2,1,0:T(8,128)(2,1)S(1)} all-to-all(bf16[4,128,128]{2,1,0:T(8,128)(2,1)S(1)} %fusion.1), channel_id=1, replica_groups=mesh['sub_0'=8,'sub_1'=2,'blk_0'=4,'blk_1'=8] {'blk_0'}, dimensions={0} | all-to-all | bytes 262144 | tf_op jit(solution)/shard_map/all_to_all | solution.py:122
  134.2 12.9 %all_to_all.153 = bf16[8,144,128]{2,1,0:T(8,128)(2,1)S(1)} all-to-all(bf16[8,144,128]{2,1,0:T(8,128)(2,1)S(1)} %broadcast_in_dim.64), channel_id=1, replica_groups=mesh['sub_0'=8,'sub_1'=2,'blk_0'=4,'blk_1'=8] {'blk_1'}, dimensions={0} | all-to-all | bytes 589824 | tf_op jit(solution)/shard_map/all_to_all | solution.py:23
  148.3 7.3 %all_to_all.154 = bf16[4,144,128]{2,1,0:T(8,128)(2,1)S(1)} all-to-all(bf16[4,144,128]{2,1,0:T(8,128)(2,1)S(1)} %pad_maximum_fusion.12), channel_id=1, replica_groups=mesh['sub_0'=8,'sub_1'=2,'blk_0'=4,'blk_1'=8] {'blk_0'}, dimensions={0} | all-to-all | bytes 294912 | tf_op jit(solution)/shard_map/all_to_all | solution.py:122
  156.5 12.4 %all_to_all.155 = bf16[8,128,128]{2,1,0:T(8,128)(2,1)S(1)} all-to-all(bf16[8,128,128]{2,1,0:T(8,128)(2,1)S(1)} %broadcast_in_dim.67), channel_id=1, replica_groups=mesh['sub_0'=8,'sub_1'=2,'blk_0'=4,'blk_1'=8] {'blk_1'}, dimensions={0} | all-to-all | bytes 524288 | tf_op jit(solution)/shard_map/all_to_all | solution.py:23
  169.5 6.6 %collective-permute-start.5 = (bf16[2,128,128]{1,2,0:T(8,128)(2,1)S(1)}, bf16[2,128,128]{1,2,0:T(8,128)(2,1)S(1)}, u32[]{:S(2)}, u32[]{:S(2)}) collective-permute-start(bf16[2,128,128]{1,2,0:T(8,128)(2,1)S(1)} %get-tuple-element.458), channel_id=1, source_target_pairs={{32,0},{64,32},{96,64},{128,96},{160,128},{192,160},{224,192},{256... | collective-permute-start | bytes 196616 | tf_op jit(solution)/shard_map/ppermute | solution.py:18
  176.1 2.1 collective-permute-start.4
  180.5 7.5 %all_to_all.156 = bf16[4,128,128]{2,1,0:T(8,128)(2,1)S(1)} all-to-all(bf16[4,128,128]{2,1,0:T(8,128)(2,1)S(1)} %fusion.2), channel_id=1, replica_groups=mesh['sub_0'=8,'sub_1'=2,'blk_0'=4,'blk_1'=8] {'blk_0'}, dimensions={0} | all-to-all | bytes 262144 | tf_op jit(solution)/shard_map/all_to_all | solution.py:122
  188.1 12.7 %all_to_all.157 = bf16[8,128,128]{2,1,0:T(8,128)(2,1)S(1)} all-to-all(bf16[8,128,128]{2,1,0:T(8,128)(2,1)S(1)} %broadcast_in_dim.68), channel_id=1, replica_groups=mesh['sub_0'=8,'sub_1'=2,'blk_0'=4,'blk_1'=8] {'blk_1'}, dimensions={0} | all-to-all | bytes 524288 | tf_op jit(solution)/shard_map/all_to_all | solution.py:23
  201.9 7.2 %all_to_all.158 = bf16[4,128,128]{2,1,0:T(8,128)(2,1)S(1)} all-to-all(bf16[4,128,128]{2,1,0:T(8,128)(2,1)S(1)} %convolution_convert_fusion.6), channel_id=1, replica_groups=mesh['sub_0'=8,'sub_1'=2,'blk_0'=4,'blk_1'=8] {'blk_0'}, dimensions={0} | all-to-all | bytes 262144 | tf_op jit(solution)/shard_map/all_to_all | solution.py:122
  209.7 12.0 %all_to_all.159 = bf16[8,128,128]{2,1,0:T(8,128)(2,1)S(1)} all-to-all(bf16[8,128,128]{2,1,0:T(8,128)(2,1)S(1)} %broadcast_in_dim.69), channel_id=1, replica_groups=mesh['sub_0'=8,'sub_1'=2,'blk_0'=4,'blk_1'=8] {'blk_1'}, dimensions={0} | all-to-all | bytes 524288 | tf_op jit(solution)/shard_map/all_to_all | solution.py:23
  222.2 6.4 %collective-permute-start.7 = (bf16[2,128,128]{1,2,0:T(8,128)(2,1)S(1)}, bf16[2,128,128]{1,2,0:T(8,128)(2,1)S(1)}, u32[]{:S(2)}, u32[]{:S(2)}) collective-permute-start(bf16[2,128,128]{1,2,0:T(8,128)(2,1)S(1)} %get-tuple-element.456), channel_id=1, source_target_pairs={{32,0},{64,32},{96,64},{128,96},{160,128},{192,160},{224,192},{256... | collective-permute-start | bytes 196616 | tf_op jit(solution)/shard_map/ppermute | solution.py:18
  228.7 2.8 collective-permute-start.6
  232.2 3.6 all-to-all-start.15
  235.9 7.3 %all-to-all-done.15 = f32[16,1,320]{2,1,0:T(1,128)S(1)} async-done(((f32[16,1,320]{2,1,0:T(1,128)}), f32[16,1,320]{2,1,0:T(1,128)S(1)}, u32[]{:S(2)}, u32[]{:S(2)}) %all-to-all-start.15) | async-done | bytes 20512 | tf_op jit(solution)/shard_map/all_to_all | solution.py:23
  246.0 7.2 %all_to_all.160 = bf16[4,128,128]{2,1,0:T(8,128)(2,1)S(1)} all-to-all(bf16[4,128,128]{2,1,0:T(8,128)(2,1)S(1)} %fusion.3), channel_id=1, replica_groups=mesh['sub_0'=8,'sub_1'=2,'blk_0'=4,'blk_1'=8] {'blk_0'}, dimensions={0} | all-to-all | bytes 262144 | tf_op jit(solution)/shard_map/all_to_all | solution.py:122
  253.3 12.9 %all_to_all.161 = bf16[8,144,128]{2,1,0:T(8,128)(2,1)S(1)} all-to-all(bf16[8,144,128]{2,1,0:T(8,128)(2,1)S(1)} %broadcast_in_dim.71), channel_id=1, replica_groups=mesh['sub_0'=8,'sub_1'=2,'blk_0'=4,'blk_1'=8] {'blk_1'}, dimensions={0} | all-to-all | bytes 589824 | tf_op jit(solution)/shard_map/all_to_all | solution.py:23
  267.4 7.3 %all_to_all.162 = bf16[4,144,128]{2,1,0:T(8,128)(2,1)S(1)} all-to-all(bf16[4,144,128]{2,1,0:T(8,128)(2,1)S(1)} %pad_maximum_fusion.13), channel_id=1, replica_groups=mesh['sub_0'=8,'sub_1'=2,'blk_0'=4,'blk_1'=8] {'blk_0'}, dimensions={0} | all-to-all | bytes 294912 | tf_op jit(solution)/shard_map/all_to_all | solution.py:122
  278.3 12.4 %all_to_all.163 = bf16[8,128,128]{2,1,0:T(8,128)(2,1)S(1)} all-to-all(bf16[8,128,128]{2,1,0:T(8,128)(2,1)S(1)} %broadcast_in_dim.74), channel_id=1, replica_groups=mesh['sub_0'=8,'sub_1'=2,'blk_0'=4,'blk_1'=8] {'blk_1'}, dimensions={0} | all-to-all | bytes 524288 | tf_op jit(solution)/shard_map/all_to_all | solution.py:23
  291.3 6.6 %collective-permute-start.9 = (bf16[2,128,128]{1,2,0:T(8,128)(2,1)S(1)}, bf16[2,128,128]{1,2,0:T(8,128)(2,1)S(1)}, u32[]{:S(2)}, u32[]{:S(2)}) collective-permute-start(bf16[2,128,128]{1,2,0:T(8,128)(2,1)S(1)} %get-tuple-element.453), channel_id=1, source_target_pairs={{32,0},{64,32},{96,64},{128,96},{160,128},{192,160},{224,192},{256... | collective-permute-start | bytes 196616 | tf_op jit(solution)/shard_map/ppermute | solution.py:18
  297.9 2.0 collective-permute-start.8
  302.2 7.4 %all_to_all.164 = bf16[4,128,128]{2,1,0:T(8,128)(2,1)S(1)} all-to-all(bf16[4,128,128]{2,1,0:T(8,128)(2,1)S(1)} %fusion.4), channel_id=1, replica_groups=mesh['sub_0'=8,'sub_1'=2,'blk_0'=4,'blk_1'=8] {'blk_0'}, dimensions={0} | all-to-all | bytes 262144 | tf_op jit(solution)/shard_map/all_to_all | solution.py:122
  309.7 12.7 %all_to_all.165 = bf16[8,128,128]{2,1,0:T(8,128)(2,1)S(1)} all-to-all(bf16[8,128,128]{2,1,0:T(8,128)(2,1)S(1)} %broadcast_in_dim.75), channel_id=1, replica_groups=mesh['sub_0'=8,'sub_1'=2,'blk_0'=4,'blk_1'=8] {'blk_1'}, dimensions={0} | all-to-all | bytes 524288 | tf_op jit(solution)/shard_map/all_to_all | solution.py:23
  323.6 7.2 %all_to_all.166 = bf16[4,128,128]{2,1,0:T(8,128)(2,1)S(1)} all-to-all(bf16[4,128,128]{2,1,0:T(8,128)(2,1)S(1)} %convolution_convert_fusion.2), channel_id=1, replica_groups=mesh['sub_0'=8,'sub_1'=2,'blk_0'=4,'blk_1'=8] {'blk_0'}, dimensions={0} | all-to-all | bytes 262144 | tf_op jit(solution)/shard_map/all_to_all | solution.py:122
  331.6 12.0 %all_to_all.167 = bf16[8,128,128]{2,1,0:T(8,128)(2,1)S(1)} all-to-all(bf16[8,128,128]{2,1,0:T(8,128)(2,1)S(1)} %broadcast_in_dim.76), channel_id=1, replica_groups=mesh['sub_0'=8,'sub_1'=2,'blk_0'=4,'blk_1'=8] {'blk_1'}, dimensions={0} | all-to-all | bytes 524288 | tf_op jit(solution)/shard_map/all_to_all | solution.py:23
  345.5 6.5 %collective-permute-start.11 = (bf16[2,128,128]{1,2,0:T(8,128)(2,1)}, bf16[2,128,128]{1,2,0:T(8,128)(2,1)S(1)}, u32[]{:S(2)}, u32[]{:S(2)}) collective-permute-start(bf16[2,128,128]{1,2,0:T(8,128)(2,1)} %get-tuple-element.451), channel_id=1, source_target_pairs={{32,0},{64,32},{96,64},{128,96},{160,128},{192,160},{224,192},{256... | collective-permute-start | bytes 196616 | tf_op jit(solution)/shard_map/ppermute | solution.py:18
  352.0 2.9 collective-permute-start.10
  355.5 4.0 all-to-all-start.24
  363.0 4.2 all-to-all-done.24
  368.9 7.2 %all_to_all.168 = bf16[4,128,128]{2,1,0:T(8,128)(2,1)S(1)} all-to-all(bf16[4,128,128]{2,1,0:T(8,128)(2,1)S(1)} %fusion.5), channel_id=1, replica_groups=mesh['sub_0'=8,'sub_1'=2,'blk_0'=4,'blk_1'=8] {'blk_0'}, dimensions={0} | all-to-all | bytes 262144 | tf_op jit(solution)/shard_map/all_to_all | solution.py:122
  376.2 13.0 %all_to_all.169 = bf16[8,144,128]{2,1,0:T(8,128)(2,1)S(1)} all-to-all(bf16[8,144,128]{2,1,0:T(8,128)(2,1)S(1)} %broadcast_in_dim.78), channel_id=1, replica_groups=mesh['sub_0'=8,'sub_1'=2,'blk_0'=4,'blk_1'=8] {'blk_1'}, dimensions={0} | all-to-all | bytes 589824 | tf_op jit(solution)/shard_map/all_to_all | solution.py:23
  390.5 7.3 %all_to_all.170 = bf16[4,144,128]{2,1,0:T(8,128)(2,1)S(1)} all-to-all(bf16[4,144,128]{2,1,0:T(8,128)(2,1)S(1)} %pad_maximum_fusion.14), channel_id=1, replica_groups=mesh['sub_0'=8,'sub_1'=2,'blk_0'=4,'blk_1'=8] {'blk_0'}, dimensions={0} | all-to-all | bytes 294912 | tf_op jit(solution)/shard_map/all_to_all | solution.py:122
  400.1 13.9 %all_to_all.171 = f32[16,1,384]{2,1,0:T(1,128)S(1)} all-to-all(f32[16,1,384]{2,1,0:T(1,128)S(1)} %reshape.479), channel_id=1, replica_groups=mesh['sub_0'=8,'sub_1'=2,'blk_0'=4,'blk_1'=8] {'sub_0','sub_1'}, dimensions={0} | all-to-all | bytes 49152 | tf_op jit(solution)/shard_map/all_to_all | solution.py:23
  414.9 11.8 %all_to_all.172 = f32[32,1,384]{2,1,0:T(1,128)S(1)} all-to-all(f32[32,1,384]{2,1,0:T(1,128)S(1)} %reshape.481), channel_id=1, replica_groups=mesh['sub_0'=8,'sub_1'=2,'blk_0'=4,'blk_1'=8] {'blk_0','blk_1'}, dimensions={0} | all-to-all | bytes 98304 | tf_op jit(solution)/shard_map/all_to_all | solution.py:23
  (382 shorter events, 55.4 us)
Async XLA Ops:
  0.0 10.8 %copy-start = (bf16[1,2,64,2048]{3,2,1,0:T(8,128)(2,1)S(1)}, bf16[1,2,64,2048]{3,2,1,0:T(8,128)(2,1)}, u32[]{:S(2)}) copy-start(bf16[1,2,64,2048]{3,2,1,0:T(8,128)(2,1)} %param.15) | copy-start | bytes 1572868
  1.8 17.1 %all-to-all-start.1 = ((bf16[8,128,128]{2,1,0:T(8,128)(2,1)}), bf16[8,128,128]{2,1,0:T(8,128)(2,1)S(1)}, u32[]{:S(2)}, u32[]{:S(2)}) async-start(bf16[8,128,128]{2,1,0:T(8,128)(2,1)} %broadcast_in_dim.58), calls=%async_computation.1 | async-start | bytes 524288 | tf_op jit(solution)/shard_map/all_to_all | solution.py:23
  18.9 28.9 %all-to-all-start = ((bf16[4,128,2048]{2,1,0:T(8,128)(2,1)}), bf16[4,128,2048]{2,1,0:T(8,128)(2,1)S(1)}, u32[]{:S(2)}, u32[]{:S(2)}) async-start(bf16[4,128,2048]{2,1,0:T(8,128)(2,1)} %maximum_maximum_fusion), calls=%async_computation | async-start | bytes 4194304 | tf_op jit(solution)/shard_map/all_to_all | solution.py:60
  24.2 68.2 %copy-start.20 = (s32[256]{0:T(256)}, s32[256]{0:T(256)S(1)}, u32[]{:S(2)}) copy-start(s32[256]{0:T(256)S(1)} %pad_add_fusion) | copy-start | bytes 3076
  24.2 68.2 %copy-start.15 = (s32[512]{0:T(512)}, s32[512]{0:T(512)S(1)}, u32[]{:S(2)}) copy-start(s32[512]{0:T(512)S(1)} %iota_add_fusion.1) | copy-start | bytes 6148
  24.6 10.0 %copy-start.5 = (f32[2]{0:T(128)S(1)}, f32[2]{0:T(128)}, u32[]{:S(2)}) copy-start(f32[2]{0:T(128)} %constant.68.clone) | copy-start | bytes 28
  24.7 8.8 %collective-permute-start.1 = (bf16[2,128,128]{1,2,0:T(8,128)(2,1)S(1)}, bf16[2,128,128]{1,2,0:T(8,128)(2,1)S(1)}, u32[]{:S(2)}, u32[]{:S(2)}) collective-permute-start(bf16[2,128,128]{1,2,0:T(8,128)(2,1)S(1)} %get-tuple-element.466), channel_id=1, source_target_pairs={{32,0},{64,32},{96,64},{128,96},{160,128},{192,160},{224,192},{256... | collective-permute-start | bytes 196616 | tf_op jit(solution)/shard_map/ppermute | solution.py:18
  29.2 5.2 %collective-permute-start = (bf16[2,128,128]{1,2,0:T(8,128)(2,1)S(1)}, bf16[2,128,128]{1,2,0:T(8,128)(2,1)S(1)}, u32[]{:S(2)}, u32[]{:S(2)}) collective-permute-start(bf16[2,128,128]{1,2,0:T(8,128)(2,1)S(1)} %get-tuple-element.465), channel_id=1, source_target_pairs={{0,32},{32,64},{64,96},{96,128},{128,160},{160,192},{192,224},{224... | collective-permute-start | bytes 196616 | tf_op jit(solution)/shard_map/ppermute | solution.py:18
  56.5 13.8 %all-to-all-start.3 = ((bf16[8,128,128]{2,1,0:T(8,128)(2,1)}), bf16[8,128,128]{2,1,0:T(8,128)(2,1)S(1)}, u32[]{:S(2)}, u32[]{:S(2)}) async-start(bf16[8,128,128]{2,1,0:T(8,128)(2,1)} %broadcast_in_dim.61), calls=%async_computation.3 | async-start | bytes 524288 | tf_op jit(solution)/shard_map/all_to_all | solution.py:23
  70.6 9.6 %copy-start.1 = (f32[1,2,2,64,64]{4,3,2,1,0:T(8,128)S(1)}, f32[1,2,2,64,64]{4,3,2,1,0:T(8,128)}, u32[]{:S(2)}) copy-start(f32[1,2,2,64,64]{4,3,2,1,0:T(8,128)} %param.18) | copy-start | bytes 196612
  72.0 8.1 %all-to-all-start.4 = ((bf16[4,128,128]{2,1,0:T(8,128)(2,1)}), bf16[4,128,128]{2,1,0:T(8,128)(2,1)S(1)}, u32[]{:S(2)}, u32[]{:S(2)}) async-start(bf16[4,128,128]{2,1,0:T(8,128)(2,1)} %convolution_convert_fusion.10), calls=%async_computation.4 | async-start | bytes 262144 | tf_op jit(solution)/shard_map/all_to_all | solution.py:122
  93.0 32.9 %collective-permute-start.3 = (bf16[2,128,128]{1,2,0:T(8,128)(2,1)S(1)}, bf16[2,128,128]{1,2,0:T(8,128)(2,1)S(1)}, u32[]{:S(2)}, u32[]{:S(2)}) collective-permute-start(bf16[2,128,128]{1,2,0:T(8,128)(2,1)S(1)} %get-tuple-element.460), channel_id=1, source_target_pairs={{32,0},{64,32},{96,64},{128,96},{160,128},{192,160},{224,192},{256... | collective-permute-start | bytes 196616 | tf_op jit(solution)/shard_map/ppermute | solution.py:18
  102.9 23.0 %collective-permute-start.2 = (bf16[2,128,128]{1,2,0:T(8,128)(2,1)S(1)}, bf16[2,128,128]{1,2,0:T(8,128)(2,1)S(1)}, u32[]{:S(2)}, u32[]{:S(2)}) collective-permute-start(bf16[2,128,128]{1,2,0:T(8,128)(2,1)S(1)} %get-tuple-element.459), channel_id=1, source_target_pairs={{0,32},{32,64},{64,96},{96,128},{128,160},{160,192},{192,224},{224... | collective-permute-start | bytes 196616 | tf_op jit(solution)/shard_map/ppermute | solution.py:18
  107.5 16.9 %all-to-all-start.6 = ((f32[16,1,192]{2,1,0:T(1,128)}), f32[16,1,192]{2,1,0:T(1,128)S(1)}, u32[]{:S(2)}, u32[]{:S(2)}) async-start(f32[16,1,192]{2,1,0:T(1,128)} %reshape.473), calls=%async_computation.6 | async-start | bytes 32768 | tf_op jit(solution)/shard_map/all_to_all | solution.py:23
  148.2 20.7 %copy-start.16 = (s32[512]{0:T(512)S(1)}, s32[512]{0:T(512)}, u32[]{:S(2)}) copy-start(s32[512]{0:T(512)} %copy-done.15) | copy-start | bytes 6148
  148.3 20.7 %copy-start.21 = (s32[256]{0:T(256)S(1)}, s32[256]{0:T(256)}, u32[]{:S(2)}) copy-start(s32[256]{0:T(256)} %copy-done.20) | copy-start | bytes 3076
  169.5 8.9 %collective-permute-start.5 = (bf16[2,128,128]{1,2,0:T(8,128)(2,1)S(1)}, bf16[2,128,128]{1,2,0:T(8,128)(2,1)S(1)}, u32[]{:S(2)}, u32[]{:S(2)}) collective-permute-start(bf16[2,128,128]{1,2,0:T(8,128)(2,1)S(1)} %get-tuple-element.458), channel_id=1, source_target_pairs={{32,0},{64,32},{96,64},{128,96},{160,128},{192,160},{224,192},{256... | collective-permute-start | bytes 196616 | tf_op jit(solution)/shard_map/ppermute | solution.py:18
  176.1 3.4 collective-permute-start.4
  222.2 21.9 %collective-permute-start.7 = (bf16[2,128,128]{1,2,0:T(8,128)(2,1)S(1)}, bf16[2,128,128]{1,2,0:T(8,128)(2,1)S(1)}, u32[]{:S(2)}, u32[]{:S(2)}) collective-permute-start(bf16[2,128,128]{1,2,0:T(8,128)(2,1)S(1)} %get-tuple-element.456), channel_id=1, source_target_pairs={{32,0},{64,32},{96,64},{128,96},{160,128},{192,160},{224,192},{256... | collective-permute-start | bytes 196616 | tf_op jit(solution)/shard_map/ppermute | solution.py:18
  228.7 15.4 %collective-permute-start.6 = (bf16[2,128,128]{1,2,0:T(8,128)(2,1)S(1)}, bf16[2,128,128]{1,2,0:T(8,128)(2,1)}, u32[]{:S(2)}, u32[]{:S(2)}) collective-permute-start(bf16[2,128,128]{1,2,0:T(8,128)(2,1)S(1)} %get-tuple-element.455), channel_id=1, source_target_pairs={{0,32},{32,64},{64,96},{96,128},{128,160},{160,192},{192,224},{224... | collective-permute-start | bytes 196616 | tf_op jit(solution)/shard_map/ppermute | solution.py:18
  232.2 11.0 %all-to-all-start.15 = ((f32[16,1,320]{2,1,0:T(1,128)}), f32[16,1,320]{2,1,0:T(1,128)S(1)}, u32[]{:S(2)}, u32[]{:S(2)}) async-start(f32[16,1,320]{2,1,0:T(1,128)} %reshape.475), calls=%async_computation.15 | async-start | bytes 49152 | tf_op jit(solution)/shard_map/all_to_all | solution.py:23
  267.4 23.4 %copy-start.17 = (s32[512]{0:T(512)S(1)}, s32[512]{0:T(512)}, u32[]{:S(2)}) copy-start(s32[512]{0:T(512)} %copy-done.15) | copy-start | bytes 6148
  267.4 23.4 %copy-start.22 = (s32[256]{0:T(256)S(1)}, s32[256]{0:T(256)}, u32[]{:S(2)}) copy-start(s32[256]{0:T(256)} %copy-done.20) | copy-start | bytes 3076
  276.2 14.9 %copy-start.3 = (f32[64]{0:T(128)}, f32[64]{0:T(128)S(1)}, u32[]{:S(2)}) copy-start(f32[64]{0:T(128)S(1)} %get-tuple-element.282) | copy-start | bytes 772
  276.3 14.8 %copy-start.18 = (f32[128]{0:T(128)}, f32[128]{0:T(128)S(1)}, u32[]{:S(2)}) copy-start(f32[128]{0:T(128)S(1)} %pad_maximum_fusion.27) | copy-start | bytes 1540
  291.3 8.8 %collective-permute-start.9 = (bf16[2,128,128]{1,2,0:T(8,128)(2,1)S(1)}, bf16[2,128,128]{1,2,0:T(8,128)(2,1)S(1)}, u32[]{:S(2)}, u32[]{:S(2)}) collective-permute-start(bf16[2,128,128]{1,2,0:T(8,128)(2,1)S(1)} %get-tuple-element.453), channel_id=1, source_target_pairs={{32,0},{64,32},{96,64},{128,96},{160,128},{192,160},{224,192},{256... | collective-permute-start | bytes 196616 | tf_op jit(solution)/shard_map/ppermute | solution.py:18
  297.9 3.3 collective-permute-start.8
  322.8 8.0 %copy-start.19 = (f32[128]{0:T(128)S(1)}, f32[128]{0:T(128)}, u32[]{:S(2)}) copy-start(f32[128]{0:T(128)} %copy-done.18) | copy-start | bytes 1540
  345.5 14.3 %collective-permute-start.11 = (bf16[2,128,128]{1,2,0:T(8,128)(2,1)}, bf16[2,128,128]{1,2,0:T(8,128)(2,1)S(1)}, u32[]{:S(2)}, u32[]{:S(2)}) collective-permute-start(bf16[2,128,128]{1,2,0:T(8,128)(2,1)} %get-tuple-element.451), channel_id=1, source_target_pairs={{32,0},{64,32},{96,64},{128,96},{160,128},{192,160},{224,192},{256... | collective-permute-start | bytes 196616 | tf_op jit(solution)/shard_map/ppermute | solution.py:18
  352.0 7.9 %collective-permute-start.10 = (bf16[2,128,128]{1,2,0:T(8,128)(2,1)S(1)}, bf16[2,128,128]{1,2,0:T(8,128)(2,1)}, u32[]{:S(2)}, u32[]{:S(2)}) collective-permute-start(bf16[2,128,128]{1,2,0:T(8,128)(2,1)S(1)} %get-tuple-element.450), channel_id=1, source_target_pairs={{0,32},{32,64},{64,96},{96,128},{128,160},{160,192},{192,224},{224... | collective-permute-start | bytes 196616 | tf_op jit(solution)/shard_map/ppermute | solution.py:18
  355.5 11.6 %all-to-all-start.24 = ((f32[16,1,576]{2,1,0:T(1,128)}), f32[16,1,576]{2,1,0:T(1,128)}, u32[]{:S(2)}, u32[]{:S(2)}) async-start(f32[16,1,576]{2,1,0:T(1,128)} %reshape.477), calls=%async_computation.24 | async-start | bytes 81920 | tf_op jit(solution)/shard_map/all_to_all | solution.py:23
  359.8 0.6 copy-start.2
  389.7 8.3 %copy-start.12 = (f32[64]{0:T(128)S(1)}, f32[64]{0:T(128)}, u32[]{:S(2)}) copy-start(f32[64]{0:T(128)} %get-tuple-element.283) | copy-start | bytes 772
  389.7 8.3 %copy-start.13 = (f32[64]{0:T(128)S(1)}, f32[64]{0:T(128)}, u32[]{:S(2)}) copy-start(f32[64]{0:T(128)} %get-tuple-element.281) | copy-start | bytes 772
  389.7 8.4 %copy-start.10 = (f32[64]{0:T(128)S(1)}, f32[64]{0:T(128)}, u32[]{:S(2)}) copy-start(f32[64]{0:T(128)} %get-tuple-element.279) | copy-start | bytes 772
  389.7 8.5 %copy-start.4 = (f32[64]{0:T(128)S(1)}, f32[64]{0:T(128)}, u32[]{:S(2)}) copy-start(f32[64]{0:T(128)} %copy-done.3) | copy-start | bytes 772
  389.7 8.5 %copy-start.6 = (f32[64]{0:T(128)S(1)}, f32[64]{0:T(128)}, u32[]{:S(2)}) copy-start(f32[64]{0:T(128)} %get-tuple-element.307) | copy-start | bytes 772
  389.7 8.5 %copy-start.7 = (f32[64]{0:T(128)S(1)}, f32[64]{0:T(128)}, u32[]{:S(2)}) copy-start(f32[64]{0:T(128)} %get-tuple-element.302) | copy-start | bytes 772
  389.7 8.5 %copy-start.8 = (f32[64]{0:T(128)S(1)}, f32[64]{0:T(128)}, u32[]{:S(2)}) copy-start(f32[64]{0:T(128)} %get-tuple-element.305) | copy-start | bytes 772
  389.8 8.5 %copy-start.9 = (f32[64]{0:T(128)S(1)}, f32[64]{0:T(128)}, u32[]{:S(2)}) copy-start(f32[64]{0:T(128)} %multiply_add_fusion.20) | copy-start | bytes 772
  389.8 8.8 %copy-start.11 = (f32[64]{0:T(128)S(1)}, f32[64]{0:T(128)}, u32[]{:S(2)}) copy-start(f32[64]{0:T(128)} %get-tuple-element.280) | copy-start | bytes 772
  390.5 37.1 %copy-start.14 = (f32[64]{0:T(128)S(1)}, f32[64]{0:T(128)}, u32[]{:S(2)}) copy-start(f32[64]{0:T(128)} %get-tuple-element.278) | copy-start | bytes 772
